TPU v7x, 256 devices: a 8x8x2 block of a 8x8x16 slice. The times are simulated.
256 devices in a mesh: grp: 2 (over z), pool: 128 (over y, x, core).
Axes of the slice: x: 8, y: 8, z: 2, core: 2. Of those that a mesh axis runs over, the one named last changes fastest.
The devices are a block of a 8x8x16 slice.
Arguments:
- query: bfloat16 [256, 4096], P(('grp', 'pool')), parts along dimension 0, may hold values from -6 to 6
- kv_pool: bfloat16 [16384, 2, 16, 512], P(('grp', 'pool')), parts along dimension 0, may hold values from -6 to 6
- holder_table: int32 [256, 128], P(('grp', 'pool')), parts along dimension 0, may hold values from 0 to 127, as said below
- slot_table: int32 [256, 128], P(('grp', 'pool')), parts along dimension 0, may hold values from 0 to 63
- lengths: int32 [256], P(('grp', 'pool')), parts along dimension 0, may hold values from 96 to 128, as said below
- out_weight: bfloat16 [4096, 8192], P('pool'), may hold values from -5 to 5
Outputs:
- mixed: bfloat16 [256, 8192], P(('grp', 'pool')), parts along dimension 0
There are 2 independent parts, one for each index of `grp`. A program takes and returns all parts, laid end to end along the dimension named above; an argument that names none is the same for every part. Nothing has to cross between parts.
Inputs may be any that keep to these rules, and one draw needn't show every extreme that they name: `holder_table`: entry [r, j] is the index along pool of the device holding block j of request r. Of one request's 128 blocks at most 2 have the same holder, and some holder has exactly 2 of the request's first 96 blocks. Request r's live blocks are 0 to lengths[r] - 1; some request has 128.
All inputs are finite; a program needn't handle non-finite values.
Results may differ from a plain program's by a relative error of at most 0.0053.
Values may be sent and summed in bfloat16 or wider, within the bound.
No kernel may reach another device: no remote copies, remote signals or barrier semaphores. Data moves between devices by JAX's collectives and lax.ppermute only.
A program may use at most 64 MiB of HBM per device.

v0:
```python
import math

import jax
import jax.numpy as jnp
from jax import lax
from jax.sharding import Mesh
from jax.sharding import PartitionSpec as P

H = 32
KVH = 4
HD = 128
POOL = ("pool_0", "pool_1", "pool_2")
GRP_POOL = ("grp", "pool_0", "pool_1", "pool_2")


lowest = -1e30


def side_by_side(arrays, axis, dim, along):
    columns = [a.reshape(*a.shape[:along], -1) for a in arrays]
    both = jnp.concatenate(columns, axis=along)
    out, at, outs = (lax.all_gather(both, axis, axis=dim, tiled=True), 0, [])
    for a, column in zip(arrays, columns):
        piece = out[..., at : at + column.shape[along]]
        outs.append(piece.reshape(*piece.shape[:along], *a.shape[along:]))
        at += column.shape[along]
    return tuple(outs)


def side_by_side_2(arrays, axis, split_dim, concat_dim, along):
    widths = [a.shape[along] for a in arrays]
    both = jnp.concatenate(arrays, axis=along)
    out = lax.all_to_all(both, axis, split_axis=split_dim, concat_axis=concat_dim, tiled=True)
    return tuple(jnp.split(out, [sum(widths[:k]) for k in range(1, len(widths))], axis=along))


def laid_out(pieces, dim):
    lengths = list(pieces.shape[1:])
    lengths[dim] *= pieces.shape[0]
    return jnp.moveaxis(pieces, 0, dim).reshape(lengths)


def gather_in_order(x, axes, order):
    pieces = x[None]
    for k in order:
        pieces = lax.all_gather(pieces, axes[k], axis=0, tiled=True)
    block = [lax.axis_size(axes[k]) for k in reversed(order)]
    pieces = pieces.reshape(*block, *x.shape)
    turned = sorted(range(len(order)), key=lambda place: order[len(order) - 1 - place])
    return pieces.transpose(*turned, *range(len(order), pieces.ndim)).reshape(-1, *x.shape)


def gathered_by_axis(x, axes, order, dim):
    return laid_out(gather_in_order(x, axes, order), dim)


def block_partials(query_heads, kv_blocks):
    head_dim = query_heads.shape[-1]
    kv_heads = query_heads.shape[1]
    block_len = kv_blocks.shape[3]
    block_shape = kv_blocks.shape[:2] + (block_len, kv_heads, head_dim)
    key_part = kv_blocks[:, :, 0].reshape(block_shape)
    value_part = kv_blocks[:, :, 1].reshape(block_shape)
    scores = jnp.einsum(
        "agqd,acbgd->acgqb", query_heads, key_part, preferred_element_type=jnp.float32
    )
    scores = scores * (1.0 / math.sqrt(head_dim))
    maxima = jnp.max(scores, axis=-1)
    shifted = jnp.exp(scores - maxima[..., None])
    totals = jnp.sum(shifted, axis=-1)
    outputs = jnp.einsum(
        "acgqb,acbgd->acgqd",
        shifted.astype(jnp.bfloat16),
        value_part,
        preferred_element_type=jnp.float32,
    )
    return (maxima, outputs, totals)


def merge_blocks(maxima, outputs, totals, live_mask, axis_pos):
    peak_score = jnp.max(jnp.where(live_mask, maxima, lowest), axis=axis_pos, keepdims=True)
    factor = jnp.exp(jnp.where(live_mask, maxima - peak_score, lowest))
    numerator = jnp.sum(factor[..., None] * outputs, axis=axis_pos)
    denominator = jnp.sum(factor * totals, axis=axis_pos)
    return (jnp.squeeze(peak_score, axis_pos), numerator, denominator)


def per_device(query, kv_pool, holder_table, slot_table, lengths, out_weight):
    pool_size = lax.axis_size(POOL)
    my_index = lax.axis_index(POOL)
    max_blocks = holder_table.shape[1]
    capacity = 2 * max_blocks // pool_size
    groups = H // KVH
    all_holders, all_slots, all_lengths = side_by_side(
        (holder_table, slot_table, lengths), POOL, 0, 1
    )
    cap_iota = jnp.arange(capacity, dtype=jnp.int32)
    block_iota = jnp.arange(max_blocks, dtype=jnp.int32)
    held_here = all_holders == my_index
    rank_here = jnp.cumsum(held_here.astype(jnp.int32), axis=1) - 1
    pick_hot = held_here[:, None, :] & (rank_here[:, None, :] == cap_iota[None, :, None])
    pick_slot = jnp.sum(jnp.where(pick_hot, all_slots[:, None, :], 0), axis=-1)
    pick_block = jnp.sum(jnp.where(pick_hot, block_iota[None, None, :], 0), axis=-1)
    send_live = jnp.any(pick_hot, axis=-1) & (pick_block < all_lengths[:, None])
    send_blocks = kv_pool[pick_slot]
    all_queries = lax.all_gather(query, POOL, axis=0, tiled=True)
    maxima, outputs, totals = block_partials(
        all_queries.reshape(pool_size, KVH, groups, HD), send_blocks
    )
    part_peak, part_numer, part_denom = merge_blocks(
        maxima, outputs, totals, send_live[:, :, None, None], 1
    )
    got_peak, got_numer, got_denom = side_by_side_2(
        (
            part_peak.reshape(pool_size, H),
            part_numer.reshape(pool_size, H * HD),
            part_denom.reshape(pool_size, H),
        ),
        POOL,
        0,
        0,
        1,
    )
    peak_score, numerator, denominator = merge_blocks(
        got_peak.reshape(pool_size, KVH, groups),
        got_numer.reshape(pool_size, KVH, groups, HD),
        got_denom.reshape(pool_size, KVH, groups),
        True,
        0,
    )
    attention = (numerator / denominator[..., None]).reshape(1, H * HD).astype(jnp.bfloat16)
    weight_block = lax.all_to_all(out_weight, POOL, split_axis=1, concat_axis=0, tiled=True)
    every_request = gathered_by_axis(attention, POOL, (0, 1, 2), 0)
    column_part = jnp.dot(every_request, weight_block, preferred_element_type=jnp.float32).astype(
        jnp.bfloat16
    )
    mixed = lax.all_to_all(column_part, POOL, split_axis=0, concat_axis=1, tiled=True)
    return mixed


def solution(mesh):
    torus = Mesh(
        mesh.devices.reshape(mesh.shape["grp"], 8, 8, 2), ("grp", "pool_0", "pool_1", "pool_2")
    )
    return jax.shard_map(
        per_device,
        mesh=torus,
        in_specs=(
            P(GRP_POOL, None),
            P(GRP_POOL, None, None, None),
            P(GRP_POOL, None),
            P(GRP_POOL, None),
            P(GRP_POOL),
            P(POOL, None),
        ),
        out_specs=P(GRP_POOL, None),
        check_vma=False,
    )
```

profile of v0, /device:TPU:513, one launch (start us, length us, event | category | flops | bytes accessed | tf_op | source)
XLA Modules:
  0.0 357.9 jit_solution(3321120689761888645)
XLA Ops:
  6.6 0.7 all-gather.7.cloned.1.call-update
  8.7 67.2 %all-gather = s32[128,1,257]{2,1,0:T(1,128)S(1)} all-gather(s32[1,1,257]{2,1,0:T(1,128)S(1)} %add_bitcast_fusion), channel_id=1, replica_groups=mesh['grp'=2,'pool_0'=8,'pool_1'=8,'pool_2'=2] {'pool_0','pool_1','pool_2'}, dimensions={0}, use_global_device_ids=true | all-gather | bytes 132612 | tf_op jit(solution)/shard_map/all_gather | solution.py:22
  77.0 8.7 %gather_fusion = bf16[256,2,16,512]{3,2,1,0:T(8,128)(2,1)} fusion(bf16[64,2,16,512]{3,2,1,0:T(8,128)(2,1)S(1)} %copy-done, s32[1024]{0:T(1024)S(1)} %pad_clamp_fusion), kind=kCustom, calls=%fused_computation | custom fusion | bytes 16778240 | tf_op jit(solution)/shard_map/gather | solution.py:105
  85.8 6.4 %fusion.10 = (bf16[128,2,1,16,512]{4,3,2,1,0:T(8,128)(2,1)}, bf16[128,2,1,16,512]{4,3,2,1,0:T(8,128)(2,1)}) fusion(bf16[128,2,2,16,512]{4,3,2,1,0:T(8,128)(2,1)} %bitcast.61), kind=kLoop, calls=%fused_computation.34 | loop fusion | bytes 16777216 | tf_op jit(solution)/shard_map/slice | solution.py:63
  92.2 7.9 %copy.129 = bf16[128,2,1,16,512]{0,4,3,1,2:T(8,128)(2,1)} copy(bf16[128,2,1,16,512]{4,3,2,1,0:T(8,128)(2,1)} %get-tuple-element.12) | data formatting | bytes 8388608 | tf_op jit(solution)/shard_map/slice | solution.py:62
  100.1 8.0 %copy.131 = bf16[128,2,16,4,128]{4,2,1,3,0:T(8,128)(2,1)} copy(bf16[128,2,16,4,128]{0,4,3,2,1:T(8,128)(2,1)} %bitcast.62) | data formatting | bytes 8388608 | tf_op jit(solution)/shard_map/reshape;squeeze | solution.py:62
  108.1 7.9 %copy.138 = bf16[128,2,1,16,512]{0,4,3,1,2:T(8,128)(2,1)} copy(bf16[128,2,1,16,512]{4,3,2,1,0:T(8,128)(2,1)} %get-tuple-element.11) | data formatting | bytes 8388608 | tf_op jit(solution)/shard_map/slice | solution.py:63
  116.0 7.9 %copy.140 = bf16[128,2,16,4,128]{4,2,3,1,0:T(8,128)(2,1)} copy(bf16[128,2,16,4,128]{0,4,3,2,1:T(8,128)(2,1)} %bitcast.63) | data formatting | bytes 8388608 | tf_op jit(solution)/shard_map/reshape;squeeze | solution.py:63
  124.1 5.0 %copy.130 = bf16[128,1,4096]{0,2,1:T(8,128)(2,1)S(1)} copy(bf16[128,1,4096]{2,1,0:T(2,128)(2,1)} %all-gather.7.cloned.1.call-done) | data formatting | bytes 2097152 | tf_op jit(solution)/shard_map/all_gather | solution.py:106
  129.1 1.0 copy.150
  130.1 14.0 %fusion.11 = f32[128,4,2,16,8]{3,4,2,1,0:T(8,128)} fusion(bf16[128,2,16,4,128]{4,2,1,3,0:T(8,128)(2,1)} %copy.131, bf16[128,4,8,128,1]{3,2,4,1,0:T(8,128)(2,1)S(1)} %copy.150), kind=kOutput, calls=%fused_computation.36 | convolution fusion | flops 33554432 | bytes 5767168 | tf_op jit(solution)/shard_map/agqd,acbgd->acgqb/dot_general | solution.py:64
  144.1 3.7 %copy.133 = f32[128,4,2,16,8]{0,3,4,1,2:T(8,128)S(1)} copy(f32[128,4,2,16,8]{3,4,2,1,0:T(8,128)} %fusion.11) | data formatting | bytes 1048576 | tf_op jit(solution)/shard_map/agqd,acbgd->acgqb/dot_general | solution.py:64
  148.4 3.0 copy.139
  151.4 4.9 %multiply_reduce_fusion = f32[128,4,8,128]{3,2,1,0:T(8,128)} fusion(bf16[128,2,4,8,16]{4,3,2,1,0:T(8,128)(2,1)S(1)} %copy.139, bf16[128,2,16,4,128]{4,2,3,1,0:T(8,128)(2,1)} %copy.140, f32[128,2,4,8]{3,2,1,0:T(4,128)S(1)} %copy.137), kind=kOutput, calls=%fused_computation.1 | convolution fusion | flops 35127296 | bytes 6586368 | tf_op jit(solution)/shard_map/acgqb,acbgd->acgqd/dot_general | solution.py:71
  156.3 2.0 copy.153
  158.3 1.4 maximum_bitcast_fusion
  159.8 5.7 %copy.144 = f32[128,1,4160]{2,1,0:T(1,128)} copy(f32[128,1,4160]{0,2,1:T(8,128)} %maximum_bitcast_fusion) | data formatting | bytes 4259840 | tf_op jit(solution)/shard_map/all_to_all | solution.py:33
  165.5 60.6 %all_to_all.47 = f32[128,1,4160]{2,1,0:T(1,128)} all-to-all(f32[128,1,4160]{2,1,0:T(1,128)} %copy.144), channel_id=1, replica_groups=mesh['grp'=2,'pool_0'=8,'pool_1'=8,'pool_2'=2] {'pool_0','pool_1','pool_2'}, dimensions={0} | all-to-all | bytes 4259840 | tf_op jit(solution)/shard_map/all_to_all | solution.py:33
  226.1 5.7 %copy.145 = f32[128,1,4160]{0,2,1:T(8,128)} copy(f32[128,1,4160]{2,1,0:T(1,128)} %all_to_all.47) | data formatting | bytes 4259840 | tf_op jit(solution)/shard_map/all_to_all | solution.py:33
  231.7 0.9 slice_reduce_fusion
  232.6 0.9 fusion.7
  233.7 0.8 fusion.8
  234.5 2.2 fusion
  236.8 18.6 %all_gather.17 = bf16[8,1,4096]{2,1,0:T(2,128)(2,1)S(1)} all-gather(bf16[1,1,4096]{2,1,0:T(2,128)(2,1)S(1)} %divide_convert_fusion), channel_id=1, replica_groups=mesh['grp'=2,'pool_0'=8,'pool_1'=8,'pool_2'=2] {'pool_0'}, dimensions={0}, use_global_device_ids=true | all-gather | bytes 73728 | tf_op jit(solution)/shard_map/all_gather | solution.py:46
  255.5 21.6 %all_gather.18 = bf16[64,1,4096]{2,0,1:T(8,128)(2,1)} all-gather(bf16[8,1,4096]{2,0,1:T(8,128)(2,1)S(1)} %copy.146), channel_id=1, replica_groups=mesh['grp'=2,'pool_0'=8,'pool_1'=8,'pool_2'=2] {'pool_1'}, dimensions={0}, use_global_device_ids=true | all-gather | bytes 589824 | tf_op jit(solution)/shard_map/all_gather | solution.py:46
  277.2 1.1 all_to_all.37
  279.6 42.9 %all_to_all.48 = bf16[128,2,1024]{2,1,0:T(2,128)(2,1)S(1)} all-to-all(bf16[128,2,1024]{2,1,0:T(2,128)(2,1)S(1)} %reshape.145), channel_id=1, replica_groups=mesh['grp'=2,'pool_0'=8,'pool_1'=8,'pool_2'=2] {'pool_0','pool_1','pool_2'}, dimensions={0} | all-to-all | bytes 1048576 | tf_op jit(solution)/shard_map/all_to_all | solution.py:132
  323.2 3.5 copy.147
  326.7 2.3 reshape_reshape.3
  328.9 1.8 fusion.1
  330.8 19.4 %all_to_all.49 = bf16[128,1,64]{2,1,0:T(2,128)(2,1)S(1)} all-to-all(bf16[128,1,64]{2,1,0:T(2,128)(2,1)S(1)} %copy.149), channel_id=1, replica_groups=mesh['grp'=2,'pool_0'=8,'pool_1'=8,'pool_2'=2] {'pool_0','pool_1','pool_2'}, dimensions={0} | all-to-all | bytes 32768 | tf_op jit(solution)/shard_map/all_to_all | solution.py:137
  350.4 0.7 all_to_all.43
  (43 shorter events, 5.1 us)
Async XLA Ops:
  6.5 70.5 %copy-start = (bf16[64,2,16,512]{3,2,1,0:T(8,128)(2,1)S(1)}, bf16[64,2,16,512]{3,2,1,0:T(8,128)(2,1)}, u32[]{:S(2)}) copy-start(bf16[64,2,16,512]{3,2,1,0:T(8,128)(2,1)} %param.7) | copy-start | bytes 6291460
  6.6 117.5 %all-gather.7.cloned.1.call-start = ((), (), s32[]{:S(2)}) async-start(), calls=%async_computation.4 | async-start | bytes 2113536 | tf_op jit(solution)/shard_map/all_gather | solution.py:106
  7.3 315.8 %all-gather.5.cloned.1.call-start = ((), (), s32[]{:S(2)}) async-start(), calls=%async_computation.3 | async-start | bytes 1572864 | tf_op jit(solution)/shard_map/all_gather | solution.py:46
  231.7 45.5 %copy-start.2 = (bf16[32,8192]{1,0:T(8,128)(2,1)S(1)}, bf16[32,8192]{1,0:T(8,128)(2,1)}, u32[]{:S(2)}) copy-start(bf16[32,8192]{1,0:T(8,128)(2,1)} %param.11) | copy-start | bytes 1572868
  323.1 27.9 %copy-start.1 = (bf16[64,2,16,512]{3,2,1,0:T(8,128)(2,1)S(1)}, bf16[64,2,16,512]{3,2,1,0:T(8,128)(2,1)}, u32[]{:S(2)}) copy-start(bf16[64,2,16,512]{3,2,1,0:T(8,128)(2,1)} %param.7) | copy-start | bytes 6291460
Sparse Core Ops, SparseCore 0:
  9.9 98.6 all-gather.6
  277.3 31.8 all-gather.4
where the time goes:
time: 359 us; the launch traced here: 358 us
  blocking collectives  230 us (64%)
  local copies, waits for them, and re-layouts  83.8 us (23%)
  matrix products  20.7 us (6%)
  between operations  14.3 us (4%)
  other arithmetic  7.94 us (2%)
    all_gather x1, blocking collectives, side_by_side(): out, at, outs = (lax.all_gather(both, axis, axis=dim, tiled=True), 0, [])  67.2 us
    all_to_all x1, blocking collectives, side_by_side_2(): lax.all_to_all(both, axis, split_axis=split_dim, concat_axis=concat_dim,...  60.6 us
    all_to_all x1, blocking collectives, per_device(): lax.all_to_all(out_weight, POOL, split_axis=1, concat_axis=0, tiled=True)  42.9 us
    all_gather x2, blocking collectives, gather_in_order(): pieces = lax.all_gather(pieces, axes[k], axis=0, tiled=True)  40.2 us
    all_to_all x1, blocking collectives, per_device(): lax.all_to_all(column_part, POOL, split_axis=0, concat_axis=1, tiled=True)  19.4 us
    slice x2, local copies, waits for them, and re-layouts, block_partials(): value_part = kv_blocks[:, :, 1].reshape(block_shape)  14.3 us
    dot_general x1, matrix products, block_partials(): jnp.einsum('agqd,acbgd->acgqb', query_heads, key_part, preferred_element_...  14 us
    all_to_all x2, local copies, waits for them, and re-layouts, side_by_side_2(): lax.all_to_all(both, axis, split_axis=split_dim, concat_axis=concat_dim,...  11.4 us
  transfers between devices with their start and end apart: 2, of which 0 were waited for; matrix products, arithmetic and copies ran while one was open for 14% of the time, Pallas kernels for 0%

commit v1 on v0

v1 whole, which is shorter than its diff:
```python
import functools
import math

import jax
import jax.numpy as jnp
from jax import lax
from jax.experimental import pallas as pl
from jax.experimental.pallas import tpu as pltpu
from jax.sharding import Mesh
from jax.sharding import PartitionSpec as P


H = 32
KVH = 4
HD = 128
GROUPS = H // KVH
CORES = 2
POOL = ("y", "x", "c")
CHIPS = ("y", "x")
GRP_POOL = ("grp", "y", "x", "c")
RATE = math.log2(math.e) / math.sqrt(HD)
TWICE = math.log(2.0) * math.sqrt(HD)
UNUSED = -32768.0
HALF = H * HD // CORES
INTERPRET = False

f32 = jnp.float32
bf16 = jnp.bfloat16


def as_product(value):
    pairs = []
    for i in range(128):
        mark = 1.0 + i / 128.0
        unit = 2.0 ** (math.floor(math.log2(value / mark)) - 7)
        bias = round(value / mark / unit) * unit
        pairs.append((abs(mark * bias - value), mark, bias))
    return min(pairs)[1:]


MARK, BIAS = as_product(TWICE)


def attention_body(pos_ref, q_ref, own_ref, other_ref, out_ref, q_scr, k_scr, v_scr, s_scr, p_scr):
    g = pl.program_id(0)
    rows = q_ref.shape[0]
    slots, _, blk, _ = own_ref.shape
    tokens = slots * blk

    @pl.when(g == 0)
    def _():
        me, core = pos_ref[0], pos_ref[1]
        partner = me + 1 - 2 * core
        holder = q_ref[:, HALF : HALF + HD].astype(f32)
        slot = q_ref[:, HALF + HD : HALF + 2 * HD].astype(f32)
        lane = lax.broadcasted_iota(jnp.int32, (rows, HD), 1)
        lane_slot = jnp.where(lane < slots, lane, lane - slots).astype(f32)

        def bias_of(device):
            hit = holder == device.astype(f32)
            first = jnp.min(jnp.where(hit, slot, 999.0), axis=1, keepdims=True)
            last = jnp.max(jnp.where(hit, slot, -1.0), axis=1, keepdims=True)
            count = jnp.sum(jnp.where(hit, 1.0, 0.0), axis=1, keepdims=True)
            used = (lane_slot == first) | (lane_slot == last)
            double = used & (first == last) & (count > 1.5)
            return jnp.where(used, jnp.where(double, BIAS, 0.0), UNUSED)

        bias = jnp.where(lane < slots, bias_of(me), bias_of(partner)).astype(bf16)
        for h in range(GROUPS):
            q_scr[h * rows : (h + 1) * rows, HD:] = bias
        token_slot = lax.broadcasted_iota(jnp.int32, (2 * tokens, HD), 0) // blk
        slot_lane = lax.broadcasted_iota(jnp.int32, (2 * tokens, HD), 1)
        k_scr[:, HD:] = jnp.where(slot_lane == token_slot, MARK, 0.0).astype(bf16)
        v_scr[HD:, :] = jnp.ones((v_scr.shape[0] - HD, 2 * tokens), bf16)

    for h in range(GROUPS):
        cols = pl.ds(pl.multiple_of(g * (GROUPS * HD) + h * HD, HD), HD)
        q_scr[h * rows : (h + 1) * rows, :HD] = q_ref[:, cols]
    for i, ref in enumerate((own_ref, other_ref)):
        at = slice(i * tokens, (i + 1) * tokens)
        k_scr[at, :HD] = ref[:, 0].reshape(tokens, HD)
        v_scr[:HD, at] = ref[:, 1].reshape(tokens, HD).T
    s_scr[...] = lax.dot_general(
        k_scr[...], q_scr[...], (((1,), (1,)), ((), ())), preferred_element_type=f32
    )

    step = 256
    for h in range(GROUPS):
        cols = slice(h * rows, (h + 1) * rows)

        def peak(i, top, cols=cols):
            at = pl.ds(pl.multiple_of(i * step, step), step)
            return jnp.maximum(top, jnp.max(s_scr[at, cols].reshape(step // 8, 8, rows), axis=0))

        top = lax.fori_loop(0, 2 * tokens // step, peak, jnp.full((8, rows), -jnp.inf, f32))
        top = jnp.max(top, axis=0, keepdims=True).astype(bf16).astype(f32)

        def weigh(i, carry, cols=cols, top=top):
            at = pl.ds(pl.multiple_of(i * step, step), step)
            p_scr[at, cols] = jnp.exp2((s_scr[at, cols] - top) * RATE).astype(bf16)
            return carry

        lax.fori_loop(0, 2 * tokens // step, weigh, 0)
        for j in range(4):
            out_ref[dest_of(g, h, j), 32:33, :] = top.astype(bf16)
    out = jnp.dot(v_scr[...], p_scr[...], preferred_element_type=f32)
    for h in range(GROUPS):
        cols = slice(h * rows, (h + 1) * rows)
        total = out[HD : HD + 1, cols]
        high = total.astype(bf16)
        low = (total - high.astype(f32)).astype(bf16)
        for j in range(4):
            dest = dest_of(g, h, j)
            out_ref[dest, 0:32, :] = out[j * 32 : (j + 1) * 32, cols].astype(bf16)
            out_ref[dest, 33:34, :] = high
            out_ref[dest, 34:35, :] = low


def dest_of(g, h, j):
    return ((j % 2) * 4 + g * 2 + h // 4) * 8 + (h % 4) * 2 + j // 2


def attention_partials(pos, q, kv_pool, kv_other, chips):
    rows = q.shape[0]
    slots, _, blk, _ = kv_pool.shape
    tokens = 2 * slots * blk
    steps = KVH // CORES
    whole = lambda shape: pl.BlockSpec(shape, lambda g, pos: (0,) * len(shape))
    out = (chips, 40, rows)
    return pl.pallas_call(
        attention_body,
        grid_spec=pltpu.PrefetchScalarGridSpec(
            num_scalar_prefetch=1,
            grid=(steps,),
            in_specs=[
                whole(q.shape),
                pl.BlockSpec((slots, 2, blk, HD), lambda g, pos: (0, 0, 0, pos[1] * steps + g)),
                pl.BlockSpec((slots, 2, blk, HD), lambda g, pos: (0, 0, 0, g)),
            ],
            out_specs=whole(out),
            scratch_shapes=[
                pltpu.VMEM((GROUPS * rows, 2 * HD), bf16),
                pltpu.VMEM((tokens, 2 * HD), bf16),
                pltpu.VMEM((HD + 16, tokens), bf16),
                pltpu.VMEM((tokens, GROUPS * rows), f32),
                pltpu.VMEM((tokens, GROUPS * rows), bf16),
            ],
        ),
        out_shape=jax.ShapeDtypeStruct(out, bf16),
        cost_estimate=pl.CostEstimate(flops=1 << 34, transcendentals=0, bytes_accessed=0),
        compiler_params=pltpu.CompilerParams(dimension_semantics=("arbitrary",), vmem_limit_bytes=32 << 20),
        interpret=INTERPRET,
    )(pos, q, kv_pool, kv_other)


def merge_body(got_ref, out_ref, f_scr):
    chips, _, rows = got_ref.shape
    peaks = [got_ref[i, 32:33, :].astype(f32) for i in range(chips)]
    top = functools.reduce(jnp.maximum, peaks)
    total = jnp.zeros((1, rows), f32)
    number = jnp.zeros((32, rows), f32)
    for i in range(chips):
        factor = jnp.exp2((peaks[i] - top) * RATE)
        total += factor * (got_ref[i, 33:34, :].astype(f32) + got_ref[i, 34:35, :].astype(f32))
        number += factor * got_ref[i, 0:32, :].astype(f32)
    attention = number / total
    high = attention.astype(bf16)
    out_ref[0:32, :] = high
    out_ref[32:64, :] = (attention - high.astype(f32)).astype(bf16)


def project_body(pos_ref, mine_ref, got_ref, w_ref, w_got_ref, out_ref):
    core = pos_ref[1]
    half = w_got_ref.shape[1]
    left = jnp.concatenate([mine_ref[...], got_ref[...]], axis=0)
    step = 512
    for i in range(half // step):
        cols = pl.ds(pl.multiple_of(core * half + i * step, step), step)
        mine = w_ref[:, cols]
        got = w_got_ref[:, i * step : (i + 1) * step]
        right = jnp.concatenate([mine, mine, got, got], axis=0)
        part = lax.dot_general(left, right, (((0,), (0,)), ((), ())), preferred_element_type=f32)
        out_ref[:, i * step : (i + 1) * step] = part.astype(bf16)


def small_call(body, out, *args, scalars=(), scratch=(), mib=8):
    smem = pl.BlockSpec(memory_space=pltpu.SMEM)
    vmem = pl.BlockSpec(memory_space=pltpu.VMEM)
    return pl.pallas_call(
        body,
        out_shape=out,
        in_specs=[smem] * len(scalars) + [vmem] * len(args),
        out_specs=vmem,
        scratch_shapes=list(scratch),
        compiler_params=pltpu.CompilerParams(vmem_limit_bytes=mib << 20),
        interpret=INTERPRET,
    )(*scalars, *args)


def swapped(v):
    return lax.ppermute(v, "c", [(0, 1), (1, 0)])


def weight_moves(ny, nx, nc):
    pairs = []
    for y in range(ny):
        for x in range(nx):
            for c in range(nc):
                upper = y // (ny // 2)
                at = (y * nx + x) * nc + c
                other = (((y + ny // 2) % ny) * nx + x) * nc + 1 - c
                pairs.append((at, at if upper == c else other))
    return pairs


def per_device(query, kv_pool, holder_table, slot_table, lengths, out_weight):
    ny, nx, nc = (lax.axis_size(a) for a in POOL)
    y, x, c = (lax.axis_index(a) for a in POOL)
    chips = ny * nx
    pos = jnp.stack([(y * nx + x) * nc + c, c]).astype(jnp.int32)

    kv_half = kv_pool.shape[-1] // nc
    kv_other = swapped(lax.dynamic_slice_in_dim(kv_pool, (1 - c) * kv_half, kv_half, axis=3))

    live = lax.broadcasted_iota(jnp.int32, holder_table.shape, 1) < lengths[:, None]
    table = jnp.concatenate([jnp.where(live, holder_table, -1), slot_table], axis=1).astype(bf16)
    width = HALF + table.shape[1]
    row = jnp.concatenate([query[:, :HALF], table, query[:, HALF:], table], axis=1).reshape(nc, 2, width // 2)
    rows = jnp.broadcast_to(row[None], (chips, nc, 2, width // 2)).reshape(chips * nc, 2, width // 2)
    q = lax.all_to_all(rows, POOL, split_axis=0, concat_axis=0, tiled=True).reshape(chips * nc, width)

    q, out_weight = lax.optimization_barrier((q, out_weight))
    weight = lax.ppermute(out_weight, POOL, weight_moves(ny, nx, nc))
    parts = attention_partials(pos, q, kv_pool, kv_other, chips)
    parts = lax.all_to_all(parts, CHIPS, split_axis=0, concat_axis=0, tiled=True)

    d_half = weight.shape[1] // nc
    w_got = swapped(lax.dynamic_slice_in_dim(weight, (1 - c) * d_half, d_half, axis=1))
    mine = small_call(merge_body, jax.ShapeDtypeStruct((64, chips * nc), bf16), parts,
                      scratch=[pltpu.VMEM((chips, chips * nc), f32)])
    got = swapped(mine)
    partial = small_call(
        project_body,
        jax.ShapeDtypeStruct((chips * nc, d_half), bf16),
        mine,
        got,
        weight,
        w_got,
        scalars=(pos,),
    )
    columns = lax.all_to_all(
        partial.reshape(chips, nc, d_half), CHIPS, split_axis=0, concat_axis=0, tiled=True
    )
    done = jnp.sum(columns.astype(f32), axis=0).astype(bf16)
    keep = lax.dynamic_slice_in_dim(done, c, 1, axis=0)
    got = swapped(lax.dynamic_slice_in_dim(done, 1 - c, 1, axis=0))
    return jnp.where(c == 0, jnp.concatenate([keep, got], axis=1), jnp.concatenate([got, keep], axis=1))


def solution(mesh):
    torus = Mesh(mesh.devices.reshape(mesh.shape["grp"], 8, 8, 2), GRP_POOL)
    return jax.shard_map(
        per_device,
        mesh=torus,
        in_specs=(
            P(GRP_POOL, None),
            P(GRP_POOL, None, None, None),
            P(GRP_POOL, None),
            P(GRP_POOL, None),
            P(GRP_POOL),
            P(POOL, None),
        ),
        out_specs=P(GRP_POOL, None),
        check_vma=False,
    )
```

time: 359 us -> 153 us (0.43)
  blocking collectives: 230 us -> 0 us
  local copies, waits for them, and re-layouts: 83.8 us -> 7.52 us
  waiting for transfers between devices: 0.84 us -> 68.3 us
  starting transfers between devices: 0.06 us -> 56.8 us
  matrix products: 20.7 us -> 0 us
  Pallas kernels: 0 us -> 14.5 us
  between operations: 14.3 us -> 0.76 us
    all_to_all x3 -> x0, blocking collectives: 123 us -> none  [the longest x1 60.6 us: side_by_side_2(): lax.all_to_all(both, axis, split_axis=split_dim, concat_axis=concat_dim,...]
    all_gather x3 -> x0, blocking collectives: 107 us -> none  [the longest x1 67.2 us: side_by_side(): out, at, outs = (lax.all_gather(both, axis, axis=dim, tiled=True), 0, [])]
    all_to_all x0 -> x3, starting transfers between devices: none -> 43.6 us  [the longest x1 28.2 us: per_device(): lax.all_to_all(rows, POOL, split_axis=0, concat_axis=0, tiled=True)]
    all_to_all x0 -> x3, waiting for transfers between devices: none -> 43.1 us  [the longest x1 27 us: per_device(): lax.all_to_all(partial.reshape(chips, nc, d_half), CHIPS, split_axis=0, c...]
    ppermute x0 -> x5, waiting for transfers between devices: none -> 25.3 us  [the longest x1 23.6 us: per_device(): weight = lax.ppermute(out_weight, POOL, weight_moves(ny, nx, nc))]
    slice x6 -> x0, local copies, waits for them, and re-layouts: 22.3 us -> none  [the longest x2 14.3 us: block_partials(): value_part = kv_blocks[:, :, 1].reshape(block_shape)]
    dot_general x3 -> x0, matrix products: 20.7 us -> none  [the longest x1 14 us: block_partials(): jnp.einsum('agqd,acbgd->acgqb', query_heads, key_part, preferred_element_...]
    another operation x3 -> x0, local copies, waits for them, and re-layouts: 18.2 us -> none  [the longest x1 7.99 us: block_partials(): key_part = kv_blocks[:, :, 0].reshape(block_shape)]
  transfers between devices with their start and end apart: 2 -> 8, of which waited for: 0 -> 6; matrix products, arithmetic and copies ran while one was open for 14% -> 2% of each run, Pallas kernels for 0% -> 0%
where the time goes in v1:
time: 153 us; the launch traced here: 152 us
  waiting for transfers between devices  68.3 us (45%)
  starting transfers between devices  56.8 us (37%)
  Pallas kernels  14.5 us (9%)
  local copies, waits for them, and re-layouts  7.52 us (5%)
  other arithmetic  4.39 us (3%)
    all_to_all x1, starting transfers between devices, per_device(): lax.all_to_all(rows, POOL, split_axis=0, concat_axis=0, tiled=True)  28.2 us
    all_to_all x1, waiting for transfers between devices, per_device(): lax.all_to_all(partial.reshape(chips, nc, d_half), CHIPS, split_axis=0, c...  27 us
    ppermute x1, waiting for transfers between devices, per_device(): weight = lax.ppermute(out_weight, POOL, weight_moves(ny, nx, nc))  23.6 us
    all_to_all x1, waiting for transfers between devices, per_device(): lax.all_to_all(rows, POOL, split_axis=0, concat_axis=0, tiled=True)  16 us
    pallas_call x1, Pallas kernels, attention_partials(): pl.pallas_call(attention_body, grid_spec=pltpu.PrefetchScalarGridSpec(num...  13.2 us
    all_to_all x1, starting transfers between devices, per_device(): lax.all_to_all(partial.reshape(chips, nc, d_half), CHIPS, split_axis=0, c...  8.94 us
    ppermute x1, starting transfers between devices, per_device(): weight = lax.ppermute(out_weight, POOL, weight_moves(ny, nx, nc))  6.95 us
    all_to_all x1, starting transfers between devices, per_device(): lax.all_to_all(parts, CHIPS, split_axis=0, concat_axis=0, tiled=True)  6.5 us
  transfers between devices with their start and end apart: 8, of which 6 were waited for; matrix products, arithmetic and copies ran while one was open for 2% of the time, Pallas kernels for 0%

profile of v1, /device:TPU:513, one launch (start us, length us, event | category | flops | bytes accessed | tf_op | source)
XLA Modules:
  0.0 152.3 jit_solution(3818957034273492751)
XLA Ops:
  0.7 0.7 constant_dynamic-update-slice_fusion.5
  1.4 0.7 constant_dynamic-update-slice_fusion.4
  2.0 0.7 constant_dynamic-update-slice_fusion.3
  2.7 0.7 constant_dynamic-update-slice_fusion.2
  3.4 0.7 constant_dynamic-update-slice_fusion.1
  4.1 0.7 constant_dynamic-update-slice_fusion
  4.7 0.1 reduce.1
  4.8 1.1 broadcast_in_dim.14
  6.0 28.2 %all-to-all-start = ((bf16[128,2,1152]{2,1,0:T(2,128)(2,1)}), bf16[128,2,1152]{2,1,0:T(2,128)(2,1)}, u32[]{:S(2)}, u32[]{:S(2)}) async-start(bf16[128,2,1152]{2,1,0:T(2,128)(2,1)} %bitcast.3), calls=%async_computation | async-start | bytes 1179648 | tf_op jit(solution)/shard_map/all_to_all | solution.py:230
  34.2 2.3 %constant_dynamic-slice_fusion.3 = bf16[64,2,16,256]{3,2,1,0:T(8,128)(2,1)} fusion(bf16[64,2,16,512]{3,2,1,0:T(8,128)(2,1)} %own_ref.1, s32[]{:T(128)S(6)} %select_n.34), kind=kLoop, calls=%fused_computation.11 | loop fusion | bytes 2097156 | tf_op jit(solution)/shard_map/dynamic_slice | solution.py:223
  36.5 2.9 %collective-permute-start = (bf16[64,2,16,256]{3,2,1,0:T(8,128)(2,1)}, bf16[64,2,16,256]{3,2,1,0:T(8,128)(2,1)S(1)}, u32[]{:S(2)}, u32[]{:S(2)}) collective-permute-start(bf16[64,2,16,256]{3,2,1,0:T(8,128)(2,1)} %constant_dynamic-slice_fusion.3), channel_id=1, source_target_pairs={{0,1},{1,0},{2,3},{3,2},{4,5},{5,4},{6,7},{7,6},{8,9},{9,8},{10,11... | collective-permute-start | bytes 3145736 | tf_op jit(solution)/shard_map/ppermute | solution.py:201
  39.4 0.1 pad_add_fusion.pos_ref
  39.5 16.0 %all-to-all-done = bf16[128,2,1152]{2,1,0:T(2,128)(2,1)} async-done(((bf16[128,2,1152]{2,1,0:T(2,128)(2,1)}), bf16[128,2,1152]{2,1,0:T(2,128)(2,1)}, u32[]{:S(2)}, u32[]{:S(2)}) %all-to-all-start) | async-done | bytes 589856 | tf_op jit(solution)/shard_map/all_to_all | solution.py:230
  55.5 1.1 copy.7
  56.6 0.0 collective-permute-done.other_ref
  56.6 13.2 %shard_map.64 = bf16[64,40,128]{2,1,0:T(8,128)(2,1)} custom-call(s32[2]{0:T(128)S(1)} %pad_add_fusion.pos_ref, bf16[128,2304]{1,0:T(8,128)(2,1)S(1)} %bitcast.8, bf16[64,2,16,512]{3,2,1,0:T(8,128)(2,1)S(1)} %copy-done, bf16[64,2,16,256]{3,2,1,0:T(8,128)(2,1)S(1)} %collective-permute-done.other_ref), custom_call_target="tpu_custom_call" | custom-call | flops 17179869184 | tf_op jit(solution)/shard_map/pallas_call | solution.py:130
  69.9 6.5 %all-to-all-start.1 = ((bf16[64,40,128]{2,1,0:T(8,128)(2,1)}), bf16[64,40,128]{2,1,0:T(8,128)(2,1)S(1)}, u32[]{:S(2)}, u32[]{:S(2)}) async-start(bf16[64,40,128]{2,1,0:T(8,128)(2,1)} %shard_map.64), calls=%async_computation.1 | async-start | bytes 1310720 | tf_op jit(solution)/shard_map/all_to_all | solution.py:235
  76.4 7.0 %collective-permute-start.2 = (bf16[32,8192]{1,0:T(8,128)(2,1)}, bf16[32,8192]{1,0:T(8,128)(2,1)S(1)}, u32[]{:S(2)}, u32[]{:S(2)}) collective-permute-start(bf16[32,8192]{1,0:T(8,128)(2,1)} %param.11), channel_id=1, source_target_pairs={{0,0},{1,64},{2,2},{3,66},{4,4},{5,68},{6,6},{7,70},{8,8},{9,72},{... | collective-permute-start | bytes 1572872 | tf_op jit(solution)/shard_map/ppermute | solution.py:233
  83.3 23.6 %collective-permute-done.2.w_ref = bf16[32,8192]{1,0:T(8,128)(2,1)S(1)} collective-permute-done((bf16[32,8192]{1,0:T(8,128)(2,1)}, bf16[32,8192]{1,0:T(8,128)(2,1)S(1)}, u32[]{:S(2)}, u32[]{:S(2)}) %collective-permute-start.2) | collective-permute-done | bytes 524320 | tf_op jit(solution)/shard_map/ppermute | solution.py:233
  107.0 0.1 collective-permute-start.3
  107.1 0.3 shard_map.65.mine_ref
  107.4 0.8 collective-permute-start.1
  108.2 0.5 collective-permute-done.3.w_got_ref
  108.6 0.4 collective-permute-done.1.got_ref
  109.0 1.0 shard_map.66
  110.0 1.5 reshape.103
  111.5 8.9 %all-to-all-start.2 = ((bf16[64,2,4096]{2,1,0:T(2,128)(2,1)}), bf16[64,2,4096]{2,1,0:T(2,128)(2,1)S(1)}, u32[]{:S(2)}, u32[]{:S(2)}) async-start(bf16[64,2,4096]{2,1,0:T(2,128)(2,1)} %reshape.103), calls=%async_computation.2 | async-start | bytes 2097152 | tf_op jit(solution)/shard_map/all_to_all | solution.py:251
  120.4 27.0 %all-to-all-done.2 = bf16[64,2,4096]{2,1,0:T(2,128)(2,1)S(1)} async-done(((bf16[64,2,4096]{2,1,0:T(2,128)(2,1)}), bf16[64,2,4096]{2,1,0:T(2,128)(2,1)S(1)}, u32[]{:S(2)}, u32[]{:S(2)}) %all-to-all-start.2) | async-done | bytes 1048608 | tf_op jit(solution)/shard_map/all_to_all | solution.py:251
  147.4 0.9 reduce_sum.12
  148.4 2.4 %collective-permute-start.4 = (bf16[1,4096]{1,0:T(2,128)(2,1)S(1)}, bf16[1,4096]{1,0:T(2,128)(2,1)S(1)}, u32[]{:S(2)}, u32[]{:S(2)}) collective-permute-start(bf16[1,4096]{1,0:T(2,128)(2,1)S(1)} %get-tuple-element.10), channel_id=1, source_target_pairs={{0,1},{1,0},{2,3},{3,2},{4,5},{5,4},{6,7},{7,6},{8,9},{9,8},{10,11... | collective-permute-start | bytes 24584 | tf_op jit(solution)/shard_map/ppermute | solution.py:201
  150.8 0.8 collective-permute-done.4
  151.6 0.7 broadcast_select_fusion
  (6 shorter events, 0.1 us)
Async XLA Ops:
  6.0 50.7 %copy-start = (bf16[64,2,16,512]{3,2,1,0:T(8,128)(2,1)S(1)}, bf16[64,2,16,512]{3,2,1,0:T(8,128)(2,1)}, u32[]{:S(2)}) copy-start(bf16[64,2,16,512]{3,2,1,0:T(8,128)(2,1)} %own_ref.1) | copy-start | bytes 6291460
  6.0 49.5 %all-to-all-start = ((bf16[128,2,1152]{2,1,0:T(2,128)(2,1)}), bf16[128,2,1152]{2,1,0:T(2,128)(2,1)}, u32[]{:S(2)}, u32[]{:S(2)}) async-start(bf16[128,2,1152]{2,1,0:T(2,128)(2,1)} %bitcast.3), calls=%async_computation | async-start | bytes 1179648 | tf_op jit(solution)/shard_map/all_to_all | solution.py:230
  36.5 20.2 %collective-permute-start = (bf16[64,2,16,256]{3,2,1,0:T(8,128)(2,1)}, bf16[64,2,16,256]{3,2,1,0:T(8,128)(2,1)S(1)}, u32[]{:S(2)}, u32[]{:S(2)}) collective-permute-start(bf16[64,2,16,256]{3,2,1,0:T(8,128)(2,1)} %constant_dynamic-slice_fusion.3), channel_id=1, source_target_pairs={{0,1},{1,0},{2,3},{3,2},{4,5},{5,4},{6,7},{7,6},{8,9},{9,8},{10,11... | collective-permute-start | bytes 3145736 | tf_op jit(solution)/shard_map/ppermute | solution.py:201
  69.9 37.2 %all-to-all-start.1 = ((bf16[64,40,128]{2,1,0:T(8,128)(2,1)}), bf16[64,40,128]{2,1,0:T(8,128)(2,1)S(1)}, u32[]{:S(2)}, u32[]{:S(2)}) async-start(bf16[64,40,128]{2,1,0:T(8,128)(2,1)} %shard_map.64), calls=%async_computation.1 | async-start | bytes 1310720 | tf_op jit(solution)/shard_map/all_to_all | solution.py:235
  76.4 30.6 %collective-permute-start.2 = (bf16[32,8192]{1,0:T(8,128)(2,1)}, bf16[32,8192]{1,0:T(8,128)(2,1)S(1)}, u32[]{:S(2)}, u32[]{:S(2)}) collective-permute-start(bf16[32,8192]{1,0:T(8,128)(2,1)} %param.11), channel_id=1, source_target_pairs={{0,0},{1,64},{2,2},{3,66},{4,4},{5,68},{6,6},{7,70},{8,8},{9,72},{... | collective-permute-start | bytes 1572872 | tf_op jit(solution)/shard_map/ppermute | solution.py:233
  107.0 1.7 %collective-permute-start.3 = (bf16[32,4096]{1,0:T(8,128)(2,1)S(1)}, bf16[32,4096]{1,0:T(8,128)(2,1)S(1)}, u32[]{:S(2)}, u32[]{:S(2)}) collective-permute-start(bf16[32,4096]{1,0:T(8,128)(2,1)S(1)} %constant_dynamic-slice_fusion.2), channel_id=1, source_target_pairs={{0,1},{1,0},{2,3},{3,2},{4,5},{5,4},{6,7},{7,6},{8,9},{9,8},{10,11... | collective-permute-start | bytes 786440 | tf_op jit(solution)/shard_map/ppermute | solution.py:201
  107.4 1.6 %collective-permute-start.1 = (bf16[64,128]{1,0:T(8,128)(2,1)S(1)}, bf16[64,128]{1,0:T(8,128)(2,1)S(1)}, u32[]{:S(2)}, u32[]{:S(2)}) collective-permute-start(bf16[64,128]{1,0:T(8,128)(2,1)S(1)} %shard_map.65.mine_ref), channel_id=1, source_target_pairs={{0,1},{1,0},{2,3},{3,2},{4,5},{5,4},{6,7},{7,6},{8,9},{9,8},{10,11... | collective-permute-start | bytes 49160 | tf_op jit(solution)/shard_map/ppermute | solution.py:201
  111.5 36.0 %all-to-all-start.2 = ((bf16[64,2,4096]{2,1,0:T(2,128)(2,1)}), bf16[64,2,4096]{2,1,0:T(2,128)(2,1)S(1)}, u32[]{:S(2)}, u32[]{:S(2)}) async-start(bf16[64,2,4096]{2,1,0:T(2,128)(2,1)} %reshape.103), calls=%async_computation.2 | async-start | bytes 2097152 | tf_op jit(solution)/shard_map/all_to_all | solution.py:251
  148.4 3.2 %collective-permute-start.4 = (bf16[1,4096]{1,0:T(2,128)(2,1)S(1)}, bf16[1,4096]{1,0:T(2,128)(2,1)S(1)}, u32[]{:S(2)}, u32[]{:S(2)}) collective-permute-start(bf16[1,4096]{1,0:T(2,128)(2,1)S(1)} %get-tuple-element.10), channel_id=1, source_target_pairs={{0,1},{1,0},{2,3},{3,2},{4,5},{5,4},{6,7},{7,6},{8,9},{9,8},{10,11... | collective-permute-start | bytes 24584 | tf_op jit(solution)/shard_map/ppermute | solution.py:201

commit v2 on v1

v2 whole, which is shorter than its diff:
```python
import functools
import math

import jax
import jax.numpy as jnp
from jax import lax
from jax.experimental import pallas as pl
from jax.experimental.pallas import tpu as pltpu
from jax.sharding import Mesh
from jax.sharding import PartitionSpec as P


H = 32
KVH = 4
HD = 128
GROUPS = H // KVH
CORES = 2
POOL = ("y", "x", "c")
CHIPS = ("y", "x")
GRP_POOL = ("grp", "y", "x", "c")
RATE = math.log2(math.e) / math.sqrt(HD)
TWICE = math.log(2.0) * math.sqrt(HD)
UNUSED = -32768.0
HALF = H * HD // CORES
INTERPRET = False

f32 = jnp.float32
bf16 = jnp.bfloat16


def as_product(value):
    pairs = []
    for i in range(128):
        mark = 1.0 + i / 128.0
        unit = 2.0 ** (math.floor(math.log2(value / mark)) - 7)
        bias = round(value / mark / unit) * unit
        pairs.append((abs(mark * bias - value), mark, bias))
    return min(pairs)[1:]


MARK, BIAS = as_product(TWICE)


def row_body(length_ref, q_ref, holder_ref, slot_ref, out_ref):
    devices, _, part = out_ref.shape
    lane = lax.broadcasted_iota(jnp.int32, holder_ref.shape, 1)
    holder = jnp.where(lane < length_ref[0], holder_ref[...], -1).astype(f32)
    table = [holder, slot_ref[...].astype(f32)]
    for core in range(CORES):
        row = jnp.concatenate([q_ref[:, core * HALF : (core + 1) * HALF].astype(f32)] + table, axis=1)
        row = jnp.concatenate([row[:, :part], row[:, part:]], axis=0).astype(bf16)

        def put(i, carry, row=row, core=core):
            out_ref[i * CORES + core] = row
            return carry

        lax.fori_loop(0, devices // CORES, put, 0)


def blocks_body(pos_ref, own_ref, other_ref, k_ref, v_ref):
    slots, _, blk, _ = own_ref.shape
    tokens = slots * blk
    token_slot = lax.broadcasted_iota(jnp.int32, (2 * tokens, HD), 0) // blk
    slot_lane = lax.broadcasted_iota(jnp.int32, (2 * tokens, HD), 1)
    mark = jnp.where(slot_lane == token_slot, MARK, 0.0).astype(bf16)
    for g in range(KVH // CORES):
        k_ref[g, :, HD:] = mark
        v_ref[g, HD:, :] = jnp.ones((v_ref.shape[1] - HD, 2 * tokens), bf16)
        at = pl.multiple_of((pos_ref[1] * (KVH // CORES) + g) * HD, HD)
        for i, (ref, cols) in enumerate(((own_ref, pl.ds(at, HD)), (other_ref, slice(g * HD, (g + 1) * HD)))):
            rows = slice(i * tokens, (i + 1) * tokens)
            k_ref[g, rows, :HD] = ref[:, 0, :, cols].reshape(tokens, HD)
            v_ref[g, :HD, rows] = ref[:, 1, :, cols].reshape(tokens, HD).T


def attention_body(pos_ref, q_ref, k_hbm, v_hbm, out_ref, k_ref, v_ref, s_scr, p_scr, sems):
    rows = q_ref.shape[0]
    steps, tokens, _ = k_ref.shape
    loads = {}
    for g in range(steps):
        for n, (source, target) in enumerate(((k_hbm, k_ref), (v_hbm, v_ref))):
            loads[n, g] = pltpu.make_async_copy(source.at[g], target.at[g], sems.at[n, g])
            loads[n, g].start()
    slots = HD // 2
    me, core = pos_ref[0], pos_ref[1]
    partner = me + 1 - 2 * core
    holder = q_ref[:, HALF : HALF + HD].astype(f32)
    slot = q_ref[:, HALF + HD : HALF + 2 * HD].astype(f32)
    lane = lax.broadcasted_iota(jnp.int32, (rows, HD), 1)
    lane_slot = jnp.where(lane < slots, lane, lane - slots).astype(f32)

    def bias_of(device):
        hit = holder == device.astype(f32)
        first = jnp.min(jnp.where(hit, slot, 999.0), axis=1, keepdims=True)
        last = jnp.max(jnp.where(hit, slot, -1.0), axis=1, keepdims=True)
        count = jnp.sum(jnp.where(hit, 1.0, 0.0), axis=1, keepdims=True)
        used = (lane_slot == first) | (lane_slot == last)
        double = used & (first == last) & (count > 1.5)
        return jnp.where(used, jnp.where(double, BIAS, 0.0), UNUSED)

    bias = jnp.where(lane < slots, bias_of(me), bias_of(partner)).astype(bf16)

    pairs = steps * GROUPS // 2
    chunk = 512
    chunks = tokens // chunk
    queries, peaks, outs = {}, {}, {}
    for i in range(pairs + 2):
        if i < pairs:
            heads = [q_ref[:, (2 * i + j) * HD : (2 * i + j + 1) * HD] for j in range(2)]
            queries[i] = jnp.concatenate([jnp.concatenate([q, bias], axis=1) for q in heads], axis=0)
            peaks[i] = None
            if 2 * i % GROUPS == 0:
                loads[0, 2 * i // GROUPS].wait()
        if 0 <= i - 2 and 2 * (i - 2) % GROUPS == 0:
            loads[1, 2 * (i - 2) // GROUPS].wait()
        if 0 <= i - 1 < pairs:
            top = jnp.max(peaks[i - 1], axis=0, keepdims=True).astype(bf16)
            peaks[i - 1] = top.astype(f32)
            for h in range(2):
                g, head = divmod(2 * (i - 1) + h, GROUPS)
                for j in range(4):
                    out_ref[dest_of(g, head, j), 32:33, :] = top[:, h * rows : (h + 1) * rows]
        for k in range(chunks):
            at = slice(k * chunk, (k + 1) * chunk)
            if i < pairs:
                s = lax.dot_general(
                    k_ref[2 * i // GROUPS, at, :], queries[i], (((1,), (1,)), ((), ())), preferred_element_type=f32
                )
                s_scr[i % 2, at, :] = s
                peak = jnp.max(s.reshape(chunk // 8, 8, 2 * rows), axis=0)
                peaks[i] = peak if peaks[i] is None else jnp.maximum(peaks[i], peak)
            if 0 <= i - 1 < pairs:
                n = i - 1
                p_scr[n % 2, at, :] = jnp.exp2((s_scr[n % 2, at, :] - peaks[n]) * RATE).astype(bf16)
            if 0 <= i - 2:
                n = i - 2
                out = jnp.dot(v_ref[2 * n // GROUPS, :, at], p_scr[n % 2, at, :], preferred_element_type=f32)
                outs[n] = out if k == 0 else outs[n] + out
        if 0 <= i - 2:
            out = outs.pop(i - 2)
            for h in range(2):
                g, head = divmod(2 * (i - 2) + h, GROUPS)
                cols = slice(h * rows, (h + 1) * rows)
                total = out[HD : HD + 1, cols]
                high = total.astype(bf16)
                low = (total - high.astype(f32)).astype(bf16)
                for j in range(4):
                    dest = dest_of(g, head, j)
                    out_ref[dest, 0:32, :] = out[j * 32 : (j + 1) * 32, cols].astype(bf16)
                    out_ref[dest, 33:34, :] = high
                    out_ref[dest, 34:35, :] = low


def dest_of(g, h, j):
    return ((j % 2) * 4 + g * 2 + h // 4) * 8 + (h % 4) * 2 + j // 2


def merge_body(got_ref, out_ref, f_scr):
    chips, _, rows = got_ref.shape
    peaks = [got_ref[i, 32:33, :].astype(f32) for i in range(chips)]
    top = functools.reduce(jnp.maximum, peaks)
    total = jnp.zeros((1, rows), f32)
    number = jnp.zeros((32, rows), f32)
    for i in range(chips):
        factor = jnp.exp2((peaks[i] - top) * RATE)
        total += factor * (got_ref[i, 33:34, :].astype(f32) + got_ref[i, 34:35, :].astype(f32))
        number += factor * got_ref[i, 0:32, :].astype(f32)
    attention = number / total
    high = attention.astype(bf16)
    out_ref[0:32, :] = high
    out_ref[32:64, :] = (attention - high.astype(f32)).astype(bf16)


def project_body(pos_ref, mine_ref, got_ref, w_ref, w_got_ref, out_ref):
    core = pos_ref[1]
    half = w_got_ref.shape[1]
    left = jnp.concatenate([mine_ref[...], got_ref[...]], axis=0)
    step = 512
    for i in range(half // step):
        cols = pl.ds(pl.multiple_of(core * half + i * step, step), step)
        mine = w_ref[:, cols]
        got = w_got_ref[:, i * step : (i + 1) * step]
        right = jnp.concatenate([mine, mine, got, got], axis=0)
        part = lax.dot_general(left, right, (((0,), (0,)), ((), ())), preferred_element_type=f32)
        out_ref[:, i * step : (i + 1) * step] = part.astype(bf16)


def small_call(body, out, *args, scalars=(), scratch=(), mib=8, flops=0, large=0):
    smem = pl.BlockSpec(memory_space=pltpu.SMEM)
    vmem = pl.BlockSpec(memory_space=pltpu.VMEM)
    return pl.pallas_call(
        body,
        out_shape=out,
        in_specs=[smem] * len(scalars) + [vmem] * (len(args) - large) + [pl.BlockSpec(memory_space=pltpu.HBM)] * large,
        out_specs=jax.tree.map(lambda _: vmem, out),
        scratch_shapes=list(scratch),
        cost_estimate=pl.CostEstimate(flops=flops, transcendentals=0, bytes_accessed=0) if flops else None,
        compiler_params=pltpu.CompilerParams(vmem_limit_bytes=mib << 20),
        interpret=INTERPRET,
    )(*scalars, *args)


def swapped(v):
    return lax.ppermute(v, "c", [(0, 1), (1, 0)])


def weight_moves(ny, nx, nc):
    pairs = []
    for y in range(ny):
        for x in range(nx):
            for c in range(nc):
                upper = y // (ny // 2)
                at = (y * nx + x) * nc + c
                other = (((y + ny // 2) % ny) * nx + x) * nc + 1 - c
                pairs.append((at, at if upper == c else other))
    return pairs


def per_device(query, kv_pool, holder_table, slot_table, lengths, out_weight):
    ny, nx, nc = (lax.axis_size(a) for a in POOL)
    y, x, c = (lax.axis_index(a) for a in POOL)
    chips = ny * nx
    pos = jnp.stack([(y * nx + x) * nc + c, c]).astype(jnp.int32)

    devices = chips * nc
    width = HALF + 2 * holder_table.shape[1]
    row_shape = jax.ShapeDtypeStruct((devices, 2, width // 2), bf16)
    rows = small_call(row_body, row_shape, query, holder_table, slot_table, scalars=(lengths,))
    q = lax.all_to_all(rows, POOL, split_axis=0, concat_axis=0, tiled=True)

    kv_half = kv_pool.shape[-1] // nc
    kv_other = swapped(lax.dynamic_slice_in_dim(kv_pool, (1 - c) * kv_half, kv_half, axis=3))
    tokens = nc * kv_pool.shape[0] * kv_pool.shape[2]
    steps = KVH // nc
    shapes = [jax.ShapeDtypeStruct((steps, tokens, 2 * HD), bf16), jax.ShapeDtypeStruct((steps, HD + 16, tokens), bf16)]
    keys, values = small_call(blocks_body, shapes, kv_pool, kv_other, scalars=(pos,), flops=1 << 32)

    q, out_weight = lax.optimization_barrier((q.reshape(devices, width), out_weight))
    weight = lax.ppermute(out_weight, POOL, weight_moves(ny, nx, nc))
    parts = small_call(
        attention_body,
        jax.ShapeDtypeStruct((chips, 40, devices), bf16),
        q,
        keys,
        values,
        scalars=(pos,),
        scratch=[
            *(pltpu.VMEM(v.shape, v.dtype) for v in shapes),
            pltpu.VMEM((2, tokens, 2 * devices), f32),
            pltpu.VMEM((2, tokens, 2 * devices), bf16),
            pltpu.SemaphoreType.DMA((2, steps)),
        ],
        mib=62,
        large=2,
        flops=1 << 34,
    )
    parts = lax.all_to_all(parts, CHIPS, split_axis=0, concat_axis=0, tiled=True)

    d_half = weight.shape[1] // nc
    w_got = swapped(lax.dynamic_slice_in_dim(weight, (1 - c) * d_half, d_half, axis=1))
    mine = small_call(merge_body, jax.ShapeDtypeStruct((64, chips * nc), bf16), parts,
                      scratch=[pltpu.VMEM((chips, chips * nc), f32)])
    got = swapped(mine)
    partial = small_call(
        project_body,
        jax.ShapeDtypeStruct((chips * nc, d_half), bf16),
        mine,
        got,
        weight,
        w_got,
        scalars=(pos,),
    )
    columns = lax.all_to_all(
        partial.reshape(chips, nc, d_half), CHIPS, split_axis=0, concat_axis=0, tiled=True
    )
    done = jnp.sum(columns.astype(f32), axis=0).astype(bf16)
    keep = lax.dynamic_slice_in_dim(done, c, 1, axis=0)
    got = swapped(lax.dynamic_slice_in_dim(done, 1 - c, 1, axis=0))
    return jnp.where(c == 0, jnp.concatenate([keep, got], axis=1), jnp.concatenate([got, keep], axis=1))


def solution(mesh):
    torus = Mesh(mesh.devices.reshape(mesh.shape["grp"], 8, 8, 2), GRP_POOL)
    return jax.shard_map(
        per_device,
        mesh=torus,
        in_specs=(
            P(GRP_POOL, None),
            P(GRP_POOL, None, None, None),
            P(GRP_POOL, None),
            P(GRP_POOL, None),
            P(GRP_POOL),
            P(POOL, None),
        ),
        out_specs=P(GRP_POOL, None),
        check_vma=False,
    )
```

time: 153 us -> 149 us (0.974)
  other arithmetic: 4.39 us -> 1.67 us
  starting transfers between devices: 56.8 us -> 54.3 us
    all_to_all x1, starting transfers between devices: 28.2 us -> 8.12 us  [per_device(): q = lax.all_to_all(rows, POOL, split_axis=0, concat_axis=0, tiled=True)]
    ppermute x4, starting transfers between devices: 6.22 us -> 23.5 us  [swapped(): return lax.ppermute(v, 'c', [(0, 1), (1, 0)])]
    pallas_call x1 -> x0, Pallas kernels: 13.2 us -> none  [attention_partials(): pl.pallas_call(attention_body, grid_spec=pltpu.PrefetchScalarGridSpec(num...]
    pallas_call x2 -> x5, Pallas kernels: 1.25 us -> 13.6 us  [small_call(): pl.pallas_call(body, out_shape=out, in_specs=[smem] * len(scalars) + [vme...]
    unnamed x3 -> x0, other arithmetic: 2 us -> none
    unnamed x5 -> x19, local copies, waits for them, and re-layouts: 2.55 us -> 4.35 us
  transfers between devices with their start and end apart: 8 -> 8, of which waited for: 6 -> 6; matrix products, arithmetic and copies ran while one was open for 2% -> 0% of each run, Pallas kernels for 0% -> 2%
where the time goes in v2:
time: 149 us; the launch traced here: 148 us
  waiting for transfers between devices  69.7 us (47%)
  starting transfers between devices  54.3 us (36%)
  Pallas kernels  13.6 us (9%)
  local copies, waits for them, and re-layouts  8.32 us (6%)
  other arithmetic  1.67 us (1%)
    all_to_all x1, waiting for transfers between devices, per_device(): lax.all_to_all(partial.reshape(chips, nc, d_half), CHIPS, split_axis=0, c...  27 us
    ppermute x1, waiting for transfers between devices, per_device(): weight = lax.ppermute(out_weight, POOL, weight_moves(ny, nx, nc))  23.9 us
    ppermute x4, starting transfers between devices, swapped(): return lax.ppermute(v, 'c', [(0, 1), (1, 0)])  23.5 us
    all_to_all x1, waiting for transfers between devices, per_device(): q = lax.all_to_all(rows, POOL, split_axis=0, concat_axis=0, tiled=True)  17.1 us
    pallas_call x5, Pallas kernels, small_call(): pl.pallas_call(body, out_shape=out, in_specs=[smem] * len(scalars) + [vme...  13.6 us
    all_to_all x1, starting transfers between devices, per_device(): lax.all_to_all(partial.reshape(chips, nc, d_half), CHIPS, split_axis=0, c...  9.2 us
    all_to_all x1, starting transfers between devices, per_device(): q = lax.all_to_all(rows, POOL, split_axis=0, concat_axis=0, tiled=True)  8.12 us
    ppermute x1, starting transfers between devices, per_device(): weight = lax.ppermute(out_weight, POOL, weight_moves(ny, nx, nc))  6.77 us
  transfers between devices with their start and end apart: 8, of which 6 were waited for; matrix products, arithmetic and copies ran while one was open for 0% of the time, Pallas kernels for 2%

profile of v2, /device:TPU:513, one launch (start us, length us, event | category | flops | bytes accessed | tf_op | source)
XLA Modules:
  0.0 148.4 jit_solution(1244937470154816193)
XLA Ops:
  0.0 0.0 copy-start.3
  0.0 2.4 %constant_dynamic-slice_fusion.3 = bf16[64,2,16,256]{3,2,1,0:T(8,128)(2,1)} fusion(bf16[64,2,16,512]{3,2,1,0:T(8,128)(2,1)} %own_ref.1, s32[]{:T(128)S(6)} %select_n.29), kind=kLoop, calls=%fused_computation.4 | loop fusion | bytes 2097156 | tf_op jit(solution)/shard_map/dynamic_slice | solution.py:232
  2.4 20.4 %collective-permute-start = (bf16[64,2,16,256]{3,2,1,0:T(8,128)(2,1)}, bf16[64,2,16,256]{3,2,1,0:T(8,128)(2,1)S(1)}, u32[]{:S(2)}, u32[]{:S(2)}) collective-permute-start(bf16[64,2,16,256]{3,2,1,0:T(8,128)(2,1)} %constant_dynamic-slice_fusion.3), channel_id=1, source_target_pairs={{0,1},{1,0},{2,3},{3,2},{4,5},{5,4},{6,7},{7,6},{8,9},{9,8},{10,11... | collective-permute-start | bytes 3145736 | tf_op jit(solution)/shard_map/ppermute | solution.py:204
  23.5 1.8 %shard_map.64 = bf16[128,2,1152]{2,1,0:T(2,128)(2,1)} custom-call(s32[1]{0:T(128)S(6)} %copy.8.length_ref, bf16[1,4096]{1,0:T(2,128)(2,1)S(1)} %copy-done.1, s32[1,128]{1,0:T(1,128)S(1)} %copy-done.2, s32[1,128]{1,0:T(1,128)S(1)} %copy-done.3), custom_call_target="tpu_custom_call" | custom-call | tf_op jit(solution)/shard_map/pallas_call | solution.py:191
  25.3 8.1 %all-to-all-start = ((bf16[128,2,1152]{2,1,0:T(2,128)(2,1)}), bf16[128,2,1152]{2,1,0:T(2,128)(2,1)}, u32[]{:S(2)}, u32[]{:S(2)}) async-start(bf16[128,2,1152]{2,1,0:T(2,128)(2,1)} %shard_map.64), calls=%async_computation | async-start | bytes 1179648 | tf_op jit(solution)/shard_map/all_to_all | solution.py:229
  33.5 0.1 pad_add_fusion.pos_ref
  33.5 0.0 collective-permute-done.other_ref
  33.5 0.0 copy-done
  33.6 1.3 shard_map.65
  34.9 1.3 copy-done.6
  36.2 1.0 copy-done.7
  37.3 17.1 %all-to-all-done = bf16[128,2,1152]{2,1,0:T(2,128)(2,1)} async-done(((bf16[128,2,1152]{2,1,0:T(2,128)(2,1)}), bf16[128,2,1152]{2,1,0:T(2,128)(2,1)}, u32[]{:S(2)}, u32[]{:S(2)}) %all-to-all-start) | async-done | bytes 589856 | tf_op jit(solution)/shard_map/all_to_all | solution.py:229
  54.3 1.9 %copy.7 = bf16[16,8,2,1152]{3,1,2,0:T(8,128)(2,1)} copy(bf16[16,8,2,1152]{3,2,1,0:T(2,128)(2,1)} %bitcast.2) | data formatting | bytes 1179648
  56.3 9.2 %shard_map.66 = bf16[64,40,128]{2,1,0:T(8,128)(2,1)} custom-call(s32[2]{0:T(128)} %copy-done.4, bf16[128,2304]{1,0:T(8,128)(2,1)} %bitcast.4, bf16[2,2048,256]{2,1,0:T(8,128)(2,1)} %copy-done.6, bf16[2,144,2048]{2,1,0:T(8,128)(2,1)} %copy-done.7), custom_call_target="tpu_custom_call" | custom-call | flops 17179869184 | tf_op jit(solution)/shard_map/pallas_call | solution.py:191
  65.5 6.7 %all-to-all-start.1 = ((bf16[64,40,128]{2,1,0:T(8,128)(2,1)}), bf16[64,40,128]{2,1,0:T(8,128)(2,1)S(1)}, u32[]{:S(2)}, u32[]{:S(2)}) async-start(bf16[64,40,128]{2,1,0:T(8,128)(2,1)} %shard_map.66), calls=%async_computation.1 | async-start | bytes 1310720 | tf_op jit(solution)/shard_map/all_to_all | solution.py:257
  72.2 6.8 %collective-permute-start.2 = (bf16[32,8192]{1,0:T(8,128)(2,1)S(1)}, bf16[32,8192]{1,0:T(8,128)(2,1)S(1)}, u32[]{:S(2)}, u32[]{:S(2)}) collective-permute-start(bf16[32,8192]{1,0:T(8,128)(2,1)S(1)} %copy-done.8), channel_id=1, source_target_pairs={{0,0},{1,64},{2,2},{3,66},{4,4},{5,68},{6,6},{7,70},{8,8},{9,72},{... | collective-permute-start | bytes 1572872 | tf_op jit(solution)/shard_map/ppermute | solution.py:239
  79.0 23.9 %collective-permute-done.2.w_ref = bf16[32,8192]{1,0:T(8,128)(2,1)S(1)} collective-permute-done((bf16[32,8192]{1,0:T(8,128)(2,1)S(1)}, bf16[32,8192]{1,0:T(8,128)(2,1)S(1)}, u32[]{:S(2)}, u32[]{:S(2)}) %collective-permute-start.2) | collective-permute-done | bytes 524320 | tf_op jit(solution)/shard_map/ppermute | solution.py:239
  103.0 0.1 collective-permute-start.3
  103.1 0.0 all-to-all-done.1.got_ref
  103.1 0.3 shard_map.67.mine_ref
  103.4 0.6 collective-permute-start.1
  104.0 0.6 collective-permute-done.3.w_got_ref
  104.6 0.2 collective-permute-done.1.got_ref
  104.8 0.0 copy-done.5
  104.8 1.0 shard_map.68
  105.8 1.5 %reshape.59 = bf16[64,2,4096]{2,1,0:T(2,128)(2,1)} reshape(bf16[128,4096]{1,0:T(8,128)(2,1)S(1)} %shard_map.68) | data formatting | bytes 2097152 | tf_op jit(solution)/shard_map/reshape | solution.py:274
  107.3 9.2 %all-to-all-start.2 = ((bf16[64,2,4096]{2,1,0:T(2,128)(2,1)}), bf16[64,2,4096]{2,1,0:T(2,128)(2,1)S(1)}, u32[]{:S(2)}, u32[]{:S(2)}) async-start(bf16[64,2,4096]{2,1,0:T(2,128)(2,1)} %reshape.59), calls=%async_computation.2 | async-start | bytes 2097152 | tf_op jit(solution)/shard_map/all_to_all | solution.py:273
  116.5 27.0 %all-to-all-done.2 = bf16[64,2,4096]{2,1,0:T(2,128)(2,1)S(1)} async-done(((bf16[64,2,4096]{2,1,0:T(2,128)(2,1)}), bf16[64,2,4096]{2,1,0:T(2,128)(2,1)S(1)}, u32[]{:S(2)}, u32[]{:S(2)}) %all-to-all-start.2) | async-done | bytes 1048608 | tf_op jit(solution)/shard_map/all_to_all | solution.py:273
  143.5 0.9 reduce_sum.12
  144.5 2.4 %collective-permute-start.4 = (bf16[1,4096]{1,0:T(2,128)(2,1)S(1)}, bf16[1,4096]{1,0:T(2,128)(2,1)S(1)}, u32[]{:S(2)}, u32[]{:S(2)}) collective-permute-start(bf16[1,4096]{1,0:T(2,128)(2,1)S(1)} %get-tuple-element.14), channel_id=1, source_target_pairs={{0,1},{1,0},{2,3},{3,2},{4,5},{5,4},{6,7},{7,6},{8,9},{9,8},{10,11... | collective-permute-start | bytes 24584 | tf_op jit(solution)/shard_map/ppermute | solution.py:204
  146.9 0.8 collective-permute-done.4
  147.7 0.7 broadcast_select_fusion
  (15 shorter events, 0.1 us)
Async XLA Ops:
  0.0 33.5 %copy-start = (bf16[64,2,16,512]{3,2,1,0:T(8,128)(2,1)S(1)}, bf16[64,2,16,512]{3,2,1,0:T(8,128)(2,1)}, u32[]{:S(2)}) copy-start(bf16[64,2,16,512]{3,2,1,0:T(8,128)(2,1)} %own_ref.1) | copy-start | bytes 6291460
  0.0 23.5 %copy-start.1 = (bf16[1,4096]{1,0:T(2,128)(2,1)S(1)}, bf16[1,4096]{1,0:T(2,128)(2,1)}, u32[]{:S(2)}) copy-start(bf16[1,4096]{1,0:T(2,128)(2,1)} %q_ref.1) | copy-start | bytes 24580
  0.0 23.5 %copy-start.2 = (s32[1,128]{1,0:T(1,128)S(1)}, s32[1,128]{1,0:T(1,128)}, u32[]{:S(2)}) copy-start(s32[1,128]{1,0:T(1,128)} %holder_ref.1) | copy-start | bytes 1540
  0.0 23.5 %copy-start.3 = (s32[1,128]{1,0:T(1,128)S(1)}, s32[1,128]{1,0:T(1,128)}, u32[]{:S(2)}) copy-start(s32[1,128]{1,0:T(1,128)} %slot_ref.1) | copy-start | bytes 1540
  2.4 31.1 %collective-permute-start = (bf16[64,2,16,256]{3,2,1,0:T(8,128)(2,1)}, bf16[64,2,16,256]{3,2,1,0:T(8,128)(2,1)S(1)}, u32[]{:S(2)}, u32[]{:S(2)}) collective-permute-start(bf16[64,2,16,256]{3,2,1,0:T(8,128)(2,1)} %constant_dynamic-slice_fusion.3), channel_id=1, source_target_pairs={{0,1},{1,0},{2,3},{3,2},{4,5},{5,4},{6,7},{7,6},{8,9},{9,8},{10,11... | collective-permute-start | bytes 3145736 | tf_op jit(solution)/shard_map/ppermute | solution.py:204
  25.3 29.0 %all-to-all-start = ((bf16[128,2,1152]{2,1,0:T(2,128)(2,1)}), bf16[128,2,1152]{2,1,0:T(2,128)(2,1)}, u32[]{:S(2)}, u32[]{:S(2)}) async-start(bf16[128,2,1152]{2,1,0:T(2,128)(2,1)} %shard_map.64), calls=%async_computation | async-start | bytes 1179648 | tf_op jit(solution)/shard_map/all_to_all | solution.py:229
  33.5 1.3 copy-start.4
  34.9 1.3 copy-start.6
  36.2 1.0 copy-start.7
  56.3 15.9 %copy-start.8 = (bf16[32,8192]{1,0:T(8,128)(2,1)S(1)}, bf16[32,8192]{1,0:T(8,128)(2,1)}, u32[]{:S(2)}) copy-start(bf16[32,8192]{1,0:T(8,128)(2,1)} %param.11) | copy-start | bytes 1572868
  65.5 39.3 %copy-start.5 = (s32[2]{0:T(128)S(1)}, s32[2]{0:T(128)}, u32[]{:S(2)}) copy-start(s32[2]{0:T(128)} %copy-done.4) | copy-start | bytes 28
  65.5 37.6 %all-to-all-start.1 = ((bf16[64,40,128]{2,1,0:T(8,128)(2,1)}), bf16[64,40,128]{2,1,0:T(8,128)(2,1)S(1)}, u32[]{:S(2)}, u32[]{:S(2)}) async-start(bf16[64,40,128]{2,1,0:T(8,128)(2,1)} %shard_map.66), calls=%async_computation.1 | async-start | bytes 1310720 | tf_op jit(solution)/shard_map/all_to_all | solution.py:257
  72.2 30.7 %collective-permute-start.2 = (bf16[32,8192]{1,0:T(8,128)(2,1)S(1)}, bf16[32,8192]{1,0:T(8,128)(2,1)S(1)}, u32[]{:S(2)}, u32[]{:S(2)}) collective-permute-start(bf16[32,8192]{1,0:T(8,128)(2,1)S(1)} %copy-done.8), channel_id=1, source_target_pairs={{0,0},{1,64},{2,2},{3,66},{4,4},{5,68},{6,6},{7,70},{8,8},{9,72},{... | collective-permute-start | bytes 1572872 | tf_op jit(solution)/shard_map/ppermute | solution.py:239
  103.0 1.7 %collective-permute-start.3 = (bf16[32,4096]{1,0:T(8,128)(2,1)S(1)}, bf16[32,4096]{1,0:T(8,128)(2,1)S(1)}, u32[]{:S(2)}, u32[]{:S(2)}) collective-permute-start(bf16[32,4096]{1,0:T(8,128)(2,1)S(1)} %constant_dynamic-slice_fusion.2), channel_id=1, source_target_pairs={{0,1},{1,0},{2,3},{3,2},{4,5},{5,4},{6,7},{7,6},{8,9},{9,8},{10,11... | collective-permute-start | bytes 786440 | tf_op jit(solution)/shard_map/ppermute | solution.py:204
  103.4 1.4 collective-permute-start.1
  107.3 36.2 %all-to-all-start.2 = ((bf16[64,2,4096]{2,1,0:T(2,128)(2,1)}), bf16[64,2,4096]{2,1,0:T(2,128)(2,1)S(1)}, u32[]{:S(2)}, u32[]{:S(2)}) async-start(bf16[64,2,4096]{2,1,0:T(2,128)(2,1)} %reshape.59), calls=%async_computation.2 | async-start | bytes 2097152 | tf_op jit(solution)/shard_map/all_to_all | solution.py:273
  144.5 3.2 %collective-permute-start.4 = (bf16[1,4096]{1,0:T(2,128)(2,1)S(1)}, bf16[1,4096]{1,0:T(2,128)(2,1)S(1)}, u32[]{:S(2)}, u32[]{:S(2)}) collective-permute-start(bf16[1,4096]{1,0:T(2,128)(2,1)S(1)} %get-tuple-element.14), channel_id=1, source_target_pairs={{0,1},{1,0},{2,3},{3,2},{4,5},{5,4},{6,7},{7,6},{8,9},{9,8},{10,11... | collective-permute-start | bytes 24584 | tf_op jit(solution)/shard_map/ppermute | solution.py:204

commit v3 on v2

--- a/solution.py
+++ b/solution.py
@@ -22,6 +22,8 @@
 TWICE = math.log(2.0) * math.sqrt(HD)
 UNUSED = -32768.0
 HALF = H * HD // CORES
+TILE = 2 * HD
+VROWS = HD + 16
 INTERPRET = False
 
 f32 = jnp.float32
@@ -57,29 +59,32 @@
         lax.fori_loop(0, devices // CORES, put, 0)
 
 
-def blocks_body(pos_ref, own_ref, other_ref, k_ref, v_ref):
+def blocks_body(pos_ref, own_ref, other_ref, out_ref):
     slots, _, blk, _ = own_ref.shape
     tokens = slots * blk
     token_slot = lax.broadcasted_iota(jnp.int32, (2 * tokens, HD), 0) // blk
     slot_lane = lax.broadcasted_iota(jnp.int32, (2 * tokens, HD), 1)
     mark = jnp.where(slot_lane == token_slot, MARK, 0.0).astype(bf16)
     for g in range(KVH // CORES):
-        k_ref[g, :, HD:] = mark
-        v_ref[g, HD:, :] = jnp.ones((v_ref.shape[1] - HD, 2 * tokens), bf16)
-        at = pl.multiple_of((pos_ref[1] * (KVH // CORES) + g) * HD, HD)
-        for i, (ref, cols) in enumerate(((own_ref, pl.ds(at, HD)), (other_ref, slice(g * HD, (g + 1) * HD)))):
-            rows = slice(i * tokens, (i + 1) * tokens)
-            k_ref[g, rows, :HD] = ref[:, 0, :, cols].reshape(tokens, HD)
-            v_ref[g, :HD, rows] = ref[:, 1, :, cols].reshape(tokens, HD).T
-
-
-def attention_body(pos_ref, q_ref, k_hbm, v_hbm, out_ref, k_ref, v_ref, s_scr, p_scr, sems):
+        out_ref[g, : 2 * tokens, HD:] = mark
+        at = pl.ds(pl.multiple_of((pos_ref[1] * (KVH // CORES) + g) * HD, HD), HD)
+        for i, ref in enumerate((own_ref, other_ref)):
+            out_ref[g, i * tokens : (i + 1) * tokens, :HD] = ref[:, 0, :, at].reshape(tokens, HD)
+            turned = ref[:, 1, :, at].reshape(tokens, HD).T
+            for j in range(tokens // TILE):
+                row = 2 * tokens + (i * (tokens // TILE) + j) * VROWS
+                out_ref[g, row : row + HD, :] = turned[:, j * TILE : (j + 1) * TILE]
+                out_ref[g, row + HD : row + VROWS, :] = jnp.ones((VROWS - HD, TILE), bf16)
+
+
+def attention_body(pos_ref, q_ref, kv_hbm, out_ref, kv_ref, s_scr, p_scr, sems):
     rows = q_ref.shape[0]
-    steps, tokens, _ = k_ref.shape
+    steps = kv_ref.shape[0]
+    tokens = s_scr.shape[1]
     loads = {}
     for g in range(steps):
-        for n, (source, target) in enumerate(((k_hbm, k_ref), (v_hbm, v_ref))):
-            loads[n, g] = pltpu.make_async_copy(source.at[g], target.at[g], sems.at[n, g])
+        for n, at in enumerate((slice(0, tokens), slice(tokens, kv_ref.shape[1]))):
+            loads[n, g] = pltpu.make_async_copy(kv_hbm.at[g, at], kv_ref.at[g, at], sems.at[n, g])
             loads[n, g].start()
     slots = HD // 2
     me, core = pos_ref[0], pos_ref[1]
@@ -124,7 +129,7 @@
             at = slice(k * chunk, (k + 1) * chunk)
             if i < pairs:
                 s = lax.dot_general(
-                    k_ref[2 * i // GROUPS, at, :], queries[i], (((1,), (1,)), ((), ())), preferred_element_type=f32
+                    kv_ref[2 * i // GROUPS, at, :], queries[i], (((1,), (1,)), ((), ())), preferred_element_type=f32
                 )
                 s_scr[i % 2, at, :] = s
                 peak = jnp.max(s.reshape(chunk // 8, 8, 2 * rows), axis=0)
@@ -134,7 +139,11 @@
                 p_scr[n % 2, at, :] = jnp.exp2((s_scr[n % 2, at, :] - peaks[n]) * RATE).astype(bf16)
             if 0 <= i - 2:
                 n = i - 2
-                out = jnp.dot(v_ref[2 * n // GROUPS, :, at], p_scr[n % 2, at, :], preferred_element_type=f32)
+                tiles = [
+                    kv_ref[2 * n // GROUPS, tokens + j * VROWS : tokens + (j + 1) * VROWS, :]
+                    for j in range(k * chunk // TILE, (k + 1) * chunk // TILE)
+                ]
+                out = jnp.dot(jnp.concatenate(tiles, axis=1), p_scr[n % 2, at, :], preferred_element_type=f32)
                 outs[n] = out if k == 0 else outs[n] + out
         if 0 <= i - 2:
             out = outs.pop(i - 2)
@@ -155,7 +164,7 @@
     return ((j % 2) * 4 + g * 2 + h // 4) * 8 + (h % 4) * 2 + j // 2
 
 
-def merge_body(got_ref, out_ref, f_scr):
+def merge_body(got_ref, out_ref):
     chips, _, rows = got_ref.shape
     peaks = [got_ref[i, 32:33, :].astype(f32) for i in range(chips)]
     top = functools.reduce(jnp.maximum, peaks)
@@ -171,18 +180,16 @@
     out_ref[32:64, :] = (attention - high.astype(f32)).astype(bf16)
 
 
-def project_body(pos_ref, mine_ref, got_ref, w_ref, w_got_ref, out_ref):
-    core = pos_ref[1]
-    half = w_got_ref.shape[1]
-    left = jnp.concatenate([mine_ref[...], got_ref[...]], axis=0)
+def project_body(*refs):
+    count = len(refs) // 2
+    lefts, rights, out_ref = refs[:count], refs[count:-1], refs[-1]
+    left = jnp.concatenate([r[...] for r in lefts], axis=0)
     step = 512
-    for i in range(half // step):
-        cols = pl.ds(pl.multiple_of(core * half + i * step, step), step)
-        mine = w_ref[:, cols]
-        got = w_got_ref[:, i * step : (i + 1) * step]
-        right = jnp.concatenate([mine, mine, got, got], axis=0)
+    for i in range(out_ref.shape[1] // step):
+        cols = slice(i * step, (i + 1) * step)
+        right = jnp.concatenate([r[:, cols] for r in rights for _ in range(2)], axis=0)
         part = lax.dot_general(left, right, (((0,), (0,)), ((), ())), preferred_element_type=f32)
-        out_ref[:, i * step : (i + 1) * step] = part.astype(bf16)
+        out_ref[:, cols] = part.astype(bf16)
 
 
 def small_call(body, out, *args, scalars=(), scratch=(), mib=8, flops=0, large=0):
@@ -204,6 +211,12 @@
     return lax.ppermute(v, "c", [(0, 1), (1, 0)])
 
 
+def to_mate(v, k):
+    nx, nc = lax.axis_size("x"), lax.axis_size("c")
+    perm = [(x * nc + c, (x ^ (k // nc)) * nc + (c ^ (k % nc))) for x in range(nx) for c in range(nc)]
+    return lax.ppermute(v, ("x", "c"), perm)
+
+
 def weight_moves(ny, nx, nc):
     pairs = []
     for y in range(ny):
@@ -226,57 +239,51 @@
     width = HALF + 2 * holder_table.shape[1]
     row_shape = jax.ShapeDtypeStruct((devices, 2, width // 2), bf16)
     rows = small_call(row_body, row_shape, query, holder_table, slot_table, scalars=(lengths,))
+    weight = lax.ppermute(out_weight, POOL, weight_moves(ny, nx, nc))
     q = lax.all_to_all(rows, POOL, split_axis=0, concat_axis=0, tiled=True)
 
-    kv_half = kv_pool.shape[-1] // nc
-    kv_other = swapped(lax.dynamic_slice_in_dim(kv_pool, (1 - c) * kv_half, kv_half, axis=3))
+    kv_other = swapped(kv_pool)
     tokens = nc * kv_pool.shape[0] * kv_pool.shape[2]
     steps = KVH // nc
-    shapes = [jax.ShapeDtypeStruct((steps, tokens, 2 * HD), bf16), jax.ShapeDtypeStruct((steps, HD + 16, tokens), bf16)]
-    keys, values = small_call(blocks_body, shapes, kv_pool, kv_other, scalars=(pos,), flops=1 << 32)
-
-    q, out_weight = lax.optimization_barrier((q.reshape(devices, width), out_weight))
-    weight = lax.ppermute(out_weight, POOL, weight_moves(ny, nx, nc))
+    kv_shape = (steps, tokens + tokens // TILE * VROWS, TILE)
+    blocks = small_call(
+        blocks_body, jax.ShapeDtypeStruct(kv_shape, bf16), kv_pool, kv_other, scalars=(pos,), flops=1 << 32
+    )
+
+    mates = 2 * nc
+    mate = (x % 2) * nc + c
+    d_part = weight.shape[1] // mates
+    weights = []
+    for k in range(mates):
+        part = lax.dynamic_slice_in_dim(weight, (mate ^ k) * d_part, d_part, axis=1)
+        weights.append(to_mate(part, k) if k else part)
+
+    q, *weights = lax.optimization_barrier((q.reshape(devices, width), *weights))
     parts = small_call(
         attention_body,
         jax.ShapeDtypeStruct((chips, 40, devices), bf16),
         q,
-        keys,
-        values,
+        blocks,
         scalars=(pos,),
         scratch=[
-            *(pltpu.VMEM(v.shape, v.dtype) for v in shapes),
+            pltpu.VMEM(kv_shape, bf16),
             pltpu.VMEM((2, tokens, 2 * devices), f32),
             pltpu.VMEM((2, tokens, 2 * devices), bf16),
             pltpu.SemaphoreType.DMA((2, steps)),
         ],
-        mib=62,
-        large=2,
+        mib=52,
+        large=1,
         flops=1 << 34,
     )
     parts = lax.all_to_all(parts, CHIPS, split_axis=0, concat_axis=0, tiled=True)
-
-    d_half = weight.shape[1] // nc
-    w_got = swapped(lax.dynamic_slice_in_dim(weight, (1 - c) * d_half, d_half, axis=1))
-    mine = small_call(merge_body, jax.ShapeDtypeStruct((64, chips * nc), bf16), parts,
-                      scratch=[pltpu.VMEM((chips, chips * nc), f32)])
-    got = swapped(mine)
-    partial = small_call(
-        project_body,
-        jax.ShapeDtypeStruct((chips * nc, d_half), bf16),
-        mine,
-        got,
-        weight,
-        w_got,
-        scalars=(pos,),
+    mine = small_call(merge_body, jax.ShapeDtypeStruct((64, devices), bf16), parts)
+    lefts = [to_mate(mine, k) if k else mine for k in range(mates)]
+    partial = small_call(project_body, jax.ShapeDtypeStruct((devices, d_part), bf16), *lefts, *weights)
+    columns = lax.all_to_all(
+        partial.reshape(devices, 2, d_part // 2), POOL, split_axis=0, concat_axis=0, tiled=True
     )
-    columns = lax.all_to_all(
-        partial.reshape(chips, nc, d_half), CHIPS, split_axis=0, concat_axis=0, tiled=True
-    )
-    done = jnp.sum(columns.astype(f32), axis=0).astype(bf16)
-    keep = lax.dynamic_slice_in_dim(done, c, 1, axis=0)
-    got = swapped(lax.dynamic_slice_in_dim(done, 1 - c, 1, axis=0))
-    return jnp.where(c == 0, jnp.concatenate([keep, got], axis=1), jnp.concatenate([got, keep], axis=1))
+    done = jnp.sum(columns.reshape(devices // mates, mates, d_part).astype(f32), axis=0).astype(bf16)
+    return done.reshape(1, mates * d_part)
 
 
 def solution(mesh):

time: 149 us -> 147 us (0.987)
  blocking collectives: 0 us -> 58.1 us
  waiting for transfers between devices: 69.7 us -> 24 us
  starting transfers between devices: 54.3 us -> 44.1 us
  local copies, waits for them, and re-layouts: 8.32 us -> 6.22 us
    all_to_all x0 -> x2, blocking collectives: none -> 58.1 us  [the longest x1 30.2 us: per_device(): lax.all_to_all(parts, CHIPS, split_axis=0, concat_axis=0, tiled=True)]
    all_to_all x2 -> x0, waiting for transfers between devices: 27 us -> none  [the longest x1 27 us: per_device(): lax.all_to_all(partial.reshape(chips, nc, d_half), CHIPS, split_axis=0, c...]
    all_to_all x1, waiting for transfers between devices: 17.1 us -> 0.01 us  [per_device(): q = lax.all_to_all(rows, POOL, split_axis=0, concat_axis=0, tiled=True)]
    all_to_all x2 -> x0, starting transfers between devices: 15.9 us -> none  [the longest x1 9.2 us: per_device(): lax.all_to_all(partial.reshape(chips, nc, d_half), CHIPS, split_axis=0, c...]
    ppermute x0 -> x6, starting transfers between devices: none -> 7.33 us  [to_mate(): return lax.ppermute(v, ('x', 'c'), perm)]
    ppermute x0 -> x6, waiting for transfers between devices: none -> 6.73 us  [to_mate(): return lax.ppermute(v, ('x', 'c'), perm)]
    ppermute x1, waiting for transfers between devices: 23.9 us -> 17.2 us  [per_device(): weight = lax.ppermute(out_weight, POOL, weight_moves(ny, nx, nc))]
    ppermute x4 -> x1, starting transfers between devices: 23.5 us -> 20.4 us  [swapped(): return lax.ppermute(v, 'c', [(0, 1), (1, 0)])]
  transfers between devices with their start and end apart: 8 -> 9, of which waited for: 6 -> 5; matrix products, arithmetic and copies ran while one was open for 0% -> 1% of each run, Pallas kernels for 2% -> 1%
where the time goes in v3:
time: 147 us; the launch traced here: 146 us
  blocking collectives  58.1 us (40%)
  starting transfers between devices  44.1 us (30%)
  waiting for transfers between devices  24 us (16%)
  Pallas kernels  12.6 us (9%)
  local copies, waits for them, and re-layouts  6.22 us (4%)
    all_to_all x1, blocking collectives, per_device(): lax.all_to_all(parts, CHIPS, split_axis=0, concat_axis=0, tiled=True)  30.2 us
    all_to_all x1, blocking collectives, per_device(): lax.all_to_all(partial.reshape(devices, 2, d_part // 2), POOL, split_axis...  27.9 us
    ppermute x1, starting transfers between devices, swapped(): return lax.ppermute(v, 'c', [(0, 1), (1, 0)])  20.4 us
    ppermute x1, waiting for transfers between devices, per_device(): weight = lax.ppermute(out_weight, POOL, weight_moves(ny, nx, nc))  17.2 us
    pallas_call x5, Pallas kernels, small_call(): pl.pallas_call(body, out_shape=out, in_specs=[smem] * len(scalars) + [vme...  12.6 us
    ppermute x1, starting transfers between devices, per_device(): weight = lax.ppermute(out_weight, POOL, weight_moves(ny, nx, nc))  8.27 us
    all_to_all x1, starting transfers between devices, per_device(): q = lax.all_to_all(rows, POOL, split_axis=0, concat_axis=0, tiled=True)  8.12 us
    ppermute x6, starting transfers between devices, to_mate(): return lax.ppermute(v, ('x', 'c'), perm)  7.33 us
  transfers between devices with their start and end apart: 9, of which 5 were waited for; matrix products, arithmetic and copies ran while one was open for 1% of the time, Pallas kernels for 1%

profile of v3, /device:TPU:513, one launch (start us, length us, event | category | flops | bytes accessed | tf_op | source)
XLA Modules:
  0.0 146.1 jit_solution(308595958200362863)
XLA Ops:
  0.0 20.4 %collective-permute-start.4 = (bf16[64,2,16,512]{3,2,1,0:T(8,128)(2,1)}, bf16[64,2,16,512]{3,2,1,0:T(8,128)(2,1)}, u32[]{:S(2)}, u32[]{:S(2)}) collective-permute-start(bf16[64,2,16,512]{3,2,1,0:T(8,128)(2,1)} %own_ref.1), channel_id=1, source_target_pairs={{0,1},{1,0},{2,3},{3,2},{4,5},{5,4},{6,7},{7,6},{8,9},{9,8},{10,11... | collective-permute-start | bytes 6291464 | tf_op jit(solution)/shard_map/ppermute | solution.py:211
  21.1 0.7 copy-done
  21.8 0.7 copy-done.1
  22.4 0.7 copy-done.2
  23.1 1.8 %shard_map.64 = bf16[128,2,1152]{2,1,0:T(2,128)(2,1)} custom-call(s32[1]{0:T(128)S(6)} %copy.9.length_ref, bf16[1,4096]{1,0:T(2,128)(2,1)S(1)} %copy-done, s32[1,128]{1,0:T(1,128)S(1)} %copy-done.1, s32[1,128]{1,0:T(1,128)S(1)} %copy-done.2), custom_call_target="tpu_custom_call" | custom-call | tf_op jit(solution)/shard_map/pallas_call | solution.py:198
  24.9 8.1 %all-to-all-start = ((bf16[128,2,1152]{2,1,0:T(2,128)(2,1)}), bf16[128,2,1152]{2,1,0:T(2,128)(2,1)}, u32[]{:S(2)}, u32[]{:S(2)}) async-start(bf16[128,2,1152]{2,1,0:T(2,128)(2,1)} %shard_map.64), calls=%async_computation | async-start | bytes 1179648 | tf_op jit(solution)/shard_map/all_to_all | solution.py:243
  33.0 8.3 %collective-permute-start = (bf16[32,8192]{1,0:T(8,128)(2,1)}, bf16[32,8192]{1,0:T(8,128)(2,1)S(1)}, u32[]{:S(2)}, u32[]{:S(2)}) collective-permute-start(bf16[32,8192]{1,0:T(8,128)(2,1)} %param.11), channel_id=1, source_target_pairs={{0,0},{1,64},{2,2},{3,66},{4,4},{5,68},{6,6},{7,70},{8,8},{9,72},{... | collective-permute-start | bytes 1572872 | tf_op jit(solution)/shard_map/ppermute | solution.py:242
  41.3 17.2 %collective-permute-done = bf16[32,8192]{1,0:T(8,128)(2,1)S(1)} collective-permute-done((bf16[32,8192]{1,0:T(8,128)(2,1)}, bf16[32,8192]{1,0:T(8,128)(2,1)S(1)}, u32[]{:S(2)}, u32[]{:S(2)}) %collective-permute-start) | collective-permute-done | bytes 524320 | tf_op jit(solution)/shard_map/ppermute | solution.py:242
  58.6 0.1 collective-permute-start.3
  58.8 2.7 %collective-permute-start.2 = (bf16[32,2048]{1,0:T(8,128)(2,1)S(1)}, bf16[32,2048]{1,0:T(8,128)(2,1)S(1)}, u32[]{:S(2)}, u32[]{:S(2)}) collective-permute-start(bf16[32,2048]{1,0:T(8,128)(2,1)S(1)} %get-tuple-element.16), channel_id=1, source_target_pairs={{0,2},{1,3},{2,0},{3,1},{4,6},{5,7},{6,4},{7,5},{8,10},{9,11},{10,... | collective-permute-start | bytes 393224 | tf_op jit(solution)/shard_map/ppermute | solution.py:217
  61.4 0.2 collective-permute-start.1
  61.7 0.1 pad_add_fusion.pos_ref
  61.8 1.1 copy.7
  62.9 1.4 collective-permute-done.3.refs_7_
  64.3 3.3 %collective-permute-done.2.refs_6_ = bf16[32,2048]{1,0:T(8,128)(2,1)S(1)} collective-permute-done((bf16[32,2048]{1,0:T(8,128)(2,1)S(1)}, bf16[32,2048]{1,0:T(8,128)(2,1)S(1)}, u32[]{:S(2)}, u32[]{:S(2)}) %collective-permute-start.2) | collective-permute-done | bytes 131104 | tf_op jit(solution)/shard_map/ppermute | solution.py:217
  67.6 0.0 collective-permute-done.1.refs_5_
  67.6 0.0 collective-permute-done.4.other_ref
  67.6 2.4 %shard_map.65.kv_hbm = bf16[2,3200,256]{2,1,0:T(8,128)(2,1)S(1)} custom-call(s32[2]{0:T(128)S(1)} %pad_add_fusion.pos_ref, bf16[64,2,16,512]{3,2,1,0:T(8,128)(2,1)S(1)} %copy-done.3, bf16[64,2,16,512]{3,2,1,0:T(8,128)(2,1)} %collective-permute-done.4.other_ref), custom_call_target="tpu_custom_call" | custom-call | flops 4294967296 | tf_op jit(solution)/shard_map/pallas_call | solution.py:198
  70.0 1.7 %copy-done.4 = bf16[2,3200,256]{2,1,0:T(8,128)(2,1)} copy-done((bf16[2,3200,256]{2,1,0:T(8,128)(2,1)}, bf16[2,3200,256]{2,1,0:T(8,128)(2,1)S(1)}, u32[]{:S(2)}) %copy-start.4) | copy-done | bytes 3276824
  71.7 7.8 %shard_map.66 = bf16[64,40,128]{2,1,0:T(8,128)(2,1)S(1)} custom-call(s32[2]{0:T(128)S(1)} %pad_add_fusion.pos_ref, bf16[128,2304]{1,0:T(8,128)(2,1)S(1)} %bitcast.7, bf16[2,3200,256]{2,1,0:T(8,128)(2,1)} %copy-done.4), custom_call_target="tpu_custom_call" | custom-call | flops 17179869184 | tf_op jit(solution)/shard_map/pallas_call | solution.py:198
  79.5 30.2 %all_to_all.15.got_ref = bf16[64,40,128]{2,1,0:T(8,128)(2,1)S(1)} all-to-all(bf16[64,40,128]{2,1,0:T(8,128)(2,1)S(1)} %shard_map.66), channel_id=1, replica_groups=mesh['grp'=2,'y'=8,'x'=8,'c'=2] {'y','x'}, dimensions={0} | all-to-all | bytes 1310720 | tf_op jit(solution)/shard_map/all_to_all | solution.py:278
  109.7 0.3 shard_map.67.refs_0_
  110.0 3.7 %collective-permute-start.7 = (bf16[64,128]{1,0:T(8,128)(2,1)S(1)}, bf16[64,128]{1,0:T(8,128)(2,1)S(1)}, u32[]{:S(2)}, u32[]{:S(2)}) collective-permute-start(bf16[64,128]{1,0:T(8,128)(2,1)S(1)} %shard_map.67.refs_0_), channel_id=1, source_target_pairs={{0,3},{1,2},{2,1},{3,0},{4,7},{5,6},{6,5},{7,4},{8,11},{9,10},{10,... | collective-permute-start | bytes 49160 | tf_op jit(solution)/shard_map/ppermute | solution.py:217
  113.7 0.5 collective-permute-start.5
  114.2 0.9 collective-permute-done.7.refs_3_
  115.1 1.2 collective-permute-done.6.refs_2_
  116.3 0.3 shard_map.68
  116.6 0.4 reshape.13
  117.0 27.9 %all_to_all.16 = bf16[128,2,1024]{2,1,0:T(2,128)(2,1)S(1)} all-to-all(bf16[128,2,1024]{2,1,0:T(2,128)(2,1)S(1)} %reshape.13), channel_id=1, replica_groups=mesh['grp'=2,'y'=8,'x'=8,'c'=2] {'y','x','c'}, dimensions={0} | all-to-all | bytes 1048576 | tf_op jit(solution)/shard_map/all_to_all | solution.py:282
  144.9 0.3 reshape.14
  145.2 0.2 reduce_sum.12
  145.5 0.6 copy.8
  (10 shorter events, 0.1 us)
Async XLA Ops:
  0.0 67.6 %collective-permute-start.4 = (bf16[64,2,16,512]{3,2,1,0:T(8,128)(2,1)}, bf16[64,2,16,512]{3,2,1,0:T(8,128)(2,1)}, u32[]{:S(2)}, u32[]{:S(2)}) collective-permute-start(bf16[64,2,16,512]{3,2,1,0:T(8,128)(2,1)} %own_ref.1), channel_id=1, source_target_pairs={{0,1},{1,0},{2,3},{3,2},{4,5},{5,4},{6,7},{7,6},{8,9},{9,8},{10,11... | collective-permute-start | bytes 6291464 | tf_op jit(solution)/shard_map/ppermute | solution.py:211
  21.1 0.7 copy-start
  21.8 0.7 copy-start.1
  22.4 0.7 copy-start.2
  23.1 44.5 %copy-start.3 = (bf16[64,2,16,512]{3,2,1,0:T(8,128)(2,1)S(1)}, bf16[64,2,16,512]{3,2,1,0:T(8,128)(2,1)}, u32[]{:S(2)}) copy-start(bf16[64,2,16,512]{3,2,1,0:T(8,128)(2,1)} %own_ref.1) | copy-start | bytes 6291460
  24.9 36.9 %all-to-all-start = ((bf16[128,2,1152]{2,1,0:T(2,128)(2,1)}), bf16[128,2,1152]{2,1,0:T(2,128)(2,1)}, u32[]{:S(2)}, u32[]{:S(2)}) async-start(bf16[128,2,1152]{2,1,0:T(2,128)(2,1)} %shard_map.64), calls=%async_computation | async-start | bytes 1179648 | tf_op jit(solution)/shard_map/all_to_all | solution.py:243
  33.0 25.5 %collective-permute-start = (bf16[32,8192]{1,0:T(8,128)(2,1)}, bf16[32,8192]{1,0:T(8,128)(2,1)S(1)}, u32[]{:S(2)}, u32[]{:S(2)}) collective-permute-start(bf16[32,8192]{1,0:T(8,128)(2,1)} %param.11), channel_id=1, source_target_pairs={{0,0},{1,64},{2,2},{3,66},{4,4},{5,68},{6,6},{7,70},{8,8},{9,72},{... | collective-permute-start | bytes 1572872 | tf_op jit(solution)/shard_map/ppermute | solution.py:242
  58.6 5.7 %collective-permute-start.3 = (bf16[32,2048]{1,0:T(8,128)(2,1)S(1)}, bf16[32,2048]{1,0:T(8,128)(2,1)S(1)}, u32[]{:S(2)}, u32[]{:S(2)}) collective-permute-start(bf16[32,2048]{1,0:T(8,128)(2,1)S(1)} %get-tuple-element.15), channel_id=1, source_target_pairs={{0,3},{1,2},{2,1},{3,0},{4,7},{5,6},{6,5},{7,4},{8,11},{9,10},{10,... | collective-permute-start | bytes 393224 | tf_op jit(solution)/shard_map/ppermute | solution.py:217
  58.8 8.8 %collective-permute-start.2 = (bf16[32,2048]{1,0:T(8,128)(2,1)S(1)}, bf16[32,2048]{1,0:T(8,128)(2,1)S(1)}, u32[]{:S(2)}, u32[]{:S(2)}) collective-permute-start(bf16[32,2048]{1,0:T(8,128)(2,1)S(1)} %get-tuple-element.16), channel_id=1, source_target_pairs={{0,2},{1,3},{2,0},{3,1},{4,6},{5,7},{6,4},{7,5},{8,10},{9,11},{10,... | collective-permute-start | bytes 393224 | tf_op jit(solution)/shard_map/ppermute | solution.py:217
  61.4 6.1 %collective-permute-start.1 = (bf16[32,2048]{1,0:T(8,128)(2,1)S(1)}, bf16[32,2048]{1,0:T(8,128)(2,1)S(1)}, u32[]{:S(2)}, u32[]{:S(2)}) collective-permute-start(bf16[32,2048]{1,0:T(8,128)(2,1)S(1)} %get-tuple-element.17), channel_id=1, source_target_pairs={{0,1},{1,0},{2,3},{3,2},{4,5},{5,4},{6,7},{7,6},{8,9},{9,8},{10,11... | collective-permute-start | bytes 393224 | tf_op jit(solution)/shard_map/ppermute | solution.py:217
  70.0 1.7 %copy-start.4 = (bf16[2,3200,256]{2,1,0:T(8,128)(2,1)}, bf16[2,3200,256]{2,1,0:T(8,128)(2,1)S(1)}, u32[]{:S(2)}) copy-start(bf16[2,3200,256]{2,1,0:T(8,128)(2,1)S(1)} %shard_map.65.kv_hbm) | copy-start | bytes 9830404
  110.0 5.1 %collective-permute-start.7 = (bf16[64,128]{1,0:T(8,128)(2,1)S(1)}, bf16[64,128]{1,0:T(8,128)(2,1)S(1)}, u32[]{:S(2)}, u32[]{:S(2)}) collective-permute-start(bf16[64,128]{1,0:T(8,128)(2,1)S(1)} %shard_map.67.refs_0_), channel_id=1, source_target_pairs={{0,3},{1,2},{2,1},{3,0},{4,7},{5,6},{6,5},{7,4},{8,11},{9,10},{10,... | collective-permute-start | bytes 49160 | tf_op jit(solution)/shard_map/ppermute | solution.py:217
  113.7 2.6 %collective-permute-start.6 = (bf16[64,128]{1,0:T(8,128)(2,1)S(1)}, bf16[64,128]{1,0:T(8,128)(2,1)S(1)}, u32[]{:S(2)}, u32[]{:S(2)}) collective-permute-start(bf16[64,128]{1,0:T(8,128)(2,1)S(1)} %shard_map.67.refs_0_), channel_id=1, source_target_pairs={{0,2},{1,3},{2,0},{3,1},{4,6},{5,7},{6,4},{7,5},{8,10},{9,11},{10,... | collective-permute-start | bytes 49160 | tf_op jit(solution)/shard_map/ppermute | solution.py:217
  113.7 2.6 %collective-permute-start.5 = (bf16[64,128]{1,0:T(8,128)(2,1)S(1)}, bf16[64,128]{1,0:T(8,128)(2,1)S(1)}, u32[]{:S(2)}, u32[]{:S(2)}) collective-permute-start(bf16[64,128]{1,0:T(8,128)(2,1)S(1)} %shard_map.67.refs_0_), channel_id=1, source_target_pairs={{0,1},{1,0},{2,3},{3,2},{4,5},{5,4},{6,7},{7,6},{8,9},{9,8},{10,11... | collective-permute-start | bytes 49160 | tf_op jit(solution)/shard_map/ppermute | solution.py:217

commit v4 on v3

--- a/solution.py
+++ b/solution.py
@@ -43,7 +43,13 @@
 MARK, BIAS = as_product(TWICE)
 
 
-def row_body(length_ref, q_ref, holder_ref, slot_ref, out_ref):
+def row_body(length_ref, q_hbm, holder_hbm, slot_hbm, out_ref, q_ref, holder_ref, slot_ref, sems):
+    pairs = ((q_hbm, q_ref), (holder_hbm, holder_ref), (slot_hbm, slot_ref))
+    loads = [pltpu.make_async_copy(source, target, sems.at[n]) for n, (source, target) in enumerate(pairs)]
+    for load in loads:
+        load.start()
+    for load in loads:
+        load.wait()
     devices, _, part = out_ref.shape
     lane = lax.broadcasted_iota(jnp.int32, holder_ref.shape, 1)
     holder = jnp.where(lane < length_ref[0], holder_ref[...], -1).astype(f32)
@@ -192,6 +198,16 @@
         out_ref[:, cols] = part.astype(bf16)
 
 
+def finish_body(got_ref, out_ref):
+    devices, parts, part = got_ref.shape
+    mates = out_ref.shape[1] // (parts * part)
+    for m in range(mates):
+        total = sum(got_ref[i].astype(f32) for i in range(m, devices, mates)).astype(bf16)
+        for r in range(parts):
+            at = (m * parts + r) * part
+            out_ref[:, at : at + part] = total[r : r + 1]
+
+
 def small_call(body, out, *args, scalars=(), scratch=(), mib=8, flops=0, large=0):
     smem = pl.BlockSpec(memory_space=pltpu.SMEM)
     vmem = pl.BlockSpec(memory_space=pltpu.VMEM)
@@ -238,7 +254,18 @@
     devices = chips * nc
     width = HALF + 2 * holder_table.shape[1]
     row_shape = jax.ShapeDtypeStruct((devices, 2, width // 2), bf16)
-    rows = small_call(row_body, row_shape, query, holder_table, slot_table, scalars=(lengths,))
+    scratch = [pltpu.VMEM(v.shape, v.dtype) for v in (query, holder_table, slot_table)]
+    rows = small_call(
+        row_body,
+        row_shape,
+        query,
+        holder_table,
+        slot_table,
+        scalars=(lengths,),
+        scratch=[*scratch, pltpu.SemaphoreType.DMA((3,))],
+        large=3,
+        mib=62,
+    )
     weight = lax.ppermute(out_weight, POOL, weight_moves(ny, nx, nc))
     q = lax.all_to_all(rows, POOL, split_axis=0, concat_axis=0, tiled=True)
 
@@ -258,7 +285,7 @@
         part = lax.dynamic_slice_in_dim(weight, (mate ^ k) * d_part, d_part, axis=1)
         weights.append(to_mate(part, k) if k else part)
 
-    q, *weights = lax.optimization_barrier((q.reshape(devices, width), *weights))
+    q = q.reshape(devices, width)
     parts = small_call(
         attention_body,
         jax.ShapeDtypeStruct((chips, 40, devices), bf16),
@@ -282,8 +309,7 @@
     columns = lax.all_to_all(
         partial.reshape(devices, 2, d_part // 2), POOL, split_axis=0, concat_axis=0, tiled=True
     )
-    done = jnp.sum(columns.reshape(devices // mates, mates, d_part).astype(f32), axis=0).astype(bf16)
-    return done.reshape(1, mates * d_part)
+    return small_call(finish_body, jax.ShapeDtypeStruct((1, mates * d_part), bf16), columns)
 
 
 def solution(mesh):

time: 147 us -> 143 us (0.973)
  blocking collectives: 58.1 us -> 29.6 us
  waiting for transfers between devices: 24 us -> 49 us
  local copies, waits for them, and re-layouts: 6.22 us -> 2.16 us
  Pallas kernels: 12.6 us -> 14.9 us
  starting transfers between devices: 44.1 us -> 45.9 us
    all_to_all x1 -> x0, blocking collectives: 30.2 us -> none  [per_device(): lax.all_to_all(parts, CHIPS, split_axis=0, concat_axis=0, tiled=True)]
    all_to_all x1, waiting for transfers between devices: 0.01 us -> 20.7 us  [per_device(): q = lax.all_to_all(rows, POOL, split_axis=0, concat_axis=0, tiled=True)]
    ppermute x1, waiting for transfers between devices: 17.2 us -> 24 us  [per_device(): weight = lax.ppermute(out_weight, POOL, weight_moves(ny, nx, nc))]
    all_to_all x0 -> x1, starting transfers between devices: none -> 6.69 us  [per_device(): lax.all_to_all(parts, CHIPS, split_axis=0, concat_axis=0, tiled=True)]
    unnamed x12 -> x7, local copies, waits for them, and re-layouts: 5.47 us -> 1.74 us
    ppermute x6, starting transfers between devices: 7.33 us -> 4.49 us  [to_mate(): return lax.ppermute(v, ('x', 'c'), perm)]
    ppermute x6, waiting for transfers between devices: 6.73 us -> 4.34 us  [to_mate(): return lax.ppermute(v, ('x', 'c'), perm)]
    pallas_call x5 -> x6, Pallas kernels: 12.6 us -> 14.9 us  [small_call(): pl.pallas_call(body, out_shape=out, in_specs=[smem] * len(scalars) + [vme...]
  transfers between devices with their start and end apart: 9 -> 10, of which waited for: 5 -> 5; matrix products, arithmetic and copies ran while one was open for 1% -> 0% of each run, Pallas kernels for 1% -> 2%
where the time goes in v4:
time: 143 us
  waiting for transfers between devices  49 us (34%)
  starting transfers between devices  45.9 us (32%)
  blocking collectives  29.6 us (21%)
  Pallas kernels  14.9 us (10%)
  local copies, waits for them, and re-layouts  2.16 us (2%)
    all_to_all x1, blocking collectives, per_device(): lax.all_to_all(partial.reshape(devices, 2, d_part // 2), POOL, split_axis...  29.6 us
    ppermute x1, waiting for transfers between devices, per_device(): weight = lax.ppermute(out_weight, POOL, weight_moves(ny, nx, nc))  24 us
    all_to_all x1, waiting for transfers between devices, per_device(): q = lax.all_to_all(rows, POOL, split_axis=0, concat_axis=0, tiled=True)  20.7 us
    ppermute x1, starting transfers between devices, swapped(): return lax.ppermute(v, 'c', [(0, 1), (1, 0)])  20.4 us
    pallas_call x6, Pallas kernels, small_call(): pl.pallas_call(body, out_shape=out, in_specs=[smem] * len(scalars) + [vme...  14.9 us
    all_to_all x1, starting transfers between devices, per_device(): q = lax.all_to_all(rows, POOL, split_axis=0, concat_axis=0, tiled=True)  7.6 us
    ppermute x1, starting transfers between devices, per_device(): weight = lax.ppermute(out_weight, POOL, weight_moves(ny, nx, nc))  6.73 us
    all_to_all x1, starting transfers between devices, per_device(): lax.all_to_all(parts, CHIPS, split_axis=0, concat_axis=0, tiled=True)  6.69 us
  transfers between devices with their start and end apart: 10, of which 5 were waited for; matrix products, arithmetic and copies ran while one was open for 0% of the time, Pallas kernels for 2%

profile of v4, /device:TPU:513, one launch (start us, length us, event | category | flops | bytes accessed | tf_op | source)
XLA Modules:
  0.0 142.5 jit_solution(10858939260641384679)
XLA Ops:
  0.0 20.4 %collective-permute-start = (bf16[64,2,16,512]{3,2,1,0:T(8,128)(2,1)}, bf16[64,2,16,512]{3,2,1,0:T(8,128)(2,1)}, u32[]{:S(2)}, u32[]{:S(2)}) collective-permute-start(bf16[64,2,16,512]{3,2,1,0:T(8,128)(2,1)} %own_ref.1), channel_id=1, source_target_pairs={{0,1},{1,0},{2,3},{3,2},{4,5},{5,4},{6,7},{7,6},{8,9},{9,8},{10,11... | collective-permute-start | bytes 6291464 | tf_op jit(solution)/shard_map/ppermute | solution.py:227
  21.1 2.5 %shard_map.64 = bf16[128,2,1152]{2,1,0:T(2,128)(2,1)} custom-call(s32[1]{0:T(128)S(6)} %copy.8.length_ref, bf16[1,4096]{1,0:T(2,128)(2,1)} %q_hbm.1, s32[1,128]{1,0:T(1,128)} %holder_hbm.1, s32[1,128]{1,0:T(1,128)} %slot_hbm.1), custom_call_target="tpu_custom_call" | custom-call | tf_op jit(solution)/shard_map/pallas_call | solution.py:214
  23.6 0.0 copy-start
  23.6 7.6 %all-to-all-start = ((bf16[128,2,1152]{2,1,0:T(2,128)(2,1)}), bf16[128,2,1152]{2,1,0:T(2,128)(2,1)S(1)}, u32[]{:S(2)}, u32[]{:S(2)}) async-start(bf16[128,2,1152]{2,1,0:T(2,128)(2,1)} %shard_map.64), calls=%async_computation | async-start | bytes 1179648 | tf_op jit(solution)/shard_map/all_to_all | solution.py:270
  31.3 0.1 pad_add_fusion.pos_ref
  31.3 20.7 %all-to-all-done = bf16[128,2,1152]{2,1,0:T(2,128)(2,1)S(1)} async-done(((bf16[128,2,1152]{2,1,0:T(2,128)(2,1)}), bf16[128,2,1152]{2,1,0:T(2,128)(2,1)S(1)}, u32[]{:S(2)}, u32[]{:S(2)}) %all-to-all-start) | async-done | bytes 589856 | tf_op jit(solution)/shard_map/all_to_all | solution.py:270
  52.1 0.1 copy.7
  52.1 0.0 collective-permute-done.other_ref
  52.2 2.4 %shard_map.65.kv_hbm = bf16[2,3200,256]{2,1,0:T(8,128)(2,1)S(1)} custom-call(s32[2]{0:T(128)S(1)} %pad_add_fusion.pos_ref, bf16[64,2,16,512]{3,2,1,0:T(8,128)(2,1)S(1)} %copy-done, bf16[64,2,16,512]{3,2,1,0:T(8,128)(2,1)} %collective-permute-done.other_ref), custom_call_target="tpu_custom_call" | custom-call | flops 4294967296 | tf_op jit(solution)/shard_map/pallas_call | solution.py:214
  54.5 1.7 %copy-done.1 = bf16[2,3200,256]{2,1,0:T(8,128)(2,1)} copy-done((bf16[2,3200,256]{2,1,0:T(8,128)(2,1)}, bf16[2,3200,256]{2,1,0:T(8,128)(2,1)S(1)}, u32[]{:S(2)}) %copy-start.1) | copy-done | bytes 3276824
  56.2 8.7 %shard_map.66 = bf16[64,40,128]{2,1,0:T(8,128)(2,1)} custom-call(s32[2]{0:T(128)S(1)} %pad_add_fusion.pos_ref, bf16[128,2304]{1,0:T(8,128)(2,1)S(1)} %bitcast.4, bf16[2,3200,256]{2,1,0:T(8,128)(2,1)} %copy-done.1), custom_call_target="tpu_custom_call" | custom-call | flops 17179869184 | tf_op jit(solution)/shard_map/pallas_call | solution.py:214
  64.9 6.7 %all-to-all-start.1 = ((bf16[64,40,128]{2,1,0:T(8,128)(2,1)}), bf16[64,40,128]{2,1,0:T(8,128)(2,1)S(1)}, u32[]{:S(2)}, u32[]{:S(2)}) async-start(bf16[64,40,128]{2,1,0:T(8,128)(2,1)} %shard_map.66), calls=%async_computation.1 | async-start | bytes 1310720 | tf_op jit(solution)/shard_map/all_to_all | solution.py:305
  71.6 6.7 %collective-permute-start.4 = (bf16[32,8192]{1,0:T(8,128)(2,1)S(1)}, bf16[32,8192]{1,0:T(8,128)(2,1)S(1)}, u32[]{:S(2)}, u32[]{:S(2)}) collective-permute-start(bf16[32,8192]{1,0:T(8,128)(2,1)S(1)} %copy-done.2), channel_id=1, source_target_pairs={{0,0},{1,64},{2,2},{3,66},{4,4},{5,68},{6,6},{7,70},{8,8},{9,72},{... | collective-permute-start | bytes 1572872 | tf_op jit(solution)/shard_map/ppermute | solution.py:269
  78.4 24.0 %collective-permute-done.4 = bf16[32,8192]{1,0:T(8,128)(2,1)S(1)} collective-permute-done((bf16[32,8192]{1,0:T(8,128)(2,1)S(1)}, bf16[32,8192]{1,0:T(8,128)(2,1)S(1)}, u32[]{:S(2)}, u32[]{:S(2)}) %collective-permute-start.4) | collective-permute-done | bytes 524320 | tf_op jit(solution)/shard_map/ppermute | solution.py:269
  102.4 0.1 collective-permute-start.5
  102.5 0.1 collective-permute-start.6
  102.7 2.0 %collective-permute-start.7 = (bf16[32,2048]{1,0:T(8,128)(2,1)S(1)}, bf16[32,2048]{1,0:T(8,128)(2,1)S(1)}, u32[]{:S(2)}, u32[]{:S(2)}) collective-permute-start(bf16[32,2048]{1,0:T(8,128)(2,1)S(1)} %get-tuple-element.5), channel_id=1, source_target_pairs={{0,3},{1,2},{2,1},{3,0},{4,7},{5,6},{6,5},{7,4},{8,11},{9,10},{10,... | collective-permute-start | bytes 393224 | tf_op jit(solution)/shard_map/ppermute | solution.py:233
  104.6 0.0 all-to-all-done.1.got_ref
  104.6 0.3 shard_map.67.refs_0_
  104.9 0.1 collective-permute-start.1
  105.0 0.1 collective-permute-start.2
  105.2 0.0 collective-permute-done.5.refs_5_
  105.2 2.0 %collective-permute-start.3 = (bf16[64,128]{1,0:T(8,128)(2,1)S(1)}, bf16[64,128]{1,0:T(8,128)(2,1)S(1)}, u32[]{:S(2)}, u32[]{:S(2)}) collective-permute-start(bf16[64,128]{1,0:T(8,128)(2,1)S(1)} %shard_map.67.refs_0_), channel_id=1, source_target_pairs={{0,3},{1,2},{2,1},{3,0},{4,7},{5,6},{6,5},{7,4},{8,11},{9,10},{10,... | collective-permute-start | bytes 49160 | tf_op jit(solution)/shard_map/ppermute | solution.py:233
  107.2 0.2 collective-permute-done.6.refs_6_
  107.3 3.7 %collective-permute-done.7.refs_7_ = bf16[32,2048]{1,0:T(8,128)(2,1)S(1)} collective-permute-done((bf16[32,2048]{1,0:T(8,128)(2,1)S(1)}, bf16[32,2048]{1,0:T(8,128)(2,1)S(1)}, u32[]{:S(2)}, u32[]{:S(2)}) %collective-permute-start.7) | collective-permute-done | bytes 131104 | tf_op jit(solution)/shard_map/ppermute | solution.py:233
  111.0 0.0 collective-permute-done.1.refs_1_
  111.0 0.0 collective-permute-done.2.refs_2_
  111.0 0.5 collective-permute-done.3.refs_3_
  111.5 0.3 shard_map.68
  111.8 0.4 reshape.7
  112.2 29.6 %all_to_all.15.got_ref = bf16[128,2,1024]{2,1,0:T(2,128)(2,1)S(1)} all-to-all(bf16[128,2,1024]{2,1,0:T(2,128)(2,1)S(1)} %reshape.7), channel_id=1, replica_groups=mesh['grp'=2,'y'=8,'x'=8,'c'=2] {'y','x','c'}, dimensions={0} | all-to-all | bytes 1048576 | tf_op jit(solution)/shard_map/all_to_all | solution.py:309
  141.8 0.7 shard_map.69
  (5 shorter events, 0.0 us)
Async XLA Ops:
  0.0 52.1 %collective-permute-start = (bf16[64,2,16,512]{3,2,1,0:T(8,128)(2,1)}, bf16[64,2,16,512]{3,2,1,0:T(8,128)(2,1)}, u32[]{:S(2)}, u32[]{:S(2)}) collective-permute-start(bf16[64,2,16,512]{3,2,1,0:T(8,128)(2,1)} %own_ref.1), channel_id=1, source_target_pairs={{0,1},{1,0},{2,3},{3,2},{4,5},{5,4},{6,7},{7,6},{8,9},{9,8},{10,11... | collective-permute-start | bytes 6291464 | tf_op jit(solution)/shard_map/ppermute | solution.py:227
  23.6 28.5 %copy-start = (bf16[64,2,16,512]{3,2,1,0:T(8,128)(2,1)S(1)}, bf16[64,2,16,512]{3,2,1,0:T(8,128)(2,1)}, u32[]{:S(2)}) copy-start(bf16[64,2,16,512]{3,2,1,0:T(8,128)(2,1)} %own_ref.1) | copy-start | bytes 6291460
  23.6 28.4 %all-to-all-start = ((bf16[128,2,1152]{2,1,0:T(2,128)(2,1)}), bf16[128,2,1152]{2,1,0:T(2,128)(2,1)S(1)}, u32[]{:S(2)}, u32[]{:S(2)}) async-start(bf16[128,2,1152]{2,1,0:T(2,128)(2,1)} %shard_map.64), calls=%async_computation | async-start | bytes 1179648 | tf_op jit(solution)/shard_map/all_to_all | solution.py:270
  54.5 1.7 %copy-start.1 = (bf16[2,3200,256]{2,1,0:T(8,128)(2,1)}, bf16[2,3200,256]{2,1,0:T(8,128)(2,1)S(1)}, u32[]{:S(2)}) copy-start(bf16[2,3200,256]{2,1,0:T(8,128)(2,1)S(1)} %shard_map.65.kv_hbm) | copy-start | bytes 9830404
  56.2 15.4 %copy-start.2 = (bf16[32,8192]{1,0:T(8,128)(2,1)S(1)}, bf16[32,8192]{1,0:T(8,128)(2,1)}, u32[]{:S(2)}) copy-start(bf16[32,8192]{1,0:T(8,128)(2,1)} %param.11) | copy-start | bytes 1572868
  64.9 39.8 %all-to-all-start.1 = ((bf16[64,40,128]{2,1,0:T(8,128)(2,1)}), bf16[64,40,128]{2,1,0:T(8,128)(2,1)S(1)}, u32[]{:S(2)}, u32[]{:S(2)}) async-start(bf16[64,40,128]{2,1,0:T(8,128)(2,1)} %shard_map.66), calls=%async_computation.1 | async-start | bytes 1310720 | tf_op jit(solution)/shard_map/all_to_all | solution.py:305
  71.6 30.7 %collective-permute-start.4 = (bf16[32,8192]{1,0:T(8,128)(2,1)S(1)}, bf16[32,8192]{1,0:T(8,128)(2,1)S(1)}, u32[]{:S(2)}, u32[]{:S(2)}) collective-permute-start(bf16[32,8192]{1,0:T(8,128)(2,1)S(1)} %copy-done.2), channel_id=1, source_target_pairs={{0,0},{1,64},{2,2},{3,66},{4,4},{5,68},{6,6},{7,70},{8,8},{9,72},{... | collective-permute-start | bytes 1572872 | tf_op jit(solution)/shard_map/ppermute | solution.py:269
  102.4 2.8 %collective-permute-start.5 = (bf16[32,2048]{1,0:T(8,128)(2,1)S(1)}, bf16[32,2048]{1,0:T(8,128)(2,1)S(1)}, u32[]{:S(2)}, u32[]{:S(2)}) collective-permute-start(bf16[32,2048]{1,0:T(8,128)(2,1)S(1)} %get-tuple-element.7), channel_id=1, source_target_pairs={{0,1},{1,0},{2,3},{3,2},{4,5},{5,4},{6,7},{7,6},{8,9},{9,8},{10,11... | collective-permute-start | bytes 393224 | tf_op jit(solution)/shard_map/ppermute | solution.py:233
  102.5 4.8 %collective-permute-start.6 = (bf16[32,2048]{1,0:T(8,128)(2,1)S(1)}, bf16[32,2048]{1,0:T(8,128)(2,1)S(1)}, u32[]{:S(2)}, u32[]{:S(2)}) collective-permute-start(bf16[32,2048]{1,0:T(8,128)(2,1)S(1)} %get-tuple-element.6), channel_id=1, source_target_pairs={{0,2},{1,3},{2,0},{3,1},{4,6},{5,7},{6,4},{7,5},{8,10},{9,11},{10,... | collective-permute-start | bytes 393224 | tf_op jit(solution)/shard_map/ppermute | solution.py:233
  102.7 8.4 %collective-permute-start.7 = (bf16[32,2048]{1,0:T(8,128)(2,1)S(1)}, bf16[32,2048]{1,0:T(8,128)(2,1)S(1)}, u32[]{:S(2)}, u32[]{:S(2)}) collective-permute-start(bf16[32,2048]{1,0:T(8,128)(2,1)S(1)} %get-tuple-element.5), channel_id=1, source_target_pairs={{0,3},{1,2},{2,1},{3,0},{4,7},{5,6},{6,5},{7,4},{8,11},{9,10},{10,... | collective-permute-start | bytes 393224 | tf_op jit(solution)/shard_map/ppermute | solution.py:233
  104.9 6.1 %collective-permute-start.1 = (bf16[64,128]{1,0:T(8,128)(2,1)S(1)}, bf16[64,128]{1,0:T(8,128)(2,1)S(1)}, u32[]{:S(2)}, u32[]{:S(2)}) collective-permute-start(bf16[64,128]{1,0:T(8,128)(2,1)S(1)} %shard_map.67.refs_0_), channel_id=1, source_target_pairs={{0,1},{1,0},{2,3},{3,2},{4,5},{5,4},{6,7},{7,6},{8,9},{9,8},{10,11... | collective-permute-start | bytes 49160 | tf_op jit(solution)/shard_map/ppermute | solution.py:233
  105.0 6.0 %collective-permute-start.2 = (bf16[64,128]{1,0:T(8,128)(2,1)S(1)}, bf16[64,128]{1,0:T(8,128)(2,1)S(1)}, u32[]{:S(2)}, u32[]{:S(2)}) collective-permute-start(bf16[64,128]{1,0:T(8,128)(2,1)S(1)} %shard_map.67.refs_0_), channel_id=1, source_target_pairs={{0,2},{1,3},{2,0},{3,1},{4,6},{5,7},{6,4},{7,5},{8,10},{9,11},{10,... | collective-permute-start | bytes 49160 | tf_op jit(solution)/shard_map/ppermute | solution.py:233
  105.2 6.3 %collective-permute-start.3 = (bf16[64,128]{1,0:T(8,128)(2,1)S(1)}, bf16[64,128]{1,0:T(8,128)(2,1)S(1)}, u32[]{:S(2)}, u32[]{:S(2)}) collective-permute-start(bf16[64,128]{1,0:T(8,128)(2,1)S(1)} %shard_map.67.refs_0_), channel_id=1, source_target_pairs={{0,3},{1,2},{2,1},{3,0},{4,7},{5,6},{6,5},{7,4},{8,11},{9,10},{10,... | collective-permute-start | bytes 49160 | tf_op jit(solution)/shard_map/ppermute | solution.py:233

commit v5 on v4

--- a/solution.py
+++ b/solution.py
@@ -233,16 +233,17 @@
     return lax.ppermute(v, ("x", "c"), perm)
 
 
-def weight_moves(ny, nx, nc):
+def to_owner(v, k):
+    ny, nx, nc = (lax.axis_size(a) for a in POOL)
     pairs = []
-    for y in range(ny):
-        for x in range(nx):
-            for c in range(nc):
-                upper = y // (ny // 2)
-                at = (y * nx + x) * nc + c
-                other = (((y + ny // 2) % ny) * nx + x) * nc + 1 - c
-                pairs.append((at, at if upper == c else other))
-    return pairs
+    for half in range(nc):
+        for y in range(ny // nc):
+            for x in range(nx):
+                for c in range(nc):
+                    source = ((half * (ny // nc) + y) * nx + x) * nc + c
+                    target = ((c * (ny // nc) + y) * nx + (x ^ (k // nc))) * nc + (half ^ (k % nc))
+                    pairs.append((source, target))
+    return lax.ppermute(v, POOL, pairs)
 
 
 def per_device(query, kv_pool, holder_table, slot_table, lengths, out_weight):
@@ -266,7 +267,6 @@
         large=3,
         mib=62,
     )
-    weight = lax.ppermute(out_weight, POOL, weight_moves(ny, nx, nc))
     q = lax.all_to_all(rows, POOL, split_axis=0, concat_axis=0, tiled=True)
 
     kv_other = swapped(kv_pool)
@@ -279,10 +279,10 @@
 
     mates = 2 * nc
     mate = (x % 2) * nc + c
-    d_part = weight.shape[1] // mates
+    d_part = out_weight.shape[1] // mates
     weights = []
     for k in range(mates):
-        part = lax.dynamic_slice_in_dim(weight, (mate ^ k) * d_part, d_part, axis=1)
+        part = lax.dynamic_slice_in_dim(out_weight, (mate ^ k) * d_part, d_part, axis=1)
         weights.append(to_mate(part, k) if k else part)
 
     q = q.reshape(devices, width)
@@ -304,7 +304,7 @@
     )
     parts = lax.all_to_all(parts, CHIPS, split_axis=0, concat_axis=0, tiled=True)
     mine = small_call(merge_body, jax.ShapeDtypeStruct((64, devices), bf16), parts)
-    lefts = [to_mate(mine, k) if k else mine for k in range(mates)]
+    lefts = [to_owner(mine, k) for k in range(mates)]
     partial = small_call(project_body, jax.ShapeDtypeStruct((devices, d_part), bf16), *lefts, *weights)
     columns = lax.all_to_all(
         partial.reshape(devices, 2, d_part // 2), POOL, split_axis=0, concat_axis=0, tiled=True

time: 143 us -> 137 us (0.958)
  waiting for transfers between devices: 49 us -> 42.6 us
    ppermute x1 -> x4, waiting for transfers between devices: 24 us -> 5.66 us  [to_owner(): return lax.ppermute(v, POOL, pairs)]
    all_to_all x1, waiting for transfers between devices: 0.01 us -> 16.2 us  [per_device(): lax.all_to_all(parts, CHIPS, split_axis=0, concat_axis=0, tiled=True)]
    ppermute x6 -> x3, waiting for transfers between devices: 4.34 us -> 0.01 us  [to_mate(): return lax.ppermute(v, ('x', 'c'), perm)]
    ppermute x1 -> x4, starting transfers between devices: 6.73 us -> 10.3 us  [to_owner(): return lax.ppermute(v, POOL, pairs)]
    ppermute x6 -> x3, starting transfers between devices: 4.49 us -> 2.26 us  [to_mate(): return lax.ppermute(v, ('x', 'c'), perm)]
  transfers between devices with their start and end apart: 10 -> 10, of which waited for: 5 -> 3; matrix products, arithmetic and copies ran while one was open for 0% -> 0% of each run, Pallas kernels for 2% -> 2%
where the time goes in v5:
time: 137 us
  starting transfers between devices  47.2 us (34%)
  waiting for transfers between devices  42.6 us (31%)
  blocking collectives  28.9 us (21%)
  Pallas kernels  14.9 us (11%)
  local copies, waits for them, and re-layouts  2.17 us (2%)
    all_to_all x1, blocking collectives, per_device(): lax.all_to_all(partial.reshape(devices, 2, d_part // 2), POOL, split_axis...  28.9 us
    all_to_all x1, waiting for transfers between devices, per_device(): q = lax.all_to_all(rows, POOL, split_axis=0, concat_axis=0, tiled=True)  20.7 us
    ppermute x1, starting transfers between devices, swapped(): return lax.ppermute(v, 'c', [(0, 1), (1, 0)])  20.4 us
    all_to_all x1, waiting for transfers between devices, per_device(): lax.all_to_all(parts, CHIPS, split_axis=0, concat_axis=0, tiled=True)  16.2 us
    pallas_call x6, Pallas kernels, small_call(): pl.pallas_call(body, out_shape=out, in_specs=[smem] * len(scalars) + [vme...  14.9 us
    ppermute x4, starting transfers between devices, to_owner(): return lax.ppermute(v, POOL, pairs)  10.3 us
    all_to_all x1, starting transfers between devices, per_device(): q = lax.all_to_all(rows, POOL, split_axis=0, concat_axis=0, tiled=True)  7.6 us
    all_to_all x1, starting transfers between devices, per_device(): lax.all_to_all(parts, CHIPS, split_axis=0, concat_axis=0, tiled=True)  6.69 us
  transfers between devices with their start and end apart: 10, of which 3 were waited for; matrix products, arithmetic and copies ran while one was open for 0% of the time, Pallas kernels for 2%

profile of v5, /device:TPU:513, one launch (start us, length us, event | category | flops | bytes accessed | tf_op | source)
XLA Modules:
  0.0 136.7 jit_solution(16526734980814041933)
XLA Ops:
  0.0 20.4 %collective-permute-start = (bf16[64,2,16,512]{3,2,1,0:T(8,128)(2,1)}, bf16[64,2,16,512]{3,2,1,0:T(8,128)(2,1)}, u32[]{:S(2)}, u32[]{:S(2)}) collective-permute-start(bf16[64,2,16,512]{3,2,1,0:T(8,128)(2,1)} %own_ref.1), channel_id=1, source_target_pairs={{0,1},{1,0},{2,3},{3,2},{4,5},{5,4},{6,7},{7,6},{8,9},{9,8},{10,11... | collective-permute-start | bytes 6291464 | tf_op jit(solution)/shard_map/ppermute | solution.py:227
  21.1 2.5 %shard_map.64 = bf16[128,2,1152]{2,1,0:T(2,128)(2,1)} custom-call(s32[1]{0:T(128)S(6)} %copy.8.length_ref, bf16[1,4096]{1,0:T(2,128)(2,1)} %q_hbm.1, s32[1,128]{1,0:T(1,128)} %holder_hbm.1, s32[1,128]{1,0:T(1,128)} %slot_hbm.1), custom_call_target="tpu_custom_call" | custom-call | tf_op jit(solution)/shard_map/pallas_call | solution.py:214
  23.6 0.0 copy-start
  23.6 7.6 %all-to-all-start = ((bf16[128,2,1152]{2,1,0:T(2,128)(2,1)}), bf16[128,2,1152]{2,1,0:T(2,128)(2,1)S(1)}, u32[]{:S(2)}, u32[]{:S(2)}) async-start(bf16[128,2,1152]{2,1,0:T(2,128)(2,1)} %shard_map.64), calls=%async_computation | async-start | bytes 1179648 | tf_op jit(solution)/shard_map/all_to_all | solution.py:270
  31.3 0.1 pad_add_fusion.pos_ref
  31.3 20.7 %all-to-all-done = bf16[128,2,1152]{2,1,0:T(2,128)(2,1)S(1)} async-done(((bf16[128,2,1152]{2,1,0:T(2,128)(2,1)}), bf16[128,2,1152]{2,1,0:T(2,128)(2,1)S(1)}, u32[]{:S(2)}, u32[]{:S(2)}) %all-to-all-start) | async-done | bytes 589856 | tf_op jit(solution)/shard_map/all_to_all | solution.py:270
  52.1 0.1 copy.7
  52.1 0.0 collective-permute-done.other_ref
  52.2 2.4 %shard_map.65.kv_hbm = bf16[2,3200,256]{2,1,0:T(8,128)(2,1)S(1)} custom-call(s32[2]{0:T(128)S(1)} %pad_add_fusion.pos_ref, bf16[64,2,16,512]{3,2,1,0:T(8,128)(2,1)S(1)} %copy-done, bf16[64,2,16,512]{3,2,1,0:T(8,128)(2,1)} %collective-permute-done.other_ref), custom_call_target="tpu_custom_call" | custom-call | flops 4294967296 | tf_op jit(solution)/shard_map/pallas_call | solution.py:214
  54.5 1.7 %copy-done.1 = bf16[2,3200,256]{2,1,0:T(8,128)(2,1)} copy-done((bf16[2,3200,256]{2,1,0:T(8,128)(2,1)}, bf16[2,3200,256]{2,1,0:T(8,128)(2,1)S(1)}, u32[]{:S(2)}) %copy-start.1) | copy-done | bytes 3276824
  56.2 8.7 %shard_map.66 = bf16[64,40,128]{2,1,0:T(8,128)(2,1)} custom-call(s32[2]{0:T(128)S(1)} %pad_add_fusion.pos_ref, bf16[128,2304]{1,0:T(8,128)(2,1)S(1)} %bitcast.4, bf16[2,3200,256]{2,1,0:T(8,128)(2,1)} %copy-done.1), custom_call_target="tpu_custom_call" | custom-call | flops 17179869184 | tf_op jit(solution)/shard_map/pallas_call | solution.py:214
  64.9 6.7 %all-to-all-start.1 = ((bf16[64,40,128]{2,1,0:T(8,128)(2,1)}), bf16[64,40,128]{2,1,0:T(8,128)(2,1)S(1)}, u32[]{:S(2)}, u32[]{:S(2)}) async-start(bf16[64,40,128]{2,1,0:T(8,128)(2,1)} %shard_map.66), calls=%async_computation.1 | async-start | bytes 1310720 | tf_op jit(solution)/shard_map/all_to_all | solution.py:305
  71.6 0.1 constant_dynamic-slice_fusion
  71.7 0.4 collective-permute-start.5
  72.1 0.4 collective-permute-start.6
  72.5 1.4 %collective-permute-start.7 = (bf16[32,2048]{1,0:T(8,128)(2,1)S(1)}, bf16[32,2048]{1,0:T(8,128)(2,1)S(1)}, u32[]{:S(2)}, u32[]{:S(2)}) collective-permute-start(bf16[32,2048]{1,0:T(8,128)(2,1)S(1)} %get-tuple-element.5), channel_id=1, source_target_pairs={{0,3},{1,2},{2,1},{3,0},{4,7},{5,6},{6,5},{7,4},{8,11},{9,10},{10,... | collective-permute-start | bytes 393224 | tf_op jit(solution)/shard_map/ppermute | solution.py:233
  74.0 16.2 %all-to-all-done.1.got_ref = bf16[64,40,128]{2,1,0:T(8,128)(2,1)S(1)} async-done(((bf16[64,40,128]{2,1,0:T(8,128)(2,1)}), bf16[64,40,128]{2,1,0:T(8,128)(2,1)S(1)}, u32[]{:S(2)}, u32[]{:S(2)}) %all-to-all-start.1) | async-done | bytes 655392 | tf_op jit(solution)/shard_map/all_to_all | solution.py:305
  90.1 0.3 shard_map.67
  90.4 7.7 %collective-permute-start.1 = (bf16[64,128]{1,0:T(8,128)(2,1)S(1)}, bf16[64,128]{1,0:T(8,128)(2,1)S(1)}, u32[]{:S(2)}, u32[]{:S(2)}) collective-permute-start(bf16[64,128]{1,0:T(8,128)(2,1)S(1)} %shard_map.67), channel_id=1, source_target_pairs={{0,0},{1,64},{2,2},{3,66},{4,4},{5,68},{6,6},{7,70},{8,8},{9,72},{... | collective-permute-start | bytes 49160 | tf_op jit(solution)/shard_map/ppermute | solution.py:246
  98.1 0.1 collective-permute-start.2
  98.3 0.0 collective-permute-done.5.refs_5_
  98.3 2.4 %collective-permute-start.3 = (bf16[64,128]{1,0:T(8,128)(2,1)S(1)}, bf16[64,128]{1,0:T(8,128)(2,1)S(1)}, u32[]{:S(2)}, u32[]{:S(2)}) collective-permute-start(bf16[64,128]{1,0:T(8,128)(2,1)S(1)} %shard_map.67), channel_id=1, source_target_pairs={{0,2},{1,66},{2,0},{3,64},{4,6},{5,70},{6,4},{7,68},{8,10},{9,74},... | collective-permute-start | bytes 49160 | tf_op jit(solution)/shard_map/ppermute | solution.py:246
  100.7 0.0 collective-permute-done.6.refs_6_
  100.7 0.0 collective-permute-start.4
  100.7 0.0 collective-permute-done.7.refs_7_
  100.7 0.0 collective-permute-done.1.refs_0_
  100.7 0.0 collective-permute-done.2.refs_1_
  100.7 5.6 %collective-permute-done.3.refs_2_ = bf16[64,128]{1,0:T(8,128)(2,1)S(1)} collective-permute-done((bf16[64,128]{1,0:T(8,128)(2,1)S(1)}, bf16[64,128]{1,0:T(8,128)(2,1)S(1)}, u32[]{:S(2)}, u32[]{:S(2)}) %collective-permute-start.3) | collective-permute-done | bytes 16416 | tf_op jit(solution)/shard_map/ppermute | solution.py:246
  106.4 0.3 shard_map.68
  106.7 0.4 reshape.7
  107.1 28.9 %all_to_all.15.got_ref = bf16[128,2,1024]{2,1,0:T(2,128)(2,1)S(1)} all-to-all(bf16[128,2,1024]{2,1,0:T(2,128)(2,1)S(1)} %reshape.7), channel_id=1, replica_groups=mesh['grp'=2,'y'=8,'x'=8,'c'=2] {'y','x','c'}, dimensions={0} | all-to-all | bytes 1048576 | tf_op jit(solution)/shard_map/all_to_all | solution.py:309
  136.0 0.7 shard_map.69
  (5 shorter events, 0.0 us)
Async XLA Ops:
  0.0 52.1 %collective-permute-start = (bf16[64,2,16,512]{3,2,1,0:T(8,128)(2,1)}, bf16[64,2,16,512]{3,2,1,0:T(8,128)(2,1)}, u32[]{:S(2)}, u32[]{:S(2)}) collective-permute-start(bf16[64,2,16,512]{3,2,1,0:T(8,128)(2,1)} %own_ref.1), channel_id=1, source_target_pairs={{0,1},{1,0},{2,3},{3,2},{4,5},{5,4},{6,7},{7,6},{8,9},{9,8},{10,11... | collective-permute-start | bytes 6291464 | tf_op jit(solution)/shard_map/ppermute | solution.py:227
  23.6 28.5 %copy-start = (bf16[64,2,16,512]{3,2,1,0:T(8,128)(2,1)S(1)}, bf16[64,2,16,512]{3,2,1,0:T(8,128)(2,1)}, u32[]{:S(2)}) copy-start(bf16[64,2,16,512]{3,2,1,0:T(8,128)(2,1)} %own_ref.1) | copy-start | bytes 6291460
  23.6 28.4 %all-to-all-start = ((bf16[128,2,1152]{2,1,0:T(2,128)(2,1)}), bf16[128,2,1152]{2,1,0:T(2,128)(2,1)S(1)}, u32[]{:S(2)}, u32[]{:S(2)}) async-start(bf16[128,2,1152]{2,1,0:T(2,128)(2,1)} %shard_map.64), calls=%async_computation | async-start | bytes 1179648 | tf_op jit(solution)/shard_map/all_to_all | solution.py:270
  54.5 1.7 %copy-start.1 = (bf16[2,3200,256]{2,1,0:T(8,128)(2,1)}, bf16[2,3200,256]{2,1,0:T(8,128)(2,1)S(1)}, u32[]{:S(2)}) copy-start(bf16[2,3200,256]{2,1,0:T(8,128)(2,1)S(1)} %shard_map.65.kv_hbm) | copy-start | bytes 9830404
  56.2 15.4 %copy-start.2 = (bf16[32,8192]{1,0:T(8,128)(2,1)S(1)}, bf16[32,8192]{1,0:T(8,128)(2,1)}, u32[]{:S(2)}) copy-start(bf16[32,8192]{1,0:T(8,128)(2,1)} %param.11) | copy-start | bytes 1572868
  64.9 25.3 %all-to-all-start.1 = ((bf16[64,40,128]{2,1,0:T(8,128)(2,1)}), bf16[64,40,128]{2,1,0:T(8,128)(2,1)S(1)}, u32[]{:S(2)}, u32[]{:S(2)}) async-start(bf16[64,40,128]{2,1,0:T(8,128)(2,1)} %shard_map.66), calls=%async_computation.1 | async-start | bytes 1310720 | tf_op jit(solution)/shard_map/all_to_all | solution.py:305
  71.7 26.6 %collective-permute-start.5 = (bf16[32,2048]{1,0:T(8,128)(2,1)S(1)}, bf16[32,2048]{1,0:T(8,128)(2,1)S(1)}, u32[]{:S(2)}, u32[]{:S(2)}) collective-permute-start(bf16[32,2048]{1,0:T(8,128)(2,1)S(1)} %get-tuple-element.6), channel_id=1, source_target_pairs={{0,1},{1,0},{2,3},{3,2},{4,5},{5,4},{6,7},{7,6},{8,9},{9,8},{10,11... | collective-permute-start | bytes 393224 | tf_op jit(solution)/shard_map/ppermute | solution.py:233
  72.1 28.6 %collective-permute-start.6 = (bf16[32,2048]{1,0:T(8,128)(2,1)S(1)}, bf16[32,2048]{1,0:T(8,128)(2,1)S(1)}, u32[]{:S(2)}, u32[]{:S(2)}) collective-permute-start(bf16[32,2048]{1,0:T(8,128)(2,1)S(1)} %get-tuple-element.8), channel_id=1, source_target_pairs={{0,2},{1,3},{2,0},{3,1},{4,6},{5,7},{6,4},{7,5},{8,10},{9,11},{10,... | collective-permute-start | bytes 393224 | tf_op jit(solution)/shard_map/ppermute | solution.py:233
  72.5 28.2 %collective-permute-start.7 = (bf16[32,2048]{1,0:T(8,128)(2,1)S(1)}, bf16[32,2048]{1,0:T(8,128)(2,1)S(1)}, u32[]{:S(2)}, u32[]{:S(2)}) collective-permute-start(bf16[32,2048]{1,0:T(8,128)(2,1)S(1)} %get-tuple-element.5), channel_id=1, source_target_pairs={{0,3},{1,2},{2,1},{3,0},{4,7},{5,6},{6,5},{7,4},{8,11},{9,10},{10,... | collective-permute-start | bytes 393224 | tf_op jit(solution)/shard_map/ppermute | solution.py:233
  90.4 10.3 %collective-permute-start.1 = (bf16[64,128]{1,0:T(8,128)(2,1)S(1)}, bf16[64,128]{1,0:T(8,128)(2,1)S(1)}, u32[]{:S(2)}, u32[]{:S(2)}) collective-permute-start(bf16[64,128]{1,0:T(8,128)(2,1)S(1)} %shard_map.67), channel_id=1, source_target_pairs={{0,0},{1,64},{2,2},{3,66},{4,4},{5,68},{6,6},{7,70},{8,8},{9,72},{... | collective-permute-start | bytes 49160 | tf_op jit(solution)/shard_map/ppermute | solution.py:246
  98.1 2.6 %collective-permute-start.2 = (bf16[64,128]{1,0:T(8,128)(2,1)S(1)}, bf16[64,128]{1,0:T(8,128)(2,1)S(1)}, u32[]{:S(2)}, u32[]{:S(2)}) collective-permute-start(bf16[64,128]{1,0:T(8,128)(2,1)S(1)} %shard_map.67), channel_id=1, source_target_pairs={{0,1},{1,65},{2,3},{3,67},{4,5},{5,69},{6,7},{7,71},{8,9},{9,73},{... | collective-permute-start | bytes 49160 | tf_op jit(solution)/shard_map/ppermute | solution.py:246
  98.3 8.1 %collective-permute-start.3 = (bf16[64,128]{1,0:T(8,128)(2,1)S(1)}, bf16[64,128]{1,0:T(8,128)(2,1)S(1)}, u32[]{:S(2)}, u32[]{:S(2)}) collective-permute-start(bf16[64,128]{1,0:T(8,128)(2,1)S(1)} %shard_map.67), channel_id=1, source_target_pairs={{0,2},{1,66},{2,0},{3,64},{4,6},{5,70},{6,4},{7,68},{8,10},{9,74},... | collective-permute-start | bytes 49160 | tf_op jit(solution)/shard_map/ppermute | solution.py:246
  100.7 5.7 %collective-permute-start.4 = (bf16[64,128]{1,0:T(8,128)(2,1)S(1)}, bf16[64,128]{1,0:T(8,128)(2,1)S(1)}, u32[]{:S(2)}, u32[]{:S(2)}) collective-permute-start(bf16[64,128]{1,0:T(8,128)(2,1)S(1)} %shard_map.67), channel_id=1, source_target_pairs={{0,3},{1,67},{2,1},{3,65},{4,7},{5,71},{6,5},{7,69},{8,11},{9,75},... | collective-permute-start | bytes 49160 | tf_op jit(solution)/shard_map/ppermute | solution.py:246

commit v6 on v5

--- a/solution.py
+++ b/solution.py
@@ -278,12 +278,12 @@
     )
 
     mates = 2 * nc
-    mate = (x % 2) * nc + c
+    first = (x % 2) * nc + y // (ny // nc)
     d_part = out_weight.shape[1] // mates
     weights = []
     for k in range(mates):
-        part = lax.dynamic_slice_in_dim(out_weight, (mate ^ k) * d_part, d_part, axis=1)
-        weights.append(to_mate(part, k) if k else part)
+        part = lax.dynamic_slice_in_dim(out_weight, (first ^ k) * d_part, d_part, axis=1)
+        weights.append(to_owner(part, k))
 
     q = q.reshape(devices, width)
     parts = small_call(
@@ -304,7 +304,7 @@
     )
     parts = lax.all_to_all(parts, CHIPS, split_axis=0, concat_axis=0, tiled=True)
     mine = small_call(merge_body, jax.ShapeDtypeStruct((64, devices), bf16), parts)
-    lefts = [to_owner(mine, k) for k in range(mates)]
+    lefts = [to_mate(mine, k) if k else mine for k in range(mates)]
     partial = small_call(project_body, jax.ShapeDtypeStruct((devices, d_part), bf16), *lefts, *weights)
     columns = lax.all_to_all(
         partial.reshape(devices, 2, d_part // 2), POOL, split_axis=0, concat_axis=0, tiled=True

time: 137 us -> 138 us (level)
  waiting for transfers between devices: 42.6 us -> 39.4 us
  blocking collectives: 28.9 us -> 31.4 us
    all_to_all x1, waiting for transfers between devices: 16.2 us -> 10.3 us  [per_device(): lax.all_to_all(parts, CHIPS, split_axis=0, concat_axis=0, tiled=True)]
    all_to_all x1, blocking collectives: 28.9 us -> 31.4 us  [per_device(): lax.all_to_all(partial.reshape(devices, 2, d_part // 2), POOL, split_axis...]
    ppermute x3, starting transfers between devices: 2.26 us -> 4.72 us  [to_mate(): return lax.ppermute(v, ('x', 'c'), perm)]
    ppermute x3, waiting for transfers between devices: 0.01 us -> 1.41 us  [to_mate(): return lax.ppermute(v, ('x', 'c'), perm)]
  transfers between devices with their start and end apart: 10 -> 10, of which waited for: 3 -> 5; matrix products, arithmetic and copies ran while one was open for 0% -> 0% of each run, Pallas kernels for 2% -> 2%
where the time goes in v6:
time: 138 us; the launch traced here: 137 us
  starting transfers between devices  48.4 us (35%)
  waiting for transfers between devices  39.4 us (29%)
  blocking collectives  31.4 us (23%)
  Pallas kernels  14.9 us (11%)
  local copies, waits for them, and re-layouts  2.17 us (2%)
    all_to_all x1, blocking collectives, per_device(): lax.all_to_all(partial.reshape(devices, 2, d_part // 2), POOL, split_axis...  31.4 us
    all_to_all x1, waiting for transfers between devices, per_device(): q = lax.all_to_all(rows, POOL, split_axis=0, concat_axis=0, tiled=True)  20.7 us
    ppermute x1, starting transfers between devices, swapped(): return lax.ppermute(v, 'c', [(0, 1), (1, 0)])  20.4 us
    pallas_call x6, Pallas kernels, small_call(): pl.pallas_call(body, out_shape=out, in_specs=[smem] * len(scalars) + [vme...  14.9 us
    all_to_all x1, waiting for transfers between devices, per_device(): lax.all_to_all(parts, CHIPS, split_axis=0, concat_axis=0, tiled=True)  10.3 us
    ppermute x4, starting transfers between devices, to_owner(): return lax.ppermute(v, POOL, pairs)  9 us
    all_to_all x1, starting transfers between devices, per_device(): q = lax.all_to_all(rows, POOL, split_axis=0, concat_axis=0, tiled=True)  7.6 us
    ppermute x4, waiting for transfers between devices, to_owner(): return lax.ppermute(v, POOL, pairs)  6.95 us
  transfers between devices with their start and end apart: 10, of which 5 were waited for; matrix products, arithmetic and copies ran while one was open for 0% of the time, Pallas kernels for 2%

profile of v6, /device:TPU:513, one launch (start us, length us, event | category | flops | bytes accessed | tf_op | source)
XLA Modules:
  0.0 137.2 jit_solution(9622812835112162008)
XLA Ops:
  0.0 20.4 %collective-permute-start = (bf16[64,2,16,512]{3,2,1,0:T(8,128)(2,1)}, bf16[64,2,16,512]{3,2,1,0:T(8,128)(2,1)}, u32[]{:S(2)}, u32[]{:S(2)}) collective-permute-start(bf16[64,2,16,512]{3,2,1,0:T(8,128)(2,1)} %own_ref.1), channel_id=1, source_target_pairs={{0,1},{1,0},{2,3},{3,2},{4,5},{5,4},{6,7},{7,6},{8,9},{9,8},{10,11... | collective-permute-start | bytes 6291464 | tf_op jit(solution)/shard_map/ppermute | solution.py:227
  21.1 2.5 %shard_map.64 = bf16[128,2,1152]{2,1,0:T(2,128)(2,1)} custom-call(s32[1]{0:T(128)S(6)} %copy.8.length_ref, bf16[1,4096]{1,0:T(2,128)(2,1)} %q_hbm.1, s32[1,128]{1,0:T(1,128)} %holder_hbm.1, s32[1,128]{1,0:T(1,128)} %slot_hbm.1), custom_call_target="tpu_custom_call" | custom-call | tf_op jit(solution)/shard_map/pallas_call | solution.py:214
  23.6 0.0 copy-start
  23.6 7.6 %all-to-all-start = ((bf16[128,2,1152]{2,1,0:T(2,128)(2,1)}), bf16[128,2,1152]{2,1,0:T(2,128)(2,1)S(1)}, u32[]{:S(2)}, u32[]{:S(2)}) async-start(bf16[128,2,1152]{2,1,0:T(2,128)(2,1)} %shard_map.64), calls=%async_computation | async-start | bytes 1179648 | tf_op jit(solution)/shard_map/all_to_all | solution.py:270
  31.3 0.1 pad_add_fusion.pos_ref
  31.3 20.7 %all-to-all-done = bf16[128,2,1152]{2,1,0:T(2,128)(2,1)S(1)} async-done(((bf16[128,2,1152]{2,1,0:T(2,128)(2,1)}), bf16[128,2,1152]{2,1,0:T(2,128)(2,1)S(1)}, u32[]{:S(2)}, u32[]{:S(2)}) %all-to-all-start) | async-done | bytes 589856 | tf_op jit(solution)/shard_map/all_to_all | solution.py:270
  52.1 0.1 copy.7
  52.1 0.0 collective-permute-done.other_ref
  52.2 2.4 %shard_map.65.kv_hbm = bf16[2,3200,256]{2,1,0:T(8,128)(2,1)S(1)} custom-call(s32[2]{0:T(128)S(1)} %pad_add_fusion.pos_ref, bf16[64,2,16,512]{3,2,1,0:T(8,128)(2,1)S(1)} %copy-done, bf16[64,2,16,512]{3,2,1,0:T(8,128)(2,1)} %collective-permute-done.other_ref), custom_call_target="tpu_custom_call" | custom-call | flops 4294967296 | tf_op jit(solution)/shard_map/pallas_call | solution.py:214
  54.5 1.7 %copy-done.1 = bf16[2,3200,256]{2,1,0:T(8,128)(2,1)} copy-done((bf16[2,3200,256]{2,1,0:T(8,128)(2,1)}, bf16[2,3200,256]{2,1,0:T(8,128)(2,1)S(1)}, u32[]{:S(2)}) %copy-start.1) | copy-done | bytes 3276824
  56.2 8.7 %shard_map.66 = bf16[64,40,128]{2,1,0:T(8,128)(2,1)} custom-call(s32[2]{0:T(128)S(1)} %pad_add_fusion.pos_ref, bf16[128,2304]{1,0:T(8,128)(2,1)S(1)} %bitcast.4, bf16[2,3200,256]{2,1,0:T(8,128)(2,1)} %copy-done.1), custom_call_target="tpu_custom_call" | custom-call | flops 17179869184 | tf_op jit(solution)/shard_map/pallas_call | solution.py:214
  64.9 6.7 %all-to-all-start.1 = ((bf16[64,40,128]{2,1,0:T(8,128)(2,1)}), bf16[64,40,128]{2,1,0:T(8,128)(2,1)S(1)}, u32[]{:S(2)}, u32[]{:S(2)}) async-start(bf16[64,40,128]{2,1,0:T(8,128)(2,1)} %shard_map.66), calls=%async_computation.1 | async-start | bytes 1310720 | tf_op jit(solution)/shard_map/all_to_all | solution.py:305
  71.6 0.1 constant_dynamic-slice_fusion
  71.7 6.7 %collective-permute-start.4 = (bf16[32,2048]{1,0:T(8,128)(2,1)S(1)}, bf16[32,2048]{1,0:T(8,128)(2,1)S(1)}, u32[]{:S(2)}, u32[]{:S(2)}) collective-permute-start(bf16[32,2048]{1,0:T(8,128)(2,1)S(1)} %get-tuple-element.7), channel_id=1, source_target_pairs={{0,0},{1,64},{2,2},{3,66},{4,4},{5,68},{6,6},{7,70},{8,8},{9,72},{... | collective-permute-start | bytes 393224 | tf_op jit(solution)/shard_map/ppermute | solution.py:246
  78.4 0.1 collective-permute-start.5
  78.6 1.1 collective-permute-start.6
  79.6 1.1 collective-permute-start.7
  80.7 10.3 %all-to-all-done.1.got_ref = bf16[64,40,128]{2,1,0:T(8,128)(2,1)S(1)} async-done(((bf16[64,40,128]{2,1,0:T(8,128)(2,1)}), bf16[64,40,128]{2,1,0:T(8,128)(2,1)S(1)}, u32[]{:S(2)}, u32[]{:S(2)}) %all-to-all-start.1) | async-done | bytes 655392 | tf_op jit(solution)/shard_map/all_to_all | solution.py:305
  91.0 0.3 shard_map.67.refs_0_
  91.2 2.7 %collective-permute-start.1 = (bf16[64,128]{1,0:T(8,128)(2,1)S(1)}, bf16[64,128]{1,0:T(8,128)(2,1)S(1)}, u32[]{:S(2)}, u32[]{:S(2)}) collective-permute-start(bf16[64,128]{1,0:T(8,128)(2,1)S(1)} %shard_map.67.refs_0_), channel_id=1, source_target_pairs={{0,1},{1,0},{2,3},{3,2},{4,5},{5,4},{6,7},{7,6},{8,9},{9,8},{10,11... | collective-permute-start | bytes 49160 | tf_op jit(solution)/shard_map/ppermute | solution.py:233
  94.0 6.9 %collective-permute-done.4.refs_4_ = bf16[32,2048]{1,0:T(8,128)(2,1)S(1)} collective-permute-done((bf16[32,2048]{1,0:T(8,128)(2,1)S(1)}, bf16[32,2048]{1,0:T(8,128)(2,1)S(1)}, u32[]{:S(2)}, u32[]{:S(2)}) %collective-permute-start.4) | collective-permute-done | bytes 131104 | tf_op jit(solution)/shard_map/ppermute | solution.py:246
  100.9 0.0 collective-permute-start.2
  100.9 2.0 %collective-permute-start.3 = (bf16[64,128]{1,0:T(8,128)(2,1)S(1)}, bf16[64,128]{1,0:T(8,128)(2,1)S(1)}, u32[]{:S(2)}, u32[]{:S(2)}) collective-permute-start(bf16[64,128]{1,0:T(8,128)(2,1)S(1)} %shard_map.67.refs_0_), channel_id=1, source_target_pairs={{0,3},{1,2},{2,1},{3,0},{4,7},{5,6},{6,5},{7,4},{8,11},{9,10},{10,... | collective-permute-start | bytes 49160 | tf_op jit(solution)/shard_map/ppermute | solution.py:233
  102.9 0.0 collective-permute-done.6.refs_6_
  102.9 0.0 collective-permute-done.7.refs_7_
  102.9 0.0 collective-permute-done.1.refs_1_
  102.9 0.6 collective-permute-done.2.refs_2_
  103.5 0.8 collective-permute-done.3.refs_3_
  104.3 0.3 shard_map.68
  104.7 0.4 reshape.7
  105.1 31.4 %all_to_all.15.got_ref = bf16[128,2,1024]{2,1,0:T(2,128)(2,1)S(1)} all-to-all(bf16[128,2,1024]{2,1,0:T(2,128)(2,1)S(1)} %reshape.7), channel_id=1, replica_groups=mesh['grp'=2,'y'=8,'x'=8,'c'=2] {'y','x','c'}, dimensions={0} | all-to-all | bytes 1048576 | tf_op jit(solution)/shard_map/all_to_all | solution.py:309
  136.4 0.7 shard_map.69
  (5 shorter events, 0.0 us)
Async XLA Ops:
  0.0 52.1 %collective-permute-start = (bf16[64,2,16,512]{3,2,1,0:T(8,128)(2,1)}, bf16[64,2,16,512]{3,2,1,0:T(8,128)(2,1)}, u32[]{:S(2)}, u32[]{:S(2)}) collective-permute-start(bf16[64,2,16,512]{3,2,1,0:T(8,128)(2,1)} %own_ref.1), channel_id=1, source_target_pairs={{0,1},{1,0},{2,3},{3,2},{4,5},{5,4},{6,7},{7,6},{8,9},{9,8},{10,11... | collective-permute-start | bytes 6291464 | tf_op jit(solution)/shard_map/ppermute | solution.py:227
  23.6 28.5 %copy-start = (bf16[64,2,16,512]{3,2,1,0:T(8,128)(2,1)S(1)}, bf16[64,2,16,512]{3,2,1,0:T(8,128)(2,1)}, u32[]{:S(2)}) copy-start(bf16[64,2,16,512]{3,2,1,0:T(8,128)(2,1)} %own_ref.1) | copy-start | bytes 6291460
  23.6 28.4 %all-to-all-start = ((bf16[128,2,1152]{2,1,0:T(2,128)(2,1)}), bf16[128,2,1152]{2,1,0:T(2,128)(2,1)S(1)}, u32[]{:S(2)}, u32[]{:S(2)}) async-start(bf16[128,2,1152]{2,1,0:T(2,128)(2,1)} %shard_map.64), calls=%async_computation | async-start | bytes 1179648 | tf_op jit(solution)/shard_map/all_to_all | solution.py:270
  54.5 1.7 %copy-start.1 = (bf16[2,3200,256]{2,1,0:T(8,128)(2,1)}, bf16[2,3200,256]{2,1,0:T(8,128)(2,1)S(1)}, u32[]{:S(2)}) copy-start(bf16[2,3200,256]{2,1,0:T(8,128)(2,1)S(1)} %shard_map.65.kv_hbm) | copy-start | bytes 9830404
  56.2 15.4 %copy-start.2 = (bf16[32,8192]{1,0:T(8,128)(2,1)S(1)}, bf16[32,8192]{1,0:T(8,128)(2,1)}, u32[]{:S(2)}) copy-start(bf16[32,8192]{1,0:T(8,128)(2,1)} %param.11) | copy-start | bytes 1572868
  64.9 26.1 %all-to-all-start.1 = ((bf16[64,40,128]{2,1,0:T(8,128)(2,1)}), bf16[64,40,128]{2,1,0:T(8,128)(2,1)S(1)}, u32[]{:S(2)}, u32[]{:S(2)}) async-start(bf16[64,40,128]{2,1,0:T(8,128)(2,1)} %shard_map.66), calls=%async_computation.1 | async-start | bytes 1310720 | tf_op jit(solution)/shard_map/all_to_all | solution.py:305
  71.7 29.2 %collective-permute-start.4 = (bf16[32,2048]{1,0:T(8,128)(2,1)S(1)}, bf16[32,2048]{1,0:T(8,128)(2,1)S(1)}, u32[]{:S(2)}, u32[]{:S(2)}) collective-permute-start(bf16[32,2048]{1,0:T(8,128)(2,1)S(1)} %get-tuple-element.7), channel_id=1, source_target_pairs={{0,0},{1,64},{2,2},{3,66},{4,4},{5,68},{6,6},{7,70},{8,8},{9,72},{... | collective-permute-start | bytes 393224 | tf_op jit(solution)/shard_map/ppermute | solution.py:246
  78.4 22.5 %collective-permute-start.5 = (bf16[32,2048]{1,0:T(8,128)(2,1)S(1)}, bf16[32,2048]{1,0:T(8,128)(2,1)S(1)}, u32[]{:S(2)}, u32[]{:S(2)}) collective-permute-start(bf16[32,2048]{1,0:T(8,128)(2,1)S(1)} %get-tuple-element.6), channel_id=1, source_target_pairs={{0,1},{1,65},{2,3},{3,67},{4,5},{5,69},{6,7},{7,71},{8,9},{9,73},{... | collective-permute-start | bytes 393224 | tf_op jit(solution)/shard_map/ppermute | solution.py:246
  78.6 24.3 %collective-permute-start.6 = (bf16[32,2048]{1,0:T(8,128)(2,1)S(1)}, bf16[32,2048]{1,0:T(8,128)(2,1)S(1)}, u32[]{:S(2)}, u32[]{:S(2)}) collective-permute-start(bf16[32,2048]{1,0:T(8,128)(2,1)S(1)} %get-tuple-element.8), channel_id=1, source_target_pairs={{0,2},{1,66},{2,0},{3,64},{4,6},{5,70},{6,4},{7,68},{8,10},{9,74},... | collective-permute-start | bytes 393224 | tf_op jit(solution)/shard_map/ppermute | solution.py:246
  79.6 23.3 %collective-permute-start.7 = (bf16[32,2048]{1,0:T(8,128)(2,1)S(1)}, bf16[32,2048]{1,0:T(8,128)(2,1)S(1)}, u32[]{:S(2)}, u32[]{:S(2)}) collective-permute-start(bf16[32,2048]{1,0:T(8,128)(2,1)S(1)} %get-tuple-element.5), channel_id=1, source_target_pairs={{0,3},{1,67},{2,1},{3,65},{4,7},{5,71},{6,5},{7,69},{8,11},{9,75},... | collective-permute-start | bytes 393224 | tf_op jit(solution)/shard_map/ppermute | solution.py:246
  91.2 11.7 %collective-permute-start.1 = (bf16[64,128]{1,0:T(8,128)(2,1)S(1)}, bf16[64,128]{1,0:T(8,128)(2,1)S(1)}, u32[]{:S(2)}, u32[]{:S(2)}) collective-permute-start(bf16[64,128]{1,0:T(8,128)(2,1)S(1)} %shard_map.67.refs_0_), channel_id=1, source_target_pairs={{0,1},{1,0},{2,3},{3,2},{4,5},{5,4},{6,7},{7,6},{8,9},{9,8},{10,11... | collective-permute-start | bytes 49160 | tf_op jit(solution)/shard_map/ppermute | solution.py:233
  100.9 2.6 %collective-permute-start.2 = (bf16[64,128]{1,0:T(8,128)(2,1)S(1)}, bf16[64,128]{1,0:T(8,128)(2,1)S(1)}, u32[]{:S(2)}, u32[]{:S(2)}) collective-permute-start(bf16[64,128]{1,0:T(8,128)(2,1)S(1)} %shard_map.67.refs_0_), channel_id=1, source_target_pairs={{0,2},{1,3},{2,0},{3,1},{4,6},{5,7},{6,4},{7,5},{8,10},{9,11},{10,... | collective-permute-start | bytes 49160 | tf_op jit(solution)/shard_map/ppermute | solution.py:233
  100.9 3.4 %collective-permute-start.3 = (bf16[64,128]{1,0:T(8,128)(2,1)S(1)}, bf16[64,128]{1,0:T(8,128)(2,1)S(1)}, u32[]{:S(2)}, u32[]{:S(2)}) collective-permute-start(bf16[64,128]{1,0:T(8,128)(2,1)S(1)} %shard_map.67.refs_0_), channel_id=1, source_target_pairs={{0,3},{1,2},{2,1},{3,0},{4,7},{5,6},{6,5},{7,4},{8,11},{9,10},{10,... | collective-permute-start | bytes 49160 | tf_op jit(solution)/shard_map/ppermute | solution.py:233

commit v7 on v6

--- a/solution.py
+++ b/solution.py
@@ -24,6 +24,7 @@
 HALF = H * HD // CORES
 TILE = 2 * HD
 VROWS = HD + 16
+SLICE = 32
 INTERPRET = False
 
 f32 = jnp.float32
@@ -127,10 +128,6 @@
         if 0 <= i - 1 < pairs:
             top = jnp.max(peaks[i - 1], axis=0, keepdims=True).astype(bf16)
             peaks[i - 1] = top.astype(f32)
-            for h in range(2):
-                g, head = divmod(2 * (i - 1) + h, GROUPS)
-                for j in range(4):
-                    out_ref[dest_of(g, head, j), 32:33, :] = top[:, h * rows : (h + 1) * rows]
         for k in range(chunks):
             at = slice(k * chunk, (k + 1) * chunk)
             if i < pairs:
@@ -156,14 +153,13 @@
             for h in range(2):
                 g, head = divmod(2 * (i - 2) + h, GROUPS)
                 cols = slice(h * rows, (h + 1) * rows)
-                total = out[HD : HD + 1, cols]
-                high = total.astype(bf16)
-                low = (total - high.astype(f32)).astype(bf16)
+                stat = jnp.concatenate([peaks[i - 2][:, cols], out[HD : HD + 1, cols]], axis=0).astype(bf16)
                 for j in range(4):
                     dest = dest_of(g, head, j)
-                    out_ref[dest, 0:32, :] = out[j * 32 : (j + 1) * 32, cols].astype(bf16)
-                    out_ref[dest, 33:34, :] = high
-                    out_ref[dest, 34:35, :] = low
+                    for t in range(SLICE // 2):
+                        pair = out[j * SLICE + 2 * t : j * SLICE + 2 * t + 2, cols]
+                        out_ref[dest, :, t * rows : (t + 1) * rows] = pair.astype(bf16)
+                    out_ref[dest, :, SLICE // 2 * rows :] = stat
 
 
 def dest_of(g, h, j):
@@ -171,19 +167,22 @@
 
 
 def merge_body(got_ref, out_ref):
-    chips, _, rows = got_ref.shape
-    peaks = [got_ref[i, 32:33, :].astype(f32) for i in range(chips)]
-    top = functools.reduce(jnp.maximum, peaks)
+    chips, _, _ = got_ref.shape
+    rows = out_ref.shape[1]
+    pairs = SLICE // 2
+    stats = [got_ref[i, :, pairs * rows :].astype(f32) for i in range(chips)]
+    top = functools.reduce(jnp.maximum, [s[:1] for s in stats])
     total = jnp.zeros((1, rows), f32)
-    number = jnp.zeros((32, rows), f32)
+    number = jnp.zeros((2, pairs * rows), f32)
     for i in range(chips):
-        factor = jnp.exp2((peaks[i] - top) * RATE)
-        total += factor * (got_ref[i, 33:34, :].astype(f32) + got_ref[i, 34:35, :].astype(f32))
-        number += factor * got_ref[i, 0:32, :].astype(f32)
-    attention = number / total
+        factor = jnp.exp2((stats[i][:1] - top) * RATE)
+        total += factor * stats[i][1:]
+        number += jnp.concatenate([factor] * pairs, axis=1) * got_ref[i, :, : pairs * rows].astype(f32)
+    attention = number / jnp.concatenate([total] * pairs, axis=1)
+    attention = jnp.concatenate([attention[:, t * rows : (t + 1) * rows] for t in range(pairs)], axis=0)
     high = attention.astype(bf16)
-    out_ref[0:32, :] = high
-    out_ref[32:64, :] = (attention - high.astype(f32)).astype(bf16)
+    out_ref[:SLICE, :] = high
+    out_ref[SLICE:, :] = (attention - high.astype(f32)).astype(bf16)
 
 
 def project_body(*refs):
@@ -288,7 +287,7 @@
     q = q.reshape(devices, width)
     parts = small_call(
         attention_body,
-        jax.ShapeDtypeStruct((chips, 40, devices), bf16),
+        jax.ShapeDtypeStruct((chips, 2, (SLICE // 2 + 1) * devices), bf16),
         q,
         blocks,
         scalars=(pos,),
@@ -303,7 +302,7 @@
         flops=1 << 34,
     )
     parts = lax.all_to_all(parts, CHIPS, split_axis=0, concat_axis=0, tiled=True)
-    mine = small_call(merge_body, jax.ShapeDtypeStruct((64, devices), bf16), parts)
+    mine = small_call(merge_body, jax.ShapeDtypeStruct((2 * SLICE, devices), bf16), parts)
     lefts = [to_mate(mine, k) if k else mine for k in range(mates)]
     partial = small_call(project_body, jax.ShapeDtypeStruct((devices, d_part), bf16), *lefts, *weights)
     columns = lax.all_to_all(

time: 138 us -> 136 us (0.986)
  waiting for transfers between devices: 39.4 us -> 37.6 us
    all_to_all x1, waiting for transfers between devices: 10.3 us -> 8.71 us  [per_device(): lax.all_to_all(parts, CHIPS, split_axis=0, concat_axis=0, tiled=True)]
where the time goes in v7:
time: 136 us
  starting transfers between devices  48 us (35%)
  waiting for transfers between devices  37.6 us (28%)
  blocking collectives  31.7 us (23%)
  Pallas kernels  15.2 us (11%)
  local copies, waits for them, and re-layouts  2.17 us (2%)
    all_to_all x1, blocking collectives, per_device(): lax.all_to_all(partial.reshape(devices, 2, d_part // 2), POOL, split_axis...  31.7 us
    all_to_all x1, waiting for transfers between devices, per_device(): q = lax.all_to_all(rows, POOL, split_axis=0, concat_axis=0, tiled=True)  20.7 us
    ppermute x1, starting transfers between devices, swapped(): return lax.ppermute(v, 'c', [(0, 1), (1, 0)])  20.4 us
    pallas_call x6, Pallas kernels, small_call(): pl.pallas_call(body, out_shape=out, in_specs=[smem] * len(scalars) + [vme...  15.2 us
    ppermute x4, starting transfers between devices, to_owner(): return lax.ppermute(v, POOL, pairs)  9 us
    all_to_all x1, waiting for transfers between devices, per_device(): lax.all_to_all(parts, CHIPS, split_axis=0, concat_axis=0, tiled=True)  8.71 us
    all_to_all x1, starting transfers between devices, per_device(): q = lax.all_to_all(rows, POOL, split_axis=0, concat_axis=0, tiled=True)  7.6 us
    ppermute x4, waiting for transfers between devices, to_owner(): return lax.ppermute(v, POOL, pairs)  6.77 us
  transfers between devices with their start and end apart: 10, of which 5 were waited for; matrix products, arithmetic and copies ran while one was open for 0% of the time, Pallas kernels for 2%

profile of v7, /device:TPU:513, one launch (start us, length us, event | category | flops | bytes accessed | tf_op | source)
XLA Modules:
  0.0 135.6 jit_solution(1535164458678865319)
XLA Ops:
  0.0 20.4 %collective-permute-start = (bf16[64,2,16,512]{3,2,1,0:T(8,128)(2,1)}, bf16[64,2,16,512]{3,2,1,0:T(8,128)(2,1)}, u32[]{:S(2)}, u32[]{:S(2)}) collective-permute-start(bf16[64,2,16,512]{3,2,1,0:T(8,128)(2,1)} %own_ref.1), channel_id=1, source_target_pairs={{0,1},{1,0},{2,3},{3,2},{4,5},{5,4},{6,7},{7,6},{8,9},{9,8},{10,11... | collective-permute-start | bytes 6291464 | tf_op jit(solution)/shard_map/ppermute | solution.py:226
  21.1 2.5 %shard_map.64 = bf16[128,2,1152]{2,1,0:T(2,128)(2,1)} custom-call(s32[1]{0:T(128)S(6)} %copy.8.length_ref, bf16[1,4096]{1,0:T(2,128)(2,1)} %q_hbm.1, s32[1,128]{1,0:T(1,128)} %holder_hbm.1, s32[1,128]{1,0:T(1,128)} %slot_hbm.1), custom_call_target="tpu_custom_call" | custom-call | tf_op jit(solution)/shard_map/pallas_call | solution.py:213
  23.6 0.0 copy-start
  23.6 7.6 %all-to-all-start = ((bf16[128,2,1152]{2,1,0:T(2,128)(2,1)}), bf16[128,2,1152]{2,1,0:T(2,128)(2,1)S(1)}, u32[]{:S(2)}, u32[]{:S(2)}) async-start(bf16[128,2,1152]{2,1,0:T(2,128)(2,1)} %shard_map.64), calls=%async_computation | async-start | bytes 1179648 | tf_op jit(solution)/shard_map/all_to_all | solution.py:269
  31.3 0.1 pad_add_fusion.pos_ref
  31.3 20.7 %all-to-all-done = bf16[128,2,1152]{2,1,0:T(2,128)(2,1)S(1)} async-done(((bf16[128,2,1152]{2,1,0:T(2,128)(2,1)}), bf16[128,2,1152]{2,1,0:T(2,128)(2,1)S(1)}, u32[]{:S(2)}, u32[]{:S(2)}) %all-to-all-start) | async-done | bytes 589856 | tf_op jit(solution)/shard_map/all_to_all | solution.py:269
  52.1 0.1 copy.7
  52.1 0.0 collective-permute-done.other_ref
  52.2 2.4 %shard_map.65.kv_hbm = bf16[2,3200,256]{2,1,0:T(8,128)(2,1)S(1)} custom-call(s32[2]{0:T(128)S(1)} %pad_add_fusion.pos_ref, bf16[64,2,16,512]{3,2,1,0:T(8,128)(2,1)S(1)} %copy-done, bf16[64,2,16,512]{3,2,1,0:T(8,128)(2,1)} %collective-permute-done.other_ref), custom_call_target="tpu_custom_call" | custom-call | flops 4294967296 | tf_op jit(solution)/shard_map/pallas_call | solution.py:213
  54.5 1.7 %copy-done.1 = bf16[2,3200,256]{2,1,0:T(8,128)(2,1)} copy-done((bf16[2,3200,256]{2,1,0:T(8,128)(2,1)}, bf16[2,3200,256]{2,1,0:T(8,128)(2,1)S(1)}, u32[]{:S(2)}) %copy-start.1) | copy-done | bytes 3276824
  56.2 8.7 %shard_map.66 = bf16[64,2,2176]{2,1,0:T(2,128)(2,1)} custom-call(s32[2]{0:T(128)S(1)} %pad_add_fusion.pos_ref, bf16[128,2304]{1,0:T(8,128)(2,1)S(1)} %bitcast.4, bf16[2,3200,256]{2,1,0:T(8,128)(2,1)} %copy-done.1), custom_call_target="tpu_custom_call" | custom-call | flops 17179869184 | tf_op jit(solution)/shard_map/pallas_call | solution.py:213
  64.9 6.7 %all-to-all-start.1 = ((bf16[64,2,2176]{2,1,0:T(2,128)(2,1)}), bf16[64,2,2176]{2,1,0:T(2,128)(2,1)S(1)}, u32[]{:S(2)}, u32[]{:S(2)}) async-start(bf16[64,2,2176]{2,1,0:T(2,128)(2,1)} %shard_map.66), calls=%async_computation.1 | async-start | bytes 1114112 | tf_op jit(solution)/shard_map/all_to_all | solution.py:304
  71.7 0.1 constant_dynamic-slice_fusion
  71.7 6.7 %collective-permute-start.4 = (bf16[32,2048]{1,0:T(8,128)(2,1)S(1)}, bf16[32,2048]{1,0:T(8,128)(2,1)S(1)}, u32[]{:S(2)}, u32[]{:S(2)}) collective-permute-start(bf16[32,2048]{1,0:T(8,128)(2,1)S(1)} %get-tuple-element.7), channel_id=1, source_target_pairs={{0,0},{1,64},{2,2},{3,66},{4,4},{5,68},{6,6},{7,70},{8,8},{9,72},{... | collective-permute-start | bytes 393224 | tf_op jit(solution)/shard_map/ppermute | solution.py:245
  78.5 0.1 collective-permute-start.5
  78.6 1.1 collective-permute-start.6
  79.7 1.1 collective-permute-start.7
  80.7 8.7 %all-to-all-done.1.got_ref = bf16[64,2,2176]{2,1,0:T(2,128)(2,1)S(1)} async-done(((bf16[64,2,2176]{2,1,0:T(2,128)(2,1)}), bf16[64,2,2176]{2,1,0:T(2,128)(2,1)S(1)}, u32[]{:S(2)}, u32[]{:S(2)}) %all-to-all-start.1) | async-done | bytes 557088 | tf_op jit(solution)/shard_map/all_to_all | solution.py:304
  89.5 0.6 shard_map.67.refs_0_
  90.0 2.1 %collective-permute-start.1 = (bf16[64,128]{1,0:T(8,128)(2,1)S(1)}, bf16[64,128]{1,0:T(8,128)(2,1)S(1)}, u32[]{:S(2)}, u32[]{:S(2)}) collective-permute-start(bf16[64,128]{1,0:T(8,128)(2,1)S(1)} %shard_map.67.refs_0_), channel_id=1, source_target_pairs={{0,1},{1,0},{2,3},{3,2},{4,5},{5,4},{6,7},{7,6},{8,9},{9,8},{10,11... | collective-permute-start | bytes 49160 | tf_op jit(solution)/shard_map/ppermute | solution.py:232
  92.1 6.8 %collective-permute-done.4.refs_4_ = bf16[32,2048]{1,0:T(8,128)(2,1)S(1)} collective-permute-done((bf16[32,2048]{1,0:T(8,128)(2,1)S(1)}, bf16[32,2048]{1,0:T(8,128)(2,1)S(1)}, u32[]{:S(2)}, u32[]{:S(2)}) %collective-permute-start.4) | collective-permute-done | bytes 131104 | tf_op jit(solution)/shard_map/ppermute | solution.py:245
  98.9 0.0 collective-permute-start.2
  98.9 0.0 collective-permute-done.5.refs_5_
  98.9 2.2 %collective-permute-start.3 = (bf16[64,128]{1,0:T(8,128)(2,1)S(1)}, bf16[64,128]{1,0:T(8,128)(2,1)S(1)}, u32[]{:S(2)}, u32[]{:S(2)}) collective-permute-start(bf16[64,128]{1,0:T(8,128)(2,1)S(1)} %shard_map.67.refs_0_), channel_id=1, source_target_pairs={{0,3},{1,2},{2,1},{3,0},{4,7},{5,6},{6,5},{7,4},{8,11},{9,10},{10,... | collective-permute-start | bytes 49160 | tf_op jit(solution)/shard_map/ppermute | solution.py:232
  101.1 0.0 collective-permute-done.6.refs_6_
  101.1 0.0 collective-permute-done.7.refs_7_
  101.1 0.4 collective-permute-done.2.refs_2_
  101.5 1.0 collective-permute-done.3.refs_3_
  102.5 0.3 shard_map.68
  102.8 0.4 reshape.7
  103.2 31.7 %all_to_all.15.got_ref = bf16[128,2,1024]{2,1,0:T(2,128)(2,1)S(1)} all-to-all(bf16[128,2,1024]{2,1,0:T(2,128)(2,1)S(1)} %reshape.7), channel_id=1, replica_groups=mesh['grp'=2,'y'=8,'x'=8,'c'=2] {'y','x','c'}, dimensions={0} | all-to-all | bytes 1048576 | tf_op jit(solution)/shard_map/all_to_all | solution.py:308
  134.9 0.7 shard_map.69
  (5 shorter events, 0.0 us)
Async XLA Ops:
  0.0 52.1 %collective-permute-start = (bf16[64,2,16,512]{3,2,1,0:T(8,128)(2,1)}, bf16[64,2,16,512]{3,2,1,0:T(8,128)(2,1)}, u32[]{:S(2)}, u32[]{:S(2)}) collective-permute-start(bf16[64,2,16,512]{3,2,1,0:T(8,128)(2,1)} %own_ref.1), channel_id=1, source_target_pairs={{0,1},{1,0},{2,3},{3,2},{4,5},{5,4},{6,7},{7,6},{8,9},{9,8},{10,11... | collective-permute-start | bytes 6291464 | tf_op jit(solution)/shard_map/ppermute | solution.py:226
  23.6 28.5 %copy-start = (bf16[64,2,16,512]{3,2,1,0:T(8,128)(2,1)S(1)}, bf16[64,2,16,512]{3,2,1,0:T(8,128)(2,1)}, u32[]{:S(2)}) copy-start(bf16[64,2,16,512]{3,2,1,0:T(8,128)(2,1)} %own_ref.1) | copy-start | bytes 6291460
  23.6 28.4 %all-to-all-start = ((bf16[128,2,1152]{2,1,0:T(2,128)(2,1)}), bf16[128,2,1152]{2,1,0:T(2,128)(2,1)S(1)}, u32[]{:S(2)}, u32[]{:S(2)}) async-start(bf16[128,2,1152]{2,1,0:T(2,128)(2,1)} %shard_map.64), calls=%async_computation | async-start | bytes 1179648 | tf_op jit(solution)/shard_map/all_to_all | solution.py:269
  54.5 1.7 %copy-start.1 = (bf16[2,3200,256]{2,1,0:T(8,128)(2,1)}, bf16[2,3200,256]{2,1,0:T(8,128)(2,1)S(1)}, u32[]{:S(2)}) copy-start(bf16[2,3200,256]{2,1,0:T(8,128)(2,1)S(1)} %shard_map.65.kv_hbm) | copy-start | bytes 9830404
  56.2 15.4 %copy-start.2 = (bf16[32,8192]{1,0:T(8,128)(2,1)S(1)}, bf16[32,8192]{1,0:T(8,128)(2,1)}, u32[]{:S(2)}) copy-start(bf16[32,8192]{1,0:T(8,128)(2,1)} %param.11) | copy-start | bytes 1572868
  64.9 24.5 %all-to-all-start.1 = ((bf16[64,2,2176]{2,1,0:T(2,128)(2,1)}), bf16[64,2,2176]{2,1,0:T(2,128)(2,1)S(1)}, u32[]{:S(2)}, u32[]{:S(2)}) async-start(bf16[64,2,2176]{2,1,0:T(2,128)(2,1)} %shard_map.66), calls=%async_computation.1 | async-start | bytes 1114112 | tf_op jit(solution)/shard_map/all_to_all | solution.py:304
  71.7 27.2 %collective-permute-start.4 = (bf16[32,2048]{1,0:T(8,128)(2,1)S(1)}, bf16[32,2048]{1,0:T(8,128)(2,1)S(1)}, u32[]{:S(2)}, u32[]{:S(2)}) collective-permute-start(bf16[32,2048]{1,0:T(8,128)(2,1)S(1)} %get-tuple-element.7), channel_id=1, source_target_pairs={{0,0},{1,64},{2,2},{3,66},{4,4},{5,68},{6,6},{7,70},{8,8},{9,72},{... | collective-permute-start | bytes 393224 | tf_op jit(solution)/shard_map/ppermute | solution.py:245
  78.5 20.4 %collective-permute-start.5 = (bf16[32,2048]{1,0:T(8,128)(2,1)S(1)}, bf16[32,2048]{1,0:T(8,128)(2,1)S(1)}, u32[]{:S(2)}, u32[]{:S(2)}) collective-permute-start(bf16[32,2048]{1,0:T(8,128)(2,1)S(1)} %get-tuple-element.6), channel_id=1, source_target_pairs={{0,1},{1,65},{2,3},{3,67},{4,5},{5,69},{6,7},{7,71},{8,9},{9,73},{... | collective-permute-start | bytes 393224 | tf_op jit(solution)/shard_map/ppermute | solution.py:245
  78.6 22.5 %collective-permute-start.6 = (bf16[32,2048]{1,0:T(8,128)(2,1)S(1)}, bf16[32,2048]{1,0:T(8,128)(2,1)S(1)}, u32[]{:S(2)}, u32[]{:S(2)}) collective-permute-start(bf16[32,2048]{1,0:T(8,128)(2,1)S(1)} %get-tuple-element.8), channel_id=1, source_target_pairs={{0,2},{1,66},{2,0},{3,64},{4,6},{5,70},{6,4},{7,68},{8,10},{9,74},... | collective-permute-start | bytes 393224 | tf_op jit(solution)/shard_map/ppermute | solution.py:245
  79.7 21.4 %collective-permute-start.7 = (bf16[32,2048]{1,0:T(8,128)(2,1)S(1)}, bf16[32,2048]{1,0:T(8,128)(2,1)S(1)}, u32[]{:S(2)}, u32[]{:S(2)}) collective-permute-start(bf16[32,2048]{1,0:T(8,128)(2,1)S(1)} %get-tuple-element.5), channel_id=1, source_target_pairs={{0,3},{1,67},{2,1},{3,65},{4,7},{5,71},{6,5},{7,69},{8,11},{9,75},... | collective-permute-start | bytes 393224 | tf_op jit(solution)/shard_map/ppermute | solution.py:245
  90.0 11.0 %collective-permute-start.1 = (bf16[64,128]{1,0:T(8,128)(2,1)S(1)}, bf16[64,128]{1,0:T(8,128)(2,1)S(1)}, u32[]{:S(2)}, u32[]{:S(2)}) collective-permute-start(bf16[64,128]{1,0:T(8,128)(2,1)S(1)} %shard_map.67.refs_0_), channel_id=1, source_target_pairs={{0,1},{1,0},{2,3},{3,2},{4,5},{5,4},{6,7},{7,6},{8,9},{9,8},{10,11... | collective-permute-start | bytes 49160 | tf_op jit(solution)/shard_map/ppermute | solution.py:232
  98.9 2.6 %collective-permute-start.2 = (bf16[64,128]{1,0:T(8,128)(2,1)S(1)}, bf16[64,128]{1,0:T(8,128)(2,1)S(1)}, u32[]{:S(2)}, u32[]{:S(2)}) collective-permute-start(bf16[64,128]{1,0:T(8,128)(2,1)S(1)} %shard_map.67.refs_0_), channel_id=1, source_target_pairs={{0,2},{1,3},{2,0},{3,1},{4,6},{5,7},{6,4},{7,5},{8,10},{9,11},{10,... | collective-permute-start | bytes 49160 | tf_op jit(solution)/shard_map/ppermute | solution.py:232
  98.9 3.6 %collective-permute-start.3 = (bf16[64,128]{1,0:T(8,128)(2,1)S(1)}, bf16[64,128]{1,0:T(8,128)(2,1)S(1)}, u32[]{:S(2)}, u32[]{:S(2)}) collective-permute-start(bf16[64,128]{1,0:T(8,128)(2,1)S(1)} %shard_map.67.refs_0_), channel_id=1, source_target_pairs={{0,3},{1,2},{2,1},{3,0},{4,7},{5,6},{6,5},{7,4},{8,11},{9,10},{10,... | collective-permute-start | bytes 49160 | tf_op jit(solution)/shard_map/ppermute | solution.py:232

commit v8 on v7

--- a/solution.py
+++ b/solution.py
@@ -25,6 +25,7 @@
 TILE = 2 * HD
 VROWS = HD + 16
 SLICE = 32
+CHUNK = 512
 INTERPRET = False
 
 f32 = jnp.float32
@@ -90,7 +91,8 @@
     tokens = s_scr.shape[1]
     loads = {}
     for g in range(steps):
-        for n, at in enumerate((slice(0, tokens), slice(tokens, kv_ref.shape[1]))):
+        ends = [*range(0, tokens + 1, CHUNK), kv_ref.shape[1]]
+        for n, at in enumerate(slice(*pair) for pair in zip(ends, ends[1:])):
             loads[n, g] = pltpu.make_async_copy(kv_hbm.at[g, at], kv_ref.at[g, at], sems.at[n, g])
             loads[n, g].start()
     slots = HD // 2
@@ -113,7 +115,7 @@
     bias = jnp.where(lane < slots, bias_of(me), bias_of(partner)).astype(bf16)
 
     pairs = steps * GROUPS // 2
-    chunk = 512
+    chunk = CHUNK
     chunks = tokens // chunk
     queries, peaks, outs = {}, {}, {}
     for i in range(pairs + 2):
@@ -121,16 +123,16 @@
             heads = [q_ref[:, (2 * i + j) * HD : (2 * i + j + 1) * HD] for j in range(2)]
             queries[i] = jnp.concatenate([jnp.concatenate([q, bias], axis=1) for q in heads], axis=0)
             peaks[i] = None
-            if 2 * i % GROUPS == 0:
-                loads[0, 2 * i // GROUPS].wait()
         if 0 <= i - 2 and 2 * (i - 2) % GROUPS == 0:
-            loads[1, 2 * (i - 2) // GROUPS].wait()
+            loads[chunks, 2 * (i - 2) // GROUPS].wait()
         if 0 <= i - 1 < pairs:
             top = jnp.max(peaks[i - 1], axis=0, keepdims=True).astype(bf16)
             peaks[i - 1] = top.astype(f32)
         for k in range(chunks):
             at = slice(k * chunk, (k + 1) * chunk)
             if i < pairs:
+                if 2 * i % GROUPS == 0:
+                    loads[k, 2 * i // GROUPS].wait()
                 s = lax.dot_general(
                     kv_ref[2 * i // GROUPS, at, :], queries[i], (((1,), (1,)), ((), ())), preferred_element_type=f32
                 )
@@ -295,7 +297,7 @@
             pltpu.VMEM(kv_shape, bf16),
             pltpu.VMEM((2, tokens, 2 * devices), f32),
             pltpu.VMEM((2, tokens, 2 * devices), bf16),
-            pltpu.SemaphoreType.DMA((2, steps)),
+            pltpu.SemaphoreType.DMA((tokens // CHUNK + 1, steps)),
         ],
         mib=52,
         large=1,

time: 136 us -> 137 us (level)
  no operation moved by 1% of the time
where the time goes in v8:
time: 137 us
  starting transfers between devices  47.9 us (35%)
  waiting for transfers between devices  37.6 us (27%)
  blocking collectives  31.7 us (23%)
  Pallas kernels  16.4 us (12%)
  local copies, waits for them, and re-layouts  2.17 us (2%)
    all_to_all x1, blocking collectives, per_device(): lax.all_to_all(partial.reshape(devices, 2, d_part // 2), POOL, split_axis...  31.7 us
    all_to_all x1, waiting for transfers between devices, per_device(): q = lax.all_to_all(rows, POOL, split_axis=0, concat_axis=0, tiled=True)  20.7 us
    ppermute x1, starting transfers between devices, swapped(): return lax.ppermute(v, 'c', [(0, 1), (1, 0)])  20.4 us
    pallas_call x6, Pallas kernels, small_call(): pl.pallas_call(body, out_shape=out, in_specs=[smem] * len(scalars) + [vme...  16.4 us
    ppermute x4, starting transfers between devices, to_owner(): return lax.ppermute(v, POOL, pairs)  9 us
    all_to_all x1, waiting for transfers between devices, per_device(): lax.all_to_all(parts, CHIPS, split_axis=0, concat_axis=0, tiled=True)  8.73 us
    all_to_all x1, starting transfers between devices, per_device(): q = lax.all_to_all(rows, POOL, split_axis=0, concat_axis=0, tiled=True)  7.6 us
    ppermute x4, waiting for transfers between devices, to_owner(): return lax.ppermute(v, POOL, pairs)  6.75 us
  transfers between devices with their start and end apart: 10, of which 5 were waited for; matrix products, arithmetic and copies ran while one was open for 0% of the time, Pallas kernels for 2%

profile of v8, /device:TPU:513, one launch (start us, length us, event | category | flops | bytes accessed | tf_op | source)
XLA Modules:
  0.0 136.8 jit_solution(17146859386401617858)
XLA Ops:
  0.0 20.4 %collective-permute-start = (bf16[64,2,16,512]{3,2,1,0:T(8,128)(2,1)}, bf16[64,2,16,512]{3,2,1,0:T(8,128)(2,1)}, u32[]{:S(2)}, u32[]{:S(2)}) collective-permute-start(bf16[64,2,16,512]{3,2,1,0:T(8,128)(2,1)} %own_ref.1), channel_id=1, source_target_pairs={{0,1},{1,0},{2,3},{3,2},{4,5},{5,4},{6,7},{7,6},{8,9},{9,8},{10,11... | collective-permute-start | bytes 6291464 | tf_op jit(solution)/shard_map/ppermute | solution.py:228
  21.1 2.5 %shard_map.64 = bf16[128,2,1152]{2,1,0:T(2,128)(2,1)} custom-call(s32[1]{0:T(128)S(6)} %copy.8.length_ref, bf16[1,4096]{1,0:T(2,128)(2,1)} %q_hbm.1, s32[1,128]{1,0:T(1,128)} %holder_hbm.1, s32[1,128]{1,0:T(1,128)} %slot_hbm.1), custom_call_target="tpu_custom_call" | custom-call | tf_op jit(solution)/shard_map/pallas_call | solution.py:215
  23.6 0.0 copy-start
  23.6 7.6 %all-to-all-start = ((bf16[128,2,1152]{2,1,0:T(2,128)(2,1)}), bf16[128,2,1152]{2,1,0:T(2,128)(2,1)S(1)}, u32[]{:S(2)}, u32[]{:S(2)}) async-start(bf16[128,2,1152]{2,1,0:T(2,128)(2,1)} %shard_map.64), calls=%async_computation | async-start | bytes 1179648 | tf_op jit(solution)/shard_map/all_to_all | solution.py:271
  31.3 0.1 pad_add_fusion.pos_ref
  31.3 20.7 %all-to-all-done = bf16[128,2,1152]{2,1,0:T(2,128)(2,1)S(1)} async-done(((bf16[128,2,1152]{2,1,0:T(2,128)(2,1)}), bf16[128,2,1152]{2,1,0:T(2,128)(2,1)S(1)}, u32[]{:S(2)}, u32[]{:S(2)}) %all-to-all-start) | async-done | bytes 589856 | tf_op jit(solution)/shard_map/all_to_all | solution.py:271
  52.1 0.1 copy.7
  52.1 0.0 collective-permute-done.other_ref
  52.2 2.4 %shard_map.65.kv_hbm = bf16[2,3200,256]{2,1,0:T(8,128)(2,1)S(1)} custom-call(s32[2]{0:T(128)S(1)} %pad_add_fusion.pos_ref, bf16[64,2,16,512]{3,2,1,0:T(8,128)(2,1)S(1)} %copy-done, bf16[64,2,16,512]{3,2,1,0:T(8,128)(2,1)} %collective-permute-done.other_ref), custom_call_target="tpu_custom_call" | custom-call | flops 4294967296 | tf_op jit(solution)/shard_map/pallas_call | solution.py:215
  54.5 1.7 %copy-done.1 = bf16[2,3200,256]{2,1,0:T(8,128)(2,1)} copy-done((bf16[2,3200,256]{2,1,0:T(8,128)(2,1)}, bf16[2,3200,256]{2,1,0:T(8,128)(2,1)S(1)}, u32[]{:S(2)}) %copy-start.1) | copy-done | bytes 3276824
  56.2 9.9 %shard_map.66 = bf16[64,2,2176]{2,1,0:T(2,128)(2,1)} custom-call(s32[2]{0:T(128)S(1)} %pad_add_fusion.pos_ref, bf16[128,2304]{1,0:T(8,128)(2,1)S(1)} %bitcast.4, bf16[2,3200,256]{2,1,0:T(8,128)(2,1)} %copy-done.1), custom_call_target="tpu_custom_call" | custom-call | flops 17179869184 | tf_op jit(solution)/shard_map/pallas_call | solution.py:215
  66.1 6.7 %all-to-all-start.1 = ((bf16[64,2,2176]{2,1,0:T(2,128)(2,1)}), bf16[64,2,2176]{2,1,0:T(2,128)(2,1)S(1)}, u32[]{:S(2)}, u32[]{:S(2)}) async-start(bf16[64,2,2176]{2,1,0:T(2,128)(2,1)} %shard_map.66), calls=%async_computation.1 | async-start | bytes 1114112 | tf_op jit(solution)/shard_map/all_to_all | solution.py:306
  72.8 0.1 constant_dynamic-slice_fusion
  72.9 6.7 %collective-permute-start.4 = (bf16[32,2048]{1,0:T(8,128)(2,1)S(1)}, bf16[32,2048]{1,0:T(8,128)(2,1)S(1)}, u32[]{:S(2)}, u32[]{:S(2)}) collective-permute-start(bf16[32,2048]{1,0:T(8,128)(2,1)S(1)} %get-tuple-element.7), channel_id=1, source_target_pairs={{0,0},{1,64},{2,2},{3,66},{4,4},{5,68},{6,6},{7,70},{8,8},{9,72},{... | collective-permute-start | bytes 393224 | tf_op jit(solution)/shard_map/ppermute | solution.py:247
  79.7 0.1 collective-permute-start.5
  79.8 1.1 collective-permute-start.6
  80.9 1.1 collective-permute-start.7
  81.9 8.7 %all-to-all-done.1.got_ref = bf16[64,2,2176]{2,1,0:T(2,128)(2,1)S(1)} async-done(((bf16[64,2,2176]{2,1,0:T(2,128)(2,1)}), bf16[64,2,2176]{2,1,0:T(2,128)(2,1)S(1)}, u32[]{:S(2)}, u32[]{:S(2)}) %all-to-all-start.1) | async-done | bytes 557088 | tf_op jit(solution)/shard_map/all_to_all | solution.py:306
  90.7 0.6 shard_map.67.refs_0_
  91.2 2.1 %collective-permute-start.1 = (bf16[64,128]{1,0:T(8,128)(2,1)S(1)}, bf16[64,128]{1,0:T(8,128)(2,1)S(1)}, u32[]{:S(2)}, u32[]{:S(2)}) collective-permute-start(bf16[64,128]{1,0:T(8,128)(2,1)S(1)} %shard_map.67.refs_0_), channel_id=1, source_target_pairs={{0,1},{1,0},{2,3},{3,2},{4,5},{5,4},{6,7},{7,6},{8,9},{9,8},{10,11... | collective-permute-start | bytes 49160 | tf_op jit(solution)/shard_map/ppermute | solution.py:234
  93.4 6.7 %collective-permute-done.4.refs_4_ = bf16[32,2048]{1,0:T(8,128)(2,1)S(1)} collective-permute-done((bf16[32,2048]{1,0:T(8,128)(2,1)S(1)}, bf16[32,2048]{1,0:T(8,128)(2,1)S(1)}, u32[]{:S(2)}, u32[]{:S(2)}) %collective-permute-start.4) | collective-permute-done | bytes 131104 | tf_op jit(solution)/shard_map/ppermute | solution.py:247
  100.1 0.0 collective-permute-start.2
  100.1 0.0 collective-permute-done.5.refs_5_
  100.1 2.1 %collective-permute-start.3 = (bf16[64,128]{1,0:T(8,128)(2,1)S(1)}, bf16[64,128]{1,0:T(8,128)(2,1)S(1)}, u32[]{:S(2)}, u32[]{:S(2)}) collective-permute-start(bf16[64,128]{1,0:T(8,128)(2,1)S(1)} %shard_map.67.refs_0_), channel_id=1, source_target_pairs={{0,3},{1,2},{2,1},{3,0},{4,7},{5,6},{6,5},{7,4},{8,11},{9,10},{10,... | collective-permute-start | bytes 49160 | tf_op jit(solution)/shard_map/ppermute | solution.py:234
  102.2 0.0 collective-permute-done.6.refs_6_
  102.2 0.0 collective-permute-done.1.refs_1_
  102.2 0.5 collective-permute-done.2.refs_2_
  102.7 1.0 collective-permute-done.3.refs_3_
  103.6 0.3 shard_map.68
  104.0 0.4 reshape.7
  104.4 31.7 %all_to_all.15.got_ref = bf16[128,2,1024]{2,1,0:T(2,128)(2,1)S(1)} all-to-all(bf16[128,2,1024]{2,1,0:T(2,128)(2,1)S(1)} %reshape.7), channel_id=1, replica_groups=mesh['grp'=2,'y'=8,'x'=8,'c'=2] {'y','x','c'}, dimensions={0} | all-to-all | bytes 1048576 | tf_op jit(solution)/shard_map/all_to_all | solution.py:310
  136.1 0.7 shard_map.69
  (5 shorter events, 0.0 us)
Async XLA Ops:
  0.0 52.1 %collective-permute-start = (bf16[64,2,16,512]{3,2,1,0:T(8,128)(2,1)}, bf16[64,2,16,512]{3,2,1,0:T(8,128)(2,1)}, u32[]{:S(2)}, u32[]{:S(2)}) collective-permute-start(bf16[64,2,16,512]{3,2,1,0:T(8,128)(2,1)} %own_ref.1), channel_id=1, source_target_pairs={{0,1},{1,0},{2,3},{3,2},{4,5},{5,4},{6,7},{7,6},{8,9},{9,8},{10,11... | collective-permute-start | bytes 6291464 | tf_op jit(solution)/shard_map/ppermute | solution.py:228
  23.6 28.5 %copy-start = (bf16[64,2,16,512]{3,2,1,0:T(8,128)(2,1)S(1)}, bf16[64,2,16,512]{3,2,1,0:T(8,128)(2,1)}, u32[]{:S(2)}) copy-start(bf16[64,2,16,512]{3,2,1,0:T(8,128)(2,1)} %own_ref.1) | copy-start | bytes 6291460
  23.6 28.4 %all-to-all-start = ((bf16[128,2,1152]{2,1,0:T(2,128)(2,1)}), bf16[128,2,1152]{2,1,0:T(2,128)(2,1)S(1)}, u32[]{:S(2)}, u32[]{:S(2)}) async-start(bf16[128,2,1152]{2,1,0:T(2,128)(2,1)} %shard_map.64), calls=%async_computation | async-start | bytes 1179648 | tf_op jit(solution)/shard_map/all_to_all | solution.py:271
  54.5 1.7 %copy-start.1 = (bf16[2,3200,256]{2,1,0:T(8,128)(2,1)}, bf16[2,3200,256]{2,1,0:T(8,128)(2,1)S(1)}, u32[]{:S(2)}) copy-start(bf16[2,3200,256]{2,1,0:T(8,128)(2,1)S(1)} %shard_map.65.kv_hbm) | copy-start | bytes 9830404
  56.2 16.6 %copy-start.2 = (bf16[32,8192]{1,0:T(8,128)(2,1)S(1)}, bf16[32,8192]{1,0:T(8,128)(2,1)}, u32[]{:S(2)}) copy-start(bf16[32,8192]{1,0:T(8,128)(2,1)} %param.11) | copy-start | bytes 1572868
  66.1 24.6 %all-to-all-start.1 = ((bf16[64,2,2176]{2,1,0:T(2,128)(2,1)}), bf16[64,2,2176]{2,1,0:T(2,128)(2,1)S(1)}, u32[]{:S(2)}, u32[]{:S(2)}) async-start(bf16[64,2,2176]{2,1,0:T(2,128)(2,1)} %shard_map.66), calls=%async_computation.1 | async-start | bytes 1114112 | tf_op jit(solution)/shard_map/all_to_all | solution.py:306
  72.9 27.2 %collective-permute-start.4 = (bf16[32,2048]{1,0:T(8,128)(2,1)S(1)}, bf16[32,2048]{1,0:T(8,128)(2,1)S(1)}, u32[]{:S(2)}, u32[]{:S(2)}) collective-permute-start(bf16[32,2048]{1,0:T(8,128)(2,1)S(1)} %get-tuple-element.7), channel_id=1, source_target_pairs={{0,0},{1,64},{2,2},{3,66},{4,4},{5,68},{6,6},{7,70},{8,8},{9,72},{... | collective-permute-start | bytes 393224 | tf_op jit(solution)/shard_map/ppermute | solution.py:247
  79.7 20.4 %collective-permute-start.5 = (bf16[32,2048]{1,0:T(8,128)(2,1)S(1)}, bf16[32,2048]{1,0:T(8,128)(2,1)S(1)}, u32[]{:S(2)}, u32[]{:S(2)}) collective-permute-start(bf16[32,2048]{1,0:T(8,128)(2,1)S(1)} %get-tuple-element.6), channel_id=1, source_target_pairs={{0,1},{1,65},{2,3},{3,67},{4,5},{5,69},{6,7},{7,71},{8,9},{9,73},{... | collective-permute-start | bytes 393224 | tf_op jit(solution)/shard_map/ppermute | solution.py:247
  79.8 22.4 %collective-permute-start.6 = (bf16[32,2048]{1,0:T(8,128)(2,1)S(1)}, bf16[32,2048]{1,0:T(8,128)(2,1)S(1)}, u32[]{:S(2)}, u32[]{:S(2)}) collective-permute-start(bf16[32,2048]{1,0:T(8,128)(2,1)S(1)} %get-tuple-element.8), channel_id=1, source_target_pairs={{0,2},{1,66},{2,0},{3,64},{4,6},{5,70},{6,4},{7,68},{8,10},{9,74},... | collective-permute-start | bytes 393224 | tf_op jit(solution)/shard_map/ppermute | solution.py:247
  80.9 21.4 %collective-permute-start.7 = (bf16[32,2048]{1,0:T(8,128)(2,1)S(1)}, bf16[32,2048]{1,0:T(8,128)(2,1)S(1)}, u32[]{:S(2)}, u32[]{:S(2)}) collective-permute-start(bf16[32,2048]{1,0:T(8,128)(2,1)S(1)} %get-tuple-element.5), channel_id=1, source_target_pairs={{0,3},{1,67},{2,1},{3,65},{4,7},{5,71},{6,5},{7,69},{8,11},{9,75},... | collective-permute-start | bytes 393224 | tf_op jit(solution)/shard_map/ppermute | solution.py:247
  91.2 11.0 %collective-permute-start.1 = (bf16[64,128]{1,0:T(8,128)(2,1)S(1)}, bf16[64,128]{1,0:T(8,128)(2,1)S(1)}, u32[]{:S(2)}, u32[]{:S(2)}) collective-permute-start(bf16[64,128]{1,0:T(8,128)(2,1)S(1)} %shard_map.67.refs_0_), channel_id=1, source_target_pairs={{0,1},{1,0},{2,3},{3,2},{4,5},{5,4},{6,7},{7,6},{8,9},{9,8},{10,11... | collective-permute-start | bytes 49160 | tf_op jit(solution)/shard_map/ppermute | solution.py:234
  100.1 2.6 %collective-permute-start.2 = (bf16[64,128]{1,0:T(8,128)(2,1)S(1)}, bf16[64,128]{1,0:T(8,128)(2,1)S(1)}, u32[]{:S(2)}, u32[]{:S(2)}) collective-permute-start(bf16[64,128]{1,0:T(8,128)(2,1)S(1)} %shard_map.67.refs_0_), channel_id=1, source_target_pairs={{0,2},{1,3},{2,0},{3,1},{4,6},{5,7},{6,4},{7,5},{8,10},{9,11},{10,... | collective-permute-start | bytes 49160 | tf_op jit(solution)/shard_map/ppermute | solution.py:234
  100.1 3.5 %collective-permute-start.3 = (bf16[64,128]{1,0:T(8,128)(2,1)S(1)}, bf16[64,128]{1,0:T(8,128)(2,1)S(1)}, u32[]{:S(2)}, u32[]{:S(2)}) collective-permute-start(bf16[64,128]{1,0:T(8,128)(2,1)S(1)} %shard_map.67.refs_0_), channel_id=1, source_target_pairs={{0,3},{1,2},{2,1},{3,0},{4,7},{5,6},{6,5},{7,4},{8,11},{9,10},{10,... | collective-permute-start | bytes 49160 | tf_op jit(solution)/shard_map/ppermute | solution.py:234
